TPU v7x, 128 devices: a whole 4x4x4 slice. The times are simulated.
128 devices in a mesh: ep: 32 (over y, x, core), dp: 4 (over z).
Axes of the slice: x: 4, y: 4, z: 4, core: 2. Of those that a mesh axis runs over, the one named last changes fastest.
Arguments:
- resid: bfloat16 [2048, 4096], P(('ep', 'dp')), may hold values from -6 to 6
- queries: bfloat16 [2048, 8192], P(('ep', 'dp')), may hold values from -4.5 to 4.5
- new_keys: bfloat16 [2048, 512], P(('ep', 'dp')), may hold values from -4.5 to 4.5
- new_values: bfloat16 [2048, 512], P(('ep', 'dp')), may hold values from -6 to 6
- cache_keys: bfloat16 [2048, 128, 512], P(('ep', 'dp')), may hold values from -4.5 to 4.5
- cache_values: bfloat16 [2048, 128, 512], P(('ep', 'dp')), may hold values from -6 to 6
- cache_len: int32 [2048], P(('ep', 'dp')), may hold values from 1 to 128
- out_proj: bfloat16 [8192, 4096], P('ep'), may hold values from -0.0625 to 0.0625
- norm_gain: float32 [4096], replicated, may hold values from 0.1 to 1.9
- router: bfloat16 [4096, 64], replicated, may hold values from -4 to 4
- expert_ids: int32 [2048, 8], P(('ep', 'dp')), may hold values from 0 to 63, all different within a row; in each aligned block of 16 rows (0 to 15, 16 to 31, ...) at most 4 rows name the same one
- gate_slab: bfloat16 [128, 4096, 384], P(('ep', 'dp')), may hold values from -0.09375 to 0.09375
- up_slab: bfloat16 [128, 4096, 384], P(('ep', 'dp')), may hold values from -0.09375 to 0.09375
- down_slab: bfloat16 [128, 384, 4096], P(('ep', 'dp')), may hold values from -0.21875 to 0.21875
Outputs:
- mixed: float32 [2048, 4096], P(('ep', 'dp'))
Inputs may be any that keep to these rules, and one draw needn't show every extreme that they name: `expert_ids`: each row names 8 different experts; among the rows of one device no expert is named by more than 4 rows.
All inputs are finite; a program needn't handle non-finite values.
Results may differ from a plain program's by a relative error of at most 0.009.
Values may be sent and summed in bfloat16 or wider, within the bound.
No kernel may reach another device: no remote copies, remote signals or barrier semaphores. Data moves between devices by JAX's collectives and lax.ppermute only.
A program may use at most 128 MiB of HBM per device.

v0:
```python
import math

import jax
import jax.numpy as jnp
from jax import lax
from jax.sharding import PartitionSpec as P

D = 4096
H = 64
KVH = 4
HD = 128
TOP = 8


def from_partner(value, axis, distance):
    mask = 2**distance
    pairs = [(source, source ^ mask) for source in range(lax.axis_size(axis))]
    return lax.ppermute(value, axis, pairs)


def attend(queries, new_keys, new_values, cache_keys, cache_values, cache_len):
    local_rows = queries.shape[0]
    cache_span = cache_keys.shape[1]
    group_size = H // KVH
    query_heads = queries.reshape(local_rows, KVH, group_size, HD)
    past_keys = cache_keys.reshape(local_rows, cache_span, KVH, HD)
    past_values = cache_values.reshape(local_rows, cache_span, KVH, HD)
    score_scale = 1.0 / math.sqrt(HD)
    past_scores = (
        jnp.einsum("tgqd,tcgd->tgqc", query_heads, past_keys, preferred_element_type=jnp.float32)
        * score_scale
    )
    own_scores = (
        jnp.einsum(
            "tgqd,tgd->tgq",
            query_heads,
            new_keys.reshape(local_rows, KVH, HD),
            preferred_element_type=jnp.float32,
        )
        * score_scale
    )
    is_valid = lax.broadcasted_iota(jnp.int32, (local_rows, cache_span), 1) < cache_len[:, None]
    past_scores = jnp.where(is_valid[:, None, None, :], past_scores, -1e30)
    peak_score = jnp.maximum(jnp.max(past_scores, axis=3), own_scores)
    past_exp = jnp.exp(past_scores - peak_score[..., None])
    own_exp = jnp.exp(own_scores - peak_score)
    denom_sum = jnp.sum(past_exp, axis=3) + own_exp
    past_weights = (past_exp / denom_sum[..., None]).astype(jnp.bfloat16)
    own_weights = (own_exp / denom_sum).astype(jnp.bfloat16)
    blended = jnp.einsum(
        "tgqc,tcgd->tgqd", past_weights, past_values, preferred_element_type=jnp.float32
    )
    blended = blended + own_weights.astype(jnp.float32)[..., None] * new_values.reshape(
        local_rows, KVH, 1, HD
    ).astype(jnp.float32)
    return blended.reshape(local_rows, H * HD).astype(jnp.bfloat16)


def expert_ffn(rows_in, gate_part, up_part, down_part):
    gate_val = jnp.dot(rows_in, gate_part, preferred_element_type=jnp.float32)
    up_val = jnp.dot(rows_in, up_part, preferred_element_type=jnp.float32)
    activated = (jax.nn.silu(gate_val) * up_val).astype(jnp.bfloat16)
    return jnp.dot(activated, down_part, preferred_element_type=jnp.float32)


def local(
    resid,
    queries,
    new_keys,
    new_values,
    cache_keys,
    cache_values,
    cache_len,
    out_proj,
    norm_gain,
    router,
    expert_ids,
    gate_slab,
    up_slab,
    down_slab,
):
    local_rows = resid.shape[0]
    attended = attend(queries, new_keys, new_values, cache_keys, cache_values, cache_len)
    regrouped = lax.all_to_all(attended, "ep", split_axis=1, concat_axis=0, tiled=True)
    attn_out = lax.psum_scatter(
        jnp.dot(regrouped, out_proj, preferred_element_type=jnp.float32).astype(jnp.bfloat16),
        "ep",
        scatter_dimension=0,
        tiled=True,
    ).astype(jnp.float32)
    hidden = resid.astype(jnp.float32) + attn_out
    meansq = jnp.mean(hidden * hidden, axis=1, keepdims=True)
    normed = (hidden * lax.rsqrt(jnp.maximum(meansq, 0.25)) * norm_gain).astype(jnp.bfloat16)
    logits = jnp.dot(normed, router, preferred_element_type=jnp.float32)
    experts = router.shape[1]
    labels = jnp.arange(experts, dtype=jnp.int32)
    onehot = expert_ids[:, :, None] == labels[None, None, :]
    chosen = jnp.sum(jnp.where(onehot, logits[:, None, :], 0.0), axis=2)
    peak_logit = jnp.max(chosen, axis=1, keepdims=True)
    exp_logit = jnp.exp(chosen - peak_logit)
    gate_probs = (exp_logit / jnp.sum(exp_logit, axis=1, keepdims=True)).astype(jnp.bfloat16)
    per_token = jnp.sum(onehot.astype(jnp.int32), axis=1)
    before = jnp.cumsum(per_token, axis=0) - per_token
    ranking = jnp.sum(jnp.where(onehot, before[:, None, :], 0), axis=2)
    slab_count = lax.axis_size("ep") * lax.axis_size("dp")
    half_slots = (4 * local_rows * TOP + 5 * experts - 1) // (5 * experts)
    target = (2 * expert_ids + ranking % 2) * half_slots + ranking // 2
    places = jnp.arange(slab_count * half_slots, dtype=jnp.int32)
    slot_match = target[:, :, None] == places[None, None, :]
    dispatch = jnp.any(slot_match, axis=1).astype(jnp.bfloat16)
    combine = jnp.sum(
        jnp.where(slot_match, gate_probs.astype(jnp.float32)[:, :, None], 0.0), axis=1
    ).astype(jnp.bfloat16)
    outgoing = lax.dot_general(
        dispatch, normed, (((0,), (0,)), ((), ())), preferred_element_type=jnp.float32
    )
    outgoing = outgoing.astype(jnp.bfloat16).reshape(slab_count, half_slots, D)
    partner = from_partner((gate_slab, up_slab, down_slab), "dp", 0)
    incoming = lax.all_to_all(outgoing, ("ep", "dp"), split_axis=0, concat_axis=0, tiled=True)
    sources, slot_count, feature_dim = incoming.shape
    flat_rows = incoming.reshape(sources * slot_count, feature_dim)
    produced = expert_ffn(flat_rows, gate_slab[0], up_slab[0], down_slab[0])
    produced = produced + expert_ffn(flat_rows, partner[0][0], partner[1][0], partner[2][0])
    returned = lax.all_to_all(
        produced.astype(jnp.bfloat16).reshape(sources, slot_count, feature_dim),
        ("ep", "dp"),
        split_axis=0,
        concat_axis=0,
        tiled=True,
    )
    expert_mix = jnp.dot(
        combine, returned.reshape(slab_count * half_slots, D), preferred_element_type=jnp.float32
    )
    return hidden + expert_mix


def solution(mesh):
    in_specs = (
        P(("ep", "dp"), None),
        P(("ep", "dp"), None),
        P(("ep", "dp"), None),
        P(("ep", "dp"), None),
        P(("ep", "dp"), None, None),
        P(("ep", "dp"), None, None),
        P(("ep", "dp")),
        P("ep", None),
        P(),
        P(),
        P(("ep", "dp"), None),
        P(("ep", "dp"), None, None),
        P(("ep", "dp"), None, None),
        P(("ep", "dp"), None, None),
    )
    out_specs = P(("ep", "dp"), None)
    return jax.shard_map(local, mesh=mesh, in_specs=in_specs, out_specs=out_specs, check_vma=False)
```

profile of v0, /device:TPU:1, one launch (start us, length us, event | category | flops | bytes accessed | tf_op | source)
XLA Modules:
  0.0 358.3 jit_solution(8555865213800240710)
XLA Ops:
  8.9 1.0 copy.44
  10.1 3.0 fusion.68
  14.7 17.3 %all_to_all.26 = bf16[16,32,256]{2,0,1:T(8,128)(2,1)S(1)} all-to-all(bf16[16,32,256]{2,0,1:T(8,128)(2,1)S(1)} %copy.33), channel_id=1, replica_groups=mesh['ep'=32,'dp'=4] {'ep'}, dimensions={1} | all-to-all | bytes 524288 | tf_op jit(solution)/shard_map/all_to_all | solution.py:84
  32.0 3.2 convolution_convert_fusion
  35.2 1.7 collective-permute-start.1
  37.7 76.6 %reduce-scatter.2.cloned.1.call-done = bf16[16,4096]{1,0:T(8,128)(2,1)} async-done(((bf16[512,4096]{1,0:T(8,128)(2,1)}), bf16[16,4096]{1,0:T(8,128)(2,1)}) %reduce-scatter.2.cloned.1.call-update) | async-done | bytes 131088 | tf_op jit(solution)/shard_map/reduce_scatter | solution.py:85
  114.2 1.1 multiply_reduce_fusion
  115.3 3.0 convolution_convert_fusion.1
  118.3 4.4 %reshape.120 = bf16[128,2,4096]{2,1,0:T(2,128)(2,1)} reshape(bf16[256,4096]{1,0:T(8,128)(2,1)} %convolution_convert_fusion.1) | data formatting | bytes 4194304 | tf_op jit(solution)/shard_map/reshape | solution.py:117
  122.7 9.9 %all-to-all-start.1 = ((bf16[128,2,4096]{2,1,0:T(2,128)(2,1)}), bf16[128,2,4096]{2,1,0:T(2,128)(2,1)}, u32[]{:S(2)}, u32[]{:S(2)}) async-start(bf16[128,2,4096]{2,1,0:T(2,128)(2,1)} %reshape.120), calls=%async_computation.2 | async-start | bytes 4194304 | tf_op jit(solution)/shard_map/all_to_all | solution.py:119
  132.6 1.6 collective-permute-start
  134.5 28.3 %all-to-all-done.1 = bf16[128,2,4096]{2,1,0:T(2,128)(2,1)} async-done(((bf16[128,2,4096]{2,1,0:T(2,128)(2,1)}), bf16[128,2,4096]{2,1,0:T(2,128)(2,1)}, u32[]{:S(2)}, u32[]{:S(2)}) %all-to-all-start.1) | async-done | bytes 2097184 | tf_op jit(solution)/shard_map/all_to_all | solution.py:119
  162.8 4.1 %reshape.121 = bf16[256,4096]{1,0:T(8,128)(2,1)} reshape(bf16[128,2,4096]{2,1,0:T(2,128)(2,1)} %all-to-all-done.1) | data formatting | bytes 4194304 | tf_op jit(solution)/shard_map/reshape | solution.py:121
  166.9 3.9 %fusion.10 = f32[256,384]{1,0:T(8,128)S(1)} fusion(bf16[256,4096]{1,0:T(8,128)(2,1)} %reshape.121, bf16[1,4096,384]{2,1,0:T(8,128)(2,1)} %param.25), kind=kOutput, calls=%fused_computation.14 | convolution fusion | flops 805306368 | bytes 5636096 | tf_op jit(solution)/shard_map/dot_general | solution.py:60
  170.8 3.2 fusion.2
  174.0 7.8 %fusion.6 = f32[256,4096]{1,0:T(8,128)} fusion(bf16[1,384,4096]{2,1,0:T(8,128)(2,1)} %param.27, bf16[256,4096]{1,0:T(8,128)(2,1)} %reshape.121, bf16[1,4096,384]{2,1,0:T(8,128)(2,1)} %param.26, f32[256,384]{1,0:T(8,128)S(1)} %fusion.10), kind=kOutput, calls=%fused_computation.10 | convolution fusion | flops 1611202560 | bytes 12976128 | tf_op jit(solution)/shard_map/dot_general | solution.py:63
  181.9 42.3 %collective-permute-done = bf16[1,4096,384]{2,1,0:T(8,128)(2,1)} collective-permute-done((bf16[1,4096,384]{2,1,0:T(8,128)(2,1)}, bf16[1,4096,384]{2,1,0:T(8,128)(2,1)}, u32[]{:S(2)}, u32[]{:S(2)}) %collective-permute-start) | collective-permute-done | bytes 3145760 | tf_op jit(solution)/shard_map/ppermute | solution.py:18
  224.2 67.4 %collective-permute-done.2 = bf16[1,384,4096]{2,1,0:T(8,128)(2,1)} collective-permute-done((bf16[1,384,4096]{2,1,0:T(8,128)(2,1)}, bf16[1,384,4096]{2,1,0:T(8,128)(2,1)}, u32[]{:S(2)}, u32[]{:S(2)}) %collective-permute-start.2) | collective-permute-done | bytes 3145760 | tf_op jit(solution)/shard_map/ppermute | solution.py:18
  291.6 8.5 %fusion = bf16[256,4096]{1,0:T(8,128)(2,1)} fusion(f32[256,4096]{1,0:T(8,128)} %fusion.6, bf16[1,384,4096]{2,1,0:T(8,128)(2,1)} %collective-permute-done.2, f32[256,384]{1,0:T(8,128)S(1)} %fusion.2, bf16[256,4096]{1,0:T(8,128)(2,1)} %reshape.121, bf16[1,4096,384]{2,1,0:T(8,128)(2,1)} %collective-permute-done), kind=kOutput, calls=%fused_computation.2 | convolution fusion | flops 1613299712 | bytes 15073280 | tf_op jit(solution)/shard_map/dot_general | solution.py:63
  300.0 4.4 %reshape.122 = bf16[128,2,4096]{2,1,0:T(2,128)(2,1)} reshape(bf16[256,4096]{1,0:T(8,128)(2,1)} %fusion) | data formatting | bytes 4194304 | tf_op jit(solution)/shard_map/reshape | solution.py:125
  304.5 10.0 %all-to-all-start.2 = ((bf16[128,2,4096]{2,1,0:T(2,128)(2,1)}), bf16[128,2,4096]{2,1,0:T(2,128)(2,1)}, u32[]{:S(2)}, u32[]{:S(2)}) async-start(bf16[128,2,4096]{2,1,0:T(2,128)(2,1)} %reshape.122), calls=%async_computation.3 | async-start | bytes 4194304 | tf_op jit(solution)/shard_map/all_to_all | solution.py:124
  315.4 29.2 %all-to-all-done.2 = bf16[128,2,4096]{2,1,0:T(2,128)(2,1)} async-done(((bf16[128,2,4096]{2,1,0:T(2,128)(2,1)}), bf16[128,2,4096]{2,1,0:T(2,128)(2,1)}, u32[]{:S(2)}, u32[]{:S(2)}) %all-to-all-start.2) | async-done | bytes 2097184 | tf_op jit(solution)/shard_map/all_to_all | solution.py:124
  344.6 4.1 %reshape.123 = bf16[256,4096]{1,0:T(8,128)(2,1)} reshape(bf16[128,2,4096]{2,1,0:T(2,128)(2,1)} %all-to-all-done.2) | data formatting | bytes 4194304 | tf_op jit(solution)/shard_map/reshape | solution.py:132
  348.8 2.7 convolution_add_fusion.1
  (46 shorter events, 6.1 us)
Async XLA Ops:
  6.5 25.4 %copy-start = (bf16[256,4096]{1,0:T(8,128)(2,1)S(1)}, bf16[256,4096]{1,0:T(8,128)(2,1)}, u32[]{:S(2)}) copy-start(bf16[256,4096]{1,0:T(8,128)(2,1)} %param.21) | copy-start | bytes 6291460
  6.5 107.7 %reduce-scatter.2.cloned.1.call-start = ((), (), s32[]{:S(2)}) async-start(), calls=%async_computation.4 | async-start | bytes 4325376 | tf_op jit(solution)/shard_map/reduce_scatter | solution.py:85
  9.9 3.8 %copy-start.7 = (bf16[16,128,512]{2,1,0:T(8,128)(2,1)S(1)}, bf16[16,128,512]{2,1,0:T(8,128)(2,1)}, u32[]{:S(2)}) copy-start(bf16[16,128,512]{2,1,0:T(8,128)(2,1)} %param.19) | copy-start | bytes 6291460
  35.1 1.8 copy-start.6
  35.1 79.1 %copy-start.2 = (bf16[16,4096]{1,0:T(8,128)(2,1)S(1)}, bf16[16,4096]{1,0:T(8,128)(2,1)}, u32[]{:S(2)}) copy-start(bf16[16,4096]{1,0:T(8,128)(2,1)} %param.14) | copy-start | bytes 393220
  35.1 80.2 %copy-start.5 = (f32[4096]{0:T(1024)S(1)}, f32[4096]{0:T(1024)}, u32[]{:S(2)}) copy-start(f32[4096]{0:T(1024)} %param.22) | copy-start | bytes 49156
  35.2 135.7 %collective-permute-start.1 = (bf16[1,4096,384]{2,1,0:T(8,128)(2,1)}, bf16[1,4096,384]{2,1,0:T(8,128)(2,1)}, u32[]{:S(2)}, u32[]{:S(2)}) collective-permute-start(bf16[1,4096,384]{2,1,0:T(8,128)(2,1)} %param.26), channel_id=1, source_target_pairs={{0,1},{1,0},{2,3},{3,2},{4,5},{5,4},{6,7},{7,6},{8,9},{9,8},{10,11... | collective-permute-start | bytes 9437192 | tf_op jit(solution)/shard_map/ppermute | solution.py:18
  122.7 40.1 %all-to-all-start.1 = ((bf16[128,2,4096]{2,1,0:T(2,128)(2,1)}), bf16[128,2,4096]{2,1,0:T(2,128)(2,1)}, u32[]{:S(2)}, u32[]{:S(2)}) async-start(bf16[128,2,4096]{2,1,0:T(2,128)(2,1)} %reshape.120), calls=%async_computation.2 | async-start | bytes 4194304 | tf_op jit(solution)/shard_map/all_to_all | solution.py:119
  132.6 91.5 %collective-permute-start = (bf16[1,4096,384]{2,1,0:T(8,128)(2,1)}, bf16[1,4096,384]{2,1,0:T(8,128)(2,1)}, u32[]{:S(2)}, u32[]{:S(2)}) collective-permute-start(bf16[1,4096,384]{2,1,0:T(8,128)(2,1)} %param.25), channel_id=1, source_target_pairs={{0,1},{1,0},{2,3},{3,2},{4,5},{5,4},{6,7},{7,6},{8,9},{9,8},{10,11... | collective-permute-start | bytes 9437192 | tf_op jit(solution)/shard_map/ppermute | solution.py:18
  134.2 157.4 %collective-permute-start.2 = (bf16[1,384,4096]{2,1,0:T(8,128)(2,1)}, bf16[1,384,4096]{2,1,0:T(8,128)(2,1)}, u32[]{:S(2)}, u32[]{:S(2)}) collective-permute-start(bf16[1,384,4096]{2,1,0:T(8,128)(2,1)} %param.27), channel_id=1, source_target_pairs={{0,1},{1,0},{2,3},{3,2},{4,5},{5,4},{6,7},{7,6},{8,9},{9,8},{10,11... | collective-permute-start | bytes 9437192 | tf_op jit(solution)/shard_map/ppermute | solution.py:18
  166.9 3.9 %copy-start.1 = (bf16[256,4096]{1,0:T(8,128)(2,1)S(1)}, bf16[256,4096]{1,0:T(8,128)(2,1)}, u32[]{:S(2)}) copy-start(bf16[256,4096]{1,0:T(8,128)(2,1)} %reshape.121) | copy-start | bytes 6291460
  304.4 10.0 %copy-start.3 = (bf16[16,4096]{1,0:T(8,128)(2,1)S(1)}, bf16[16,4096]{1,0:T(8,128)(2,1)}, u32[]{:S(2)}) copy-start(bf16[16,4096]{1,0:T(8,128)(2,1)} %reduce-scatter.2.cloned.1.call-done) | copy-start | bytes 393220
  304.5 10.0 %copy-start.4 = (bf16[4096,64]{0,1:T(8,128)(2,1)S(1)}, bf16[4096,64]{0,1:T(8,128)(2,1)}, u32[]{:S(2)}) copy-start(bf16[4096,64]{0,1:T(8,128)(2,1)} %param.23) | copy-start | bytes 1572868
  304.5 40.2 %all-to-all-start.2 = ((bf16[128,2,4096]{2,1,0:T(2,128)(2,1)}), bf16[128,2,4096]{2,1,0:T(2,128)(2,1)}, u32[]{:S(2)}, u32[]{:S(2)}) async-start(bf16[128,2,4096]{2,1,0:T(2,128)(2,1)} %reshape.122), calls=%async_computation.3 | async-start | bytes 4194304 | tf_op jit(solution)/shard_map/all_to_all | solution.py:124
Sparse Core Ops, SparseCore 0:
  35.3 78.8 reduce-scatter.1
where the time goes:
time: 359 us; the launch traced here: 358 us
  waiting for transfers between devices  244 us (68%)
  matrix products  36.6 us (10%)
  starting transfers between devices  23.4 us (7%)
  local copies, waits for them, and re-layouts  20 us (6%)
  blocking collectives  17.3 us (5%)
  between operations  13.6 us (4%)
    ppermute x3, waiting for transfers between devices, from_partner(): return lax.ppermute(value, axis, pairs)  110 us
    reduce_scatter x1, waiting for transfers between devices, local(): lax.psum_scatter(jnp.dot(regrouped, out_proj, preferred_element_type=jnp....  76.6 us
    all_to_all x1, waiting for transfers between devices, local(): lax.all_to_all(produced.astype(jnp.bfloat16).reshape(sources, slot_count,...  29.2 us
    all_to_all x1, waiting for transfers between devices, local(): lax.all_to_all(outgoing, ('ep', 'dp'), split_axis=0, concat_axis=0, tiled...  28.3 us
    all_to_all x1, blocking collectives, local(): lax.all_to_all(attended, 'ep', split_axis=1, concat_axis=0, tiled=True)  17.3 us
    dot_general x2, matrix products, expert_ffn(): return jnp.dot(activated, down_part, preferred_element_type=jnp.float32)  16.3 us
    all_to_all x1, starting transfers between devices, local(): lax.all_to_all(produced.astype(jnp.bfloat16).reshape(sources, slot_count,...  10 us
    all_to_all x1, starting transfers between devices, local(): lax.all_to_all(outgoing, ('ep', 'dp'), split_axis=0, concat_axis=0, tiled...  9.87 us
  transfers between devices with their start and end apart: 6, of which 5 were waited for; matrix products, arithmetic and copies ran while one was open for 8% of the time, Pallas kernels for 0%

commit v1 on v0

v1 whole, which is shorter than its diff:
```python
import math

import jax
import jax.numpy as jnp
from jax import lax
from jax.sharding import Mesh
from jax.sharding import PartitionSpec as P

D = 4096
H = 64
KVH = 4
HD = 128
TOP = 8
CAP = 4


EP = ("chip", "core")
ALL = ("chip", "core", "dp")


def flipped(value, axis, mask):
    pairs = [(source, source ^ mask) for source in range(lax.axis_size(axis))]
    return lax.ppermute(value, axis, pairs)


def attend(queries, new_keys, new_values, cache_keys, cache_values, cache_len):
    local_rows = queries.shape[0]
    cache_span = cache_keys.shape[1]
    group_size = H // KVH
    query_heads = queries.reshape(local_rows, KVH, group_size, HD)
    past_keys = cache_keys.reshape(local_rows, cache_span, KVH, HD)
    past_values = cache_values.reshape(local_rows, cache_span, KVH, HD)
    score_scale = 1.0 / math.sqrt(HD)
    past_scores = (
        jnp.einsum("tgqd,tcgd->tgqc", query_heads, past_keys, preferred_element_type=jnp.float32)
        * score_scale
    )
    own_scores = (
        jnp.einsum(
            "tgqd,tgd->tgq",
            query_heads,
            new_keys.reshape(local_rows, KVH, HD),
            preferred_element_type=jnp.float32,
        )
        * score_scale
    )
    is_valid = lax.broadcasted_iota(jnp.int32, (local_rows, cache_span), 1) < cache_len[:, None]
    past_scores = jnp.where(is_valid[:, None, None, :], past_scores, -1e30)
    peak_score = jnp.maximum(jnp.max(past_scores, axis=3), own_scores)
    past_exp = jnp.exp(past_scores - peak_score[..., None])
    own_exp = jnp.exp(own_scores - peak_score)
    denom_sum = jnp.sum(past_exp, axis=3) + own_exp
    past_weights = (past_exp / denom_sum[..., None]).astype(jnp.bfloat16)
    own_weights = (own_exp / denom_sum).astype(jnp.bfloat16)
    blended = jnp.einsum(
        "tgqc,tcgd->tgqd", past_weights, past_values, preferred_element_type=jnp.float32
    )
    blended = blended + own_weights.astype(jnp.float32)[..., None] * new_values.reshape(
        local_rows, KVH, 1, HD
    ).astype(jnp.float32)
    return blended.reshape(local_rows, H * HD).astype(jnp.bfloat16)


def local(
    resid,
    queries,
    new_keys,
    new_values,
    cache_keys,
    cache_values,
    cache_len,
    out_proj,
    norm_gain,
    router,
    expert_ids,
    gate_slab,
    up_slab,
    down_slab,
):
    rows = resid.shape[0]
    chips = lax.axis_size("chip")
    groups = lax.axis_size("chip") * lax.axis_size("core")
    core = lax.axis_index("core")
    half = lax.axis_index("dp") // 2

    other_proj = flipped(out_proj, "core", 1)
    other_down = flipped(down_slab, "dp", 1)
    ids = jnp.concatenate([expert_ids] + [flipped(expert_ids, "dp", m) for m in (3, 1, 2)], axis=0)

    attended = attend(queries, new_keys, new_values, cache_keys, cache_values, cache_len)
    piece = out_proj.shape[0]
    pieces = attended.reshape(rows, chips, 2, piece)
    first = jnp.where(core == 0, pieces[:, :, 0], pieces[:, :, 1])
    second = jnp.where(core == 0, pieces[:, :, 1], pieces[:, :, 0])
    sent = jnp.concatenate([first, second], axis=2).transpose(1, 0, 2)
    regrouped = lax.all_to_all(sent, "chip", split_axis=0, concat_axis=0, tiled=True)
    regrouped = regrouped.reshape(chips * rows, 2 * piece)
    partial = jnp.dot(regrouped[:, :piece], out_proj, preferred_element_type=jnp.float32)
    partial = partial + jnp.dot(
        regrouped[:, piece:], other_proj, preferred_element_type=jnp.float32
    )
    partial = lax.all_to_all(
        partial.astype(jnp.bfloat16).reshape(chips, rows, D),
        "chip",
        split_axis=0,
        concat_axis=0,
        tiled=True,
    )
    hidden = resid.astype(jnp.float32) + jnp.sum(partial.astype(jnp.float32), axis=0)
    meansq = jnp.mean(hidden * hidden, axis=1, keepdims=True)
    normed = (hidden * lax.rsqrt(jnp.maximum(meansq, 0.25)) * norm_gain).astype(jnp.bfloat16)

    mirror = flipped(normed, "dp", 3)
    tokens = jnp.concatenate(
        [normed, mirror, flipped(normed, "dp", 1), flipped(normed, "dp", 2)], axis=0
    )

    count = tokens.shape[0]
    labels = 2 * jnp.arange(groups, dtype=jnp.int32) + half
    hits = ids.T[:, None, :] == labels[None, :, None]
    member = jnp.any(hits, axis=0)
    at = jnp.arange(count, dtype=jnp.int32)
    before = (at[:, None] < at[None, :]) & (at[:, None] // rows == at[None, :] // rows)
    rank = jnp.dot(
        member.astype(jnp.bfloat16),
        before.astype(jnp.bfloat16),
        preferred_element_type=jnp.float32,
    ).astype(jnp.int32)
    place = jnp.where(member, rank + CAP * (at // rows)[None, :], -1)
    slots = CAP * (count // rows)
    dispatch = place[:, None, :] == jnp.arange(slots, dtype=jnp.int32)[None, :, None]
    outgoing = jnp.dot(
        dispatch.reshape(groups * slots, count).astype(jnp.bfloat16),
        tokens,
        preferred_element_type=jnp.float32,
    ).astype(jnp.bfloat16)
    incoming = lax.all_to_all(
        outgoing.reshape(groups, slots, D), EP, split_axis=0, concat_axis=0, tiled=True
    )

    kept = 2 * rows
    logits = jnp.dot(
        jnp.concatenate([normed, mirror], axis=0), router, preferred_element_type=jnp.float32
    )
    experts = router.shape[1]
    onehot = ids[:kept, :, None] == jnp.arange(experts, dtype=jnp.int32)[None, None, :]
    chosen = jnp.sum(jnp.where(onehot, logits[:, None, :], 0.0), axis=2)
    peak_logit = jnp.max(chosen, axis=1, keepdims=True)
    exp_logit = jnp.exp(chosen - peak_logit)
    gate_probs = (exp_logit / jnp.sum(exp_logit, axis=1, keepdims=True)).astype(jnp.bfloat16)
    spread = jnp.sum(
        jnp.where(hits[:, :, :kept], gate_probs.astype(jnp.float32).T[:, None, :], 0.0), axis=0
    )
    back = slots // 2
    combine = jnp.where(
        place[:, None, :kept] == jnp.arange(back, dtype=jnp.int32)[None, :, None],
        spread[:, None, :],
        0.0,
    ).astype(jnp.bfloat16)

    flat = incoming.reshape(groups * slots, D)
    gate_val = jnp.dot(flat, gate_slab[0], preferred_element_type=jnp.float32)
    up_val = jnp.dot(flat, up_slab[0], preferred_element_type=jnp.float32)
    act = (jax.nn.silu(gate_val) * up_val).astype(jnp.bfloat16).reshape(groups, slots, -1)
    other_act = flipped(act[:, back:].reshape(groups * back, -1), "dp", 1)
    produced = jnp.dot(
        act[:, :back].reshape(groups * back, -1), down_slab[0], preferred_element_type=jnp.float32
    )
    produced = produced + jnp.dot(other_act, other_down[0], preferred_element_type=jnp.float32)
    returned = lax.all_to_all(
        produced.astype(jnp.bfloat16).reshape(groups, back, D),
        EP,
        split_axis=0,
        concat_axis=0,
        tiled=True,
    )
    mix = lax.dot_general(
        combine.reshape(groups * back, kept),
        returned.reshape(groups * back, D),
        (((0,), (0,)), ((), ())),
        preferred_element_type=jnp.float32,
    )
    return hidden + mix[:rows] + flipped(mix[rows:], "dp", 3)


def solution(mesh):
    split = Mesh(mesh.devices.reshape(-1, 2, mesh.shape["dp"]), ALL)
    in_specs = (
        P(ALL, None),
        P(ALL, None),
        P(ALL, None),
        P(ALL, None),
        P(ALL, None, None),
        P(ALL, None, None),
        P(ALL),
        P(EP, None),
        P(),
        P(),
        P(ALL, None),
        P(ALL, None, None),
        P(ALL, None, None),
        P(ALL, None, None),
    )
    return jax.shard_map(
        local, mesh=split, in_specs=in_specs, out_specs=P(ALL, None), check_vma=False
    )
```

time: 359 us -> 218 us (0.61)
  waiting for transfers between devices: 244 us -> 111 us
  starting transfers between devices: 23.4 us -> 37.8 us
  between operations: 13.6 us -> 0.28 us
  local copies, waits for them, and re-layouts: 20 us -> 7.82 us
  other arithmetic: 3.57 us -> 11.4 us
  matrix products: 36.6 us -> 32.2 us
    ppermute x3 -> x10, waiting for transfers between devices: 110 us -> 22.3 us  [flipped(): return lax.ppermute(value, axis, pairs)]
    reduce_scatter x1 -> x0, waiting for transfers between devices: 76.6 us -> none  [local(): lax.psum_scatter(jnp.dot(regrouped, out_proj, preferred_element_type=jnp....]
    all_to_all x2 -> x3, waiting for transfers between devices: 57.6 us -> 89.2 us  [the longest x1 48.7 us: local(): lax.all_to_all(outgoing.reshape(groups, slots, D), EP, split_axis=0, conc...]
    reshape x4 -> x1, local copies, waits for them, and re-layouts: 17 us -> 0.02 us  [local(): other_act = flipped(act[:, back:].reshape(groups * back, -1), 'dp', 1)]
    ppermute x3 -> x10, starting transfers between devices: 3.55 us -> 17.5 us  [flipped(): return lax.ppermute(value, axis, pairs)]
    dot_general x8 -> x10, matrix products: 32.6 us -> 27.4 us  [the longest x1 4.71 us: local(): up_val = jnp.dot(flat, up_slab[0], preferred_element_type=jnp.float32)]
    all_to_all x2 -> x3, starting transfers between devices: 19.9 us -> 20.3 us  [the longest x1 8.15 us: local(): lax.all_to_all(produced.astype(jnp.bfloat16).reshape(groups, back, D), EP...]
  transfers between devices with their start and end apart: 6 -> 13, of which waited for: 5 -> 11; matrix products, arithmetic and copies ran while one was open for 8% -> 16% of each run, Pallas kernels for 0% -> 0%
where the time goes in v1:
time: 218 us; the launch traced here: 216 us
  waiting for transfers between devices  111 us (51%)
  starting transfers between devices  37.8 us (17%)
  matrix products  32.2 us (15%)
  blocking collectives  15.5 us (7%)
  other arithmetic  11.4 us (5%)
  local copies, waits for them, and re-layouts  7.82 us (4%)
    all_to_all x1, waiting for transfers between devices, local(): lax.all_to_all(outgoing.reshape(groups, slots, D), EP, split_axis=0, conc...  48.7 us
    ppermute x10, waiting for transfers between devices, flipped(): return lax.ppermute(value, axis, pairs)  22.3 us
    all_to_all x1, waiting for transfers between devices, local(): lax.all_to_all(partial.astype(jnp.bfloat16).reshape(chips, rows, D), 'chi...  21.1 us
    all_to_all x1, waiting for transfers between devices, local(): lax.all_to_all(produced.astype(jnp.bfloat16).reshape(groups, back, D), EP...  19.4 us
    ppermute x10, starting transfers between devices, flipped(): return lax.ppermute(value, axis, pairs)  17.5 us
    all_to_all x1, blocking collectives, local(): lax.all_to_all(sent, 'chip', split_axis=0, concat_axis=0, tiled=True)  15.5 us
    all_to_all x1, starting transfers between devices, local(): lax.all_to_all(produced.astype(jnp.bfloat16).reshape(groups, back, D), EP...  8.15 us
    all_to_all x1, starting transfers between devices, local(): lax.all_to_all(outgoing.reshape(groups, slots, D), EP, split_axis=0, conc...  7.59 us
  transfers between devices with their start and end apart: 13, of which 11 were waited for; matrix products, arithmetic and copies ran while one was open for 16% of the time, Pallas kernels for 0%

profile of v1, /device:TPU:1, one launch (start us, length us, event | category | flops | bytes accessed | tf_op | source)
XLA Modules:
  0.0 216.5 jit_solution(9645194923921128882)
XLA Ops:
  4.8 3.0 %fusion.71 = (f32[16,4,16]{2,1,0:T(4,128)S(1)}, f32[16,4,16,128]{3,2,1,0:T(8,128)S(1)}) fusion(bf16[16,4,16,128]{3,2,1,0:T(8,128)(2,1)S(1)} %bitcast.90, pred[16,128]{1,0:T(8,128)(4,1)S(1)} %iota_compare_fusion.3, bf16[16,128,512]{2,1,0:T(8,128)(2,1)} %param.18), kind=kOutput, calls=%fused_computation.99 | convolution fusion | flops 33946624 | bytes 2889728 | tf_op jit(solution)/shard_map/tgqd,tcgd->tgqc/dot_general | solution.py:35
  11.8 15.5 %all_to_all.20 = bf16[16,16,512]{2,1,0:T(8,128)(2,1)S(1)} all-to-all(bf16[16,16,512]{2,1,0:T(8,128)(2,1)S(1)} %copy.56), channel_id=1, replica_groups=mesh['chip'=16,'core'=2,'dp'=4] {'chip'}, dimensions={0} | all-to-all | bytes 524288 | tf_op jit(solution)/shard_map/all_to_all | solution.py:96
  28.0 3.7 %fusion = bf16[256,4096]{1,0:T(8,128)(2,1)} fusion(f32[256,4096]{1,0:T(8,128)S(1)} %fusion.53, bf16[256,4096]{1,0:T(8,128)(2,1)} %collective-permute-done, bf16[256,512]{1,0:T(8,128)(2,1)S(1)} %bitcast.88), kind=kOutput, calls=%fused_computation.3 | convolution fusion | flops 538968064 | bytes 8519680 | tf_op jit(solution)/shard_map/dot_general | solution.py:99
  31.7 4.6 %all-to-all-start.1 = ((bf16[16,16,4096]{2,1,0:T(8,128)(2,1)}), bf16[16,16,4096]{2,1,0:T(8,128)(2,1)}, u32[]{:S(2)}, u32[]{:S(2)}) async-start(bf16[16,16,4096]{2,1,0:T(8,128)(2,1)} %bitcast.86), calls=%async_computation.1 | async-start | bytes 4194304 | tf_op jit(solution)/shard_map/all_to_all | solution.py:102
  36.3 3.8 %collective-permute-start.1 = (s32[16,8]{0,1:T(8,128)S(1)}, s32[16,8]{0,1:T(8,128)S(1)}, u32[]{:S(2)}, u32[]{:S(2)}) collective-permute-start(s32[16,8]{0,1:T(8,128)S(1)} %copy-done.7), channel_id=1, source_target_pairs={{0,3},{1,2},{2,1},{3,0},{4,7},{5,6},{6,5},{7,4},{8,11},{9,10},{10,... | collective-permute-start | bytes 1544 | tf_op jit(solution)/shard_map/ppermute | solution.py:23
  45.5 21.1 %all-to-all-done.1 = bf16[16,16,4096]{2,1,0:T(8,128)(2,1)} async-done(((bf16[16,16,4096]{2,1,0:T(8,128)(2,1)}), bf16[16,16,4096]{2,1,0:T(8,128)(2,1)}, u32[]{:S(2)}, u32[]{:S(2)}) %all-to-all-start.1) | async-done | bytes 2097184 | tf_op jit(solution)/shard_map/all_to_all | solution.py:102
  66.6 1.9 convert_reduce_fusion
  68.8 3.8 %collective-permute-start.4 = (bf16[16,4096]{1,0:T(8,128)(2,1)S(1)}, bf16[16,4096]{1,0:T(8,128)(2,1)S(1)}, u32[]{:S(2)}, u32[]{:S(2)}) collective-permute-start(bf16[16,4096]{1,0:T(8,128)(2,1)S(1)} %multiply_convert_fusion), channel_id=1, source_target_pairs={{0,3},{1,2},{2,1},{3,0},{4,7},{5,6},{6,5},{7,4},{8,11},{9,10},{10,... | collective-permute-start | bytes 393224 | tf_op jit(solution)/shard_map/ppermute | solution.py:23
  75.0 1.8 collective-permute-done.5
  78.4 3.2 %convolution_convert_fusion = bf16[512,4096]{1,0:T(8,128)(2,1)} fusion(pred[512,64]{1,0:T(32,128)(4,1)S(1)} %bitcast_compare_fusion, bf16[16,4096]{1,0:T(8,128)(2,1)S(1)} %collective-permute-done.6, bf16[16,4096]{1,0:T(8,128)(2,1)S(1)} %collective-permute-done.5, bf16[16,4096]{1,0:T(8,128)(2,1)S(1)} %collective-permute-done.4, ...), kind=kOutput, calls=%fused_computation | convolution fusion | flops 272629760 | bytes 4751360 | tf_op jit(solution)/shard_map/dot_general | solution.py:132
  81.6 7.6 %all-to-all-start.2 = ((bf16[32,16,4096]{2,1,0:T(8,128)(2,1)}), bf16[32,16,4096]{2,1,0:T(8,128)(2,1)}, u32[]{:S(2)}, u32[]{:S(2)}) async-start(bf16[32,16,4096]{2,1,0:T(8,128)(2,1)} %bitcast.85), calls=%async_computation.2 | async-start | bytes 8388608 | tf_op jit(solution)/shard_map/all_to_all | solution.py:137
  89.2 2.0 collective-permute-start.8
  91.2 48.7 %all-to-all-done.2 = bf16[32,16,4096]{2,1,0:T(8,128)(2,1)} async-done(((bf16[32,16,4096]{2,1,0:T(8,128)(2,1)}), bf16[32,16,4096]{2,1,0:T(8,128)(2,1)}, u32[]{:S(2)}, u32[]{:S(2)}) %all-to-all-start.2) | async-done | bytes 4194336 | tf_op jit(solution)/shard_map/all_to_all | solution.py:137
  139.9 4.7 %fusion.8 = f32[512,384]{1,0:T(8,128)S(1)} fusion(bf16[512,4096]{1,0:T(8,128)(2,1)} %bitcast.11, bf16[1,4096,384]{2,1,0:T(8,128)(2,1)S(1)} %copy-done), kind=kOutput, calls=%fused_computation.13 | convolution fusion | flops 1610612736 | bytes 8126464 | tf_op jit(solution)/shard_map/dot_general | solution.py:162
  144.6 4.7 %fusion.20 = bf16[512,384]{1,0:T(8,128)(2,1)S(1)} fusion(bf16[512,4096]{1,0:T(8,128)(2,1)} %bitcast.11, bf16[1,4096,384]{2,1,0:T(8,128)(2,1)S(1)} %copy-done.11, f32[512,384]{1,0:T(8,128)S(1)} %fusion.8), kind=kOutput, calls=%fused_computation.23 | convolution fusion | flops 1611792384 | bytes 8519680 | tf_op jit(solution)/shard_map/dot_general | solution.py:163
  149.4 1.8 collective-permute-start.7
  152.5 7.1 %collective-permute-done.8 = bf16[1,384,4096]{2,1,0:T(8,128)(2,1)} collective-permute-done((bf16[1,384,4096]{2,1,0:T(8,128)(2,1)}, bf16[1,384,4096]{2,1,0:T(8,128)(2,1)}, u32[]{:S(2)}, u32[]{:S(2)}) %collective-permute-start.8) | collective-permute-done | bytes 3145760 | tf_op jit(solution)/shard_map/ppermute | solution.py:23
  159.6 4.1 %collective-permute-done.7 = bf16[256,384]{1,0:T(8,128)(2,1)S(1)} collective-permute-done((bf16[256,384]{1,0:T(8,128)(2,1)S(1)}, bf16[256,384]{1,0:T(8,128)(2,1)S(1)}, u32[]{:S(2)}, u32[]{:S(2)}) %collective-permute-start.7) | collective-permute-done | bytes 196640 | tf_op jit(solution)/shard_map/ppermute | solution.py:23
  163.7 4.6 %fusion.2 = bf16[32,8,4096]{2,1,0:T(8,128)(2,1)} fusion(f32[256,4096]{1,0:T(8,128)S(1)} %fusion.4, bf16[256,384]{1,0:T(8,128)(2,1)S(1)} %collective-permute-done.7, bf16[1,384,4096]{2,1,0:T(8,128)(2,1)} %collective-permute-done.8), kind=kOutput, calls=%fused_computation.5 | convolution fusion | flops 807403520 | bytes 9633792 | tf_op jit(solution)/shard_map/dot_general | solution.py:169
  168.3 8.2 %all-to-all-start.3 = ((bf16[32,8,4096]{2,1,0:T(8,128)(2,1)}), bf16[32,8,4096]{2,1,0:T(8,128)(2,1)}, u32[]{:S(2)}, u32[]{:S(2)}) async-start(bf16[32,8,4096]{2,1,0:T(8,128)(2,1)} %fusion.2), calls=%async_computation.3 | async-start | bytes 4194304 | tf_op jit(solution)/shard_map/all_to_all | solution.py:170
  185.8 19.4 %all-to-all-done.3 = bf16[32,8,4096]{2,1,0:T(8,128)(2,1)} async-done(((bf16[32,8,4096]{2,1,0:T(8,128)(2,1)}), bf16[32,8,4096]{2,1,0:T(8,128)(2,1)}, u32[]{:S(2)}, u32[]{:S(2)}) %all-to-all-start.3) | async-done | bytes 2097184 | tf_op jit(solution)/shard_map/all_to_all | solution.py:170
  205.2 3.0 %convolution_bitcast_fusion = f32[32,4096]{1,0:T(8,128)S(1)} fusion(bf16[32,8,4096]{2,1,0:T(8,128)(2,1)} %all-to-all-done.3, bf16[32,32]{0,1:T(8,128)(2,1)S(1)} %copy.61, s32[32,32]{0,1:T(8,128)} %copy.57), kind=kOutput, calls=%fused_computation.6 | convolution fusion | flops 67125248 | bytes 2627584 | tf_op jit(solution)/shard_map/dot_general | solution.py:177
  208.2 2.1 collective-permute-start.9
  210.3 5.4 %collective-permute-done.9 = f32[16,4096]{1,0:T(8,128)S(1)} collective-permute-done((f32[16,4096]{1,0:T(8,128)S(1)}, f32[16,4096]{1,0:T(8,128)S(1)}, u32[]{:S(2)}, u32[]{:S(2)}) %collective-permute-start.9) | collective-permute-done | bytes 262176 | tf_op jit(solution)/shard_map/ppermute | solution.py:23
  (82 shorter events, 30.4 us)
Async XLA Ops:
  0.0 139.9 %copy-start = (bf16[1,4096,384]{2,1,0:T(8,128)(2,1)S(1)}, bf16[1,4096,384]{2,1,0:T(8,128)(2,1)}, u32[]{:S(2)}) copy-start(bf16[1,4096,384]{2,1,0:T(8,128)(2,1)} %param.25) | copy-start | bytes 9437188
  0.0 27.9 %collective-permute-start = (bf16[256,4096]{1,0:T(8,128)(2,1)}, bf16[256,4096]{1,0:T(8,128)(2,1)}, u32[]{:S(2)}, u32[]{:S(2)}) collective-permute-start(bf16[256,4096]{1,0:T(8,128)(2,1)} %param.21), channel_id=1, source_target_pairs={{0,4},{4,0},{1,5},{5,1},{2,6},{6,2},{3,7},{7,3},{8,12},{12,8},{9,1... | collective-permute-start | bytes 6291464 | tf_op jit(solution)/shard_map/ppermute | solution.py:23
  11.0 16.3 %copy-start.2 = (bf16[256,4096]{1,0:T(8,128)(2,1)S(1)}, bf16[256,4096]{1,0:T(8,128)(2,1)}, u32[]{:S(2)}) copy-start(bf16[256,4096]{1,0:T(8,128)(2,1)} %param.21) | copy-start | bytes 6291460
  31.7 36.8 %copy-start.3 = (bf16[16,4096]{1,0:T(8,128)(2,1)S(1)}, bf16[16,4096]{1,0:T(8,128)(2,1)}, u32[]{:S(2)}) copy-start(bf16[16,4096]{1,0:T(8,128)(2,1)} %param.14) | copy-start | bytes 393220
  31.7 37.0 %copy-start.6 = (f32[4096]{0:T(1024)S(1)}, f32[4096]{0:T(1024)}, u32[]{:S(2)}) copy-start(f32[4096]{0:T(1024)} %param.22) | copy-start | bytes 49156
  31.7 34.9 %all-to-all-start.1 = ((bf16[16,16,4096]{2,1,0:T(8,128)(2,1)}), bf16[16,16,4096]{2,1,0:T(8,128)(2,1)}, u32[]{:S(2)}, u32[]{:S(2)}) async-start(bf16[16,16,4096]{2,1,0:T(8,128)(2,1)} %bitcast.86), calls=%async_computation.1 | async-start | bytes 4194304 | tf_op jit(solution)/shard_map/all_to_all | solution.py:102
  36.3 6.4 %collective-permute-start.1 = (s32[16,8]{0,1:T(8,128)S(1)}, s32[16,8]{0,1:T(8,128)S(1)}, u32[]{:S(2)}, u32[]{:S(2)}) collective-permute-start(s32[16,8]{0,1:T(8,128)S(1)} %copy-done.7), channel_id=1, source_target_pairs={{0,3},{1,2},{2,1},{3,0},{4,7},{5,6},{6,5},{7,4},{8,11},{9,10},{10,... | collective-permute-start | bytes 1544 | tf_op jit(solution)/shard_map/ppermute | solution.py:23
  40.1 2.9 %collective-permute-start.2 = (s32[16,8]{0,1:T(8,128)S(1)}, s32[16,8]{0,1:T(8,128)S(1)}, u32[]{:S(2)}, u32[]{:S(2)}) collective-permute-start(s32[16,8]{0,1:T(8,128)S(1)} %copy-done.7), channel_id=1, source_target_pairs={{0,1},{1,0},{2,3},{3,2},{4,5},{5,4},{6,7},{7,6},{8,9},{9,8},{10,11... | collective-permute-start | bytes 1544 | tf_op jit(solution)/shard_map/ppermute | solution.py:23
  40.1 4.0 %collective-permute-start.3 = (s32[16,8]{0,1:T(8,128)S(1)}, s32[16,8]{0,1:T(8,128)S(1)}, u32[]{:S(2)}, u32[]{:S(2)}) collective-permute-start(s32[16,8]{0,1:T(8,128)S(1)} %copy-done.7), channel_id=1, source_target_pairs={{0,2},{1,3},{2,0},{3,1},{4,6},{5,7},{6,4},{7,5},{8,10},{9,11},{10,... | collective-permute-start | bytes 1544 | tf_op jit(solution)/shard_map/ppermute | solution.py:23
  66.6 7.3 %copy-start.10 = (pred[32,64]{1,0:T(8,128)(4,1)S(1)}, pred[32,64]{1,0:T(8,128)(4,1)}, u32[]{:S(2)}) copy-start(pred[32,64]{1,0:T(8,128)(4,1)} %get-tuple-element.12) | copy-start | bytes 6148
  66.6 7.3 %copy-start.13 = (s32[64]{0:T(128)S(1)}, s32[64]{0:T(128)}, u32[]{:S(2)}) copy-start(s32[64]{0:T(128)} %get-tuple-element.15) | copy-start | bytes 772
  66.6 7.3 %copy-start.14 = (s32[64]{0:T(128)S(1)}, s32[64]{0:T(128)}, u32[]{:S(2)}) copy-start(s32[64]{0:T(128)} %get-tuple-element.16) | copy-start | bytes 772
  66.6 7.5 %copy-start.9 = (s32[512]{0:T(512)S(1)}, s32[512]{0:T(512)}, u32[]{:S(2)}) copy-start(s32[512]{0:T(512)} %eq.92) | copy-start | bytes 6148
  68.8 12.8 %copy-start.4 = (bf16[16,4096]{1,0:T(8,128)(2,1)}, bf16[16,4096]{1,0:T(8,128)(2,1)S(1)}, u32[]{:S(2)}) copy-start(bf16[16,4096]{1,0:T(8,128)(2,1)S(1)} %multiply_convert_fusion) | copy-start | bytes 393220
  68.8 6.2 %collective-permute-start.4 = (bf16[16,4096]{1,0:T(8,128)(2,1)S(1)}, bf16[16,4096]{1,0:T(8,128)(2,1)S(1)}, u32[]{:S(2)}, u32[]{:S(2)}) collective-permute-start(bf16[16,4096]{1,0:T(8,128)(2,1)S(1)} %multiply_convert_fusion), channel_id=1, source_target_pairs={{0,3},{1,2},{2,1},{3,0},{4,7},{5,6},{6,5},{7,4},{8,11},{9,10},{10,... | collective-permute-start | bytes 393224 | tf_op jit(solution)/shard_map/ppermute | solution.py:23
  72.6 4.1 %collective-permute-start.5 = (bf16[16,4096]{1,0:T(8,128)(2,1)S(1)}, bf16[16,4096]{1,0:T(8,128)(2,1)S(1)}, u32[]{:S(2)}, u32[]{:S(2)}) collective-permute-start(bf16[16,4096]{1,0:T(8,128)(2,1)S(1)} %multiply_convert_fusion), channel_id=1, source_target_pairs={{0,1},{1,0},{2,3},{3,2},{4,5},{5,4},{6,7},{7,6},{8,9},{9,8},{10,11... | collective-permute-start | bytes 393224 | tf_op jit(solution)/shard_map/ppermute | solution.py:23
  72.6 5.8 %collective-permute-start.6 = (bf16[16,4096]{1,0:T(8,128)(2,1)S(1)}, bf16[16,4096]{1,0:T(8,128)(2,1)S(1)}, u32[]{:S(2)}, u32[]{:S(2)}) collective-permute-start(bf16[16,4096]{1,0:T(8,128)(2,1)S(1)} %multiply_convert_fusion), channel_id=1, source_target_pairs={{0,2},{1,3},{2,0},{3,1},{4,6},{5,7},{6,4},{7,5},{8,10},{9,11},{10,... | collective-permute-start | bytes 393224 | tf_op jit(solution)/shard_map/ppermute | solution.py:23
  75.0 6.7 %copy-start.5 = (bf16[16,4096]{1,0:T(8,128)(2,1)}, bf16[16,4096]{1,0:T(8,128)(2,1)S(1)}, u32[]{:S(2)}) copy-start(bf16[16,4096]{1,0:T(8,128)(2,1)S(1)} %collective-permute-done.4) | copy-start | bytes 393220
  81.6 58.3 %all-to-all-start.2 = ((bf16[32,16,4096]{2,1,0:T(8,128)(2,1)}), bf16[32,16,4096]{2,1,0:T(8,128)(2,1)}, u32[]{:S(2)}, u32[]{:S(2)}) async-start(bf16[32,16,4096]{2,1,0:T(8,128)(2,1)} %bitcast.85), calls=%async_computation.2 | async-start | bytes 8388608 | tf_op jit(solution)/shard_map/all_to_all | solution.py:137
  89.2 70.4 %collective-permute-start.8 = (bf16[1,384,4096]{2,1,0:T(8,128)(2,1)}, bf16[1,384,4096]{2,1,0:T(8,128)(2,1)}, u32[]{:S(2)}, u32[]{:S(2)}) collective-permute-start(bf16[1,384,4096]{2,1,0:T(8,128)(2,1)} %param.27), channel_id=1, source_target_pairs={{0,1},{1,0},{2,3},{3,2},{4,5},{5,4},{6,7},{7,6},{8,9},{9,8},{10,11... | collective-permute-start | bytes 9437192 | tf_op jit(solution)/shard_map/ppermute | solution.py:23
  144.6 6.6 %copy-start.1 = (bf16[1,384,4096]{2,1,0:T(8,128)(2,1)S(1)}, bf16[1,384,4096]{2,1,0:T(8,128)(2,1)}, u32[]{:S(2)}) copy-start(bf16[1,384,4096]{2,1,0:T(8,128)(2,1)} %param.27) | copy-start | bytes 9437188
  149.4 14.4 %collective-permute-start.7 = (bf16[256,384]{1,0:T(8,128)(2,1)S(1)}, bf16[256,384]{1,0:T(8,128)(2,1)S(1)}, u32[]{:S(2)}, u32[]{:S(2)}) collective-permute-start(bf16[256,384]{1,0:T(8,128)(2,1)S(1)} %slice_bitcast_fusion), channel_id=1, source_target_pairs={{0,1},{1,0},{2,3},{3,2},{4,5},{5,4},{6,7},{7,6},{8,9},{9,8},{10,11... | collective-permute-start | bytes 589832 | tf_op jit(solution)/shard_map/ppermute | solution.py:23
  168.3 36.9 %all-to-all-start.3 = ((bf16[32,8,4096]{2,1,0:T(8,128)(2,1)}), bf16[32,8,4096]{2,1,0:T(8,128)(2,1)}, u32[]{:S(2)}, u32[]{:S(2)}) async-start(bf16[32,8,4096]{2,1,0:T(8,128)(2,1)} %fusion.2), calls=%async_computation.3 | async-start | bytes 4194304 | tf_op jit(solution)/shard_map/all_to_all | solution.py:170
  208.2 7.5 %collective-permute-start.9 = (f32[16,4096]{1,0:T(8,128)S(1)}, f32[16,4096]{1,0:T(8,128)S(1)}, u32[]{:S(2)}, u32[]{:S(2)}) collective-permute-start(f32[16,4096]{1,0:T(8,128)S(1)} %slice.53), channel_id=1, source_target_pairs={{0,3},{1,2},{2,1},{3,0},{4,7},{5,6},{6,5},{7,4},{8,11},{9,10},{10,... | collective-permute-start | bytes 786440 | tf_op jit(solution)/shard_map/ppermute | solution.py:23
  (4 other events, 15.8 us)

commit v2 on v1

v2 whole, which is shorter than its diff:
```python
import math

import jax
import jax.numpy as jnp
from jax import lax
from jax.experimental import pallas as pl
from jax.experimental.pallas import tpu as pltpu
from jax.sharding import Mesh
from jax.sharding import PartitionSpec as P

D = 4096
H = 64
KVH = 4
HD = 128
CAP = 4
ATTN_STEPS = 2
IN_STEPS = 4
OUT_STEPS = 4


EP = ("chip", "core")
ALL = ("chip", "core", "dp")


def flipped(value, axis, mask):
    pairs = [(source, source ^ mask) for source in range(lax.axis_size(axis))]
    return lax.ppermute(value, axis, pairs)


def attention_kernel(swap, lengths, q_in, nk_in, nv_in, keys, values, out, q_buf, o_buf):
    step = pl.program_id(0)
    tokens = q_in.shape[0]
    group = H // KVH
    scale = 1.0 / math.sqrt(HD)

    @pl.when(step == 0)
    def _():
        for head in range(H):
            q_buf[pl.ds(head, tokens, stride=H), :] = q_in[:, head * HD : (head + 1) * HD].astype(
                jnp.float32
            )

    nk = nk_in[...].astype(jnp.float32)
    nv = nv_in[...].astype(jnp.float32)
    span = keys.shape[1]
    owner = lax.broadcasted_iota(jnp.int32, (H, HD), 0) // group
    position = lax.broadcasted_iota(jnp.int32, (H, span), 1)
    for local_row in range(keys.shape[0]):
        row = step * keys.shape[0] + local_row
        q = q_buf[pl.ds(row * H, H), :]
        blocks = [jnp.where(owner == g, q, 0.0).astype(jnp.bfloat16) for g in range(KVH)]
        scores = scale * lax.dot_general(
            jnp.concatenate(blocks, axis=1),
            keys[local_row],
            (((1,), (1,)), ((), ())),
            preferred_element_type=jnp.float32,
        )
        new_key = jnp.concatenate(
            [
                jnp.broadcast_to(nk[local_row : local_row + 1, g * HD : (g + 1) * HD], (group, HD))
                for g in range(KVH)
            ],
            axis=0,
        )
        new_value = jnp.concatenate(
            [
                jnp.broadcast_to(nv[local_row : local_row + 1, g * HD : (g + 1) * HD], (group, HD))
                for g in range(KVH)
            ],
            axis=0,
        )
        own = scale * jnp.sum(q * new_key, axis=1, keepdims=True)
        scores = jnp.where(position < lengths[row], scores, -1e30)
        peak = jnp.maximum(jnp.max(scores, axis=1, keepdims=True), own)
        past_exp = jnp.exp(scores - peak)
        own_exp = jnp.exp(own - peak)
        denom = jnp.sum(past_exp, axis=1, keepdims=True) + own_exp
        weights = (past_exp / denom).astype(jnp.bfloat16)
        own_weight = (own_exp / denom).astype(jnp.bfloat16).astype(jnp.float32)
        wide = jnp.dot(weights, values[local_row], preferred_element_type=jnp.float32)
        blended = jnp.concatenate(
            [wide[g * group : (g + 1) * group, g * HD : (g + 1) * HD] for g in range(KVH)], axis=0
        )
        o_buf[pl.ds(row * H, H), :] = blended + own_weight * new_value

    @pl.when(step == pl.num_programs(0) - 1)
    def _():
        chips, _, width = out.shape
        per = width // HD
        for chip in range(chips):
            for at in range(per):
                head = chip * per + at
                first = o_buf[pl.ds(head, tokens, stride=H), :]
                second = o_buf[pl.ds(chip * per + (at ^ (per // 2)), tokens, stride=H), :]
                out[chip, :, at * HD : (at + 1) * HD] = jnp.where(
                    swap[0] == 1, second, first
                ).astype(jnp.bfloat16)


def attention(swap, queries, new_keys, new_values, cache_keys, cache_values, cache_len, chips):
    rows = queries.shape[0]
    span = cache_keys.shape[1]
    each = rows // ATTN_STEPS
    smem = pl.BlockSpec(memory_space=pltpu.SMEM)
    return pl.pallas_call(
        attention_kernel,
        grid=(ATTN_STEPS,),
        out_shape=jax.ShapeDtypeStruct((chips, rows, H * HD // chips), jnp.bfloat16),
        in_specs=[
            smem,
            smem,
            pl.BlockSpec((rows, H * HD), lambda i: (0, 0)),
            pl.BlockSpec((each, KVH * HD), lambda i: (i, 0)),
            pl.BlockSpec((each, KVH * HD), lambda i: (i, 0)),
            pl.BlockSpec((each, span, KVH * HD), lambda i: (i, 0, 0)),
            pl.BlockSpec((each, span, KVH * HD), lambda i: (i, 0, 0)),
        ],
        out_specs=pl.BlockSpec((chips, rows, H * HD // chips), lambda i: (0, 0, 0)),
        scratch_shapes=[
            pltpu.VMEM((rows * H, HD), jnp.float32),
            pltpu.VMEM((rows * H, HD), jnp.float32),
        ],
        compiler_params=pltpu.CompilerParams(dimension_semantics=("arbitrary",)),
        cost_estimate=pl.CostEstimate(
            flops=8 * rows * H * HD * span, bytes_accessed=4 * rows * span * KVH * HD, transcendentals=0
        ),
        name="attention",
    )(swap, cache_len, queries, new_keys, new_values, cache_keys, cache_values)


def start_slabs(flag, own, crossed, near, far, start):
    @pl.when(flag[0] == 1)
    def _():
        start(0, own)
        start(1, crossed)

    @pl.when(flag[0] != 1)
    def _():
        start(0, near)
        start(1, far)


def act_kernel(flag, rows_in, *refs):
    own, crossed, near, far = refs[0:2], refs[2:4], refs[4:6], refs[6:8]
    out, x_buf, in_buf, x_sem, in_sem = refs[8:]
    hf = own[0].shape[2]
    span = D // IN_STEPS

    def copy(side, source, step, part):
        return pltpu.make_async_copy(
            source[part].at[0, pl.ds(step * span, span)],
            in_buf.at[side, pl.ds(step * span, span), pl.ds(part * hf, hf)],
            in_sem.at[side, step, part],
        )

    def start(side, source):
        for step in range(IN_STEPS):
            for part in range(2):
                copy(side, source, step, part).start()

    x_copy = pltpu.make_async_copy(rows_in, x_buf, x_sem)
    x_copy.start()
    start_slabs(flag, own, crossed, near, far, start)
    x_copy.wait()
    for side in range(2):
        total = None
        for step in range(IN_STEPS):
            for part in range(2):
                copy(side, own, step, part).wait()
            piece = jnp.dot(
                x_buf[:, step * span : (step + 1) * span],
                in_buf[side, step * span : (step + 1) * span],
                preferred_element_type=jnp.float32,
            )
            total = piece if total is None else total + piece
        gate_val = total[:, :hf]
        out[:, side * hf : (side + 1) * hf] = (
            gate_val / (1.0 + jnp.exp(-gate_val)) * total[:, hf:]
        ).astype(jnp.bfloat16)


def down_kernel(flag, act, own, crossed, near, far, out, buf, sem):
    hf = own.shape[1]
    wide = D // OUT_STEPS

    def copy(side, source, step):
        return pltpu.make_async_copy(
            source.at[0, :, pl.ds(step * wide, wide)],
            buf.at[pl.ds(side * hf, hf), pl.ds(step * wide, wide)],
            sem.at[side, step],
        )

    def start(side, source):
        for step in range(OUT_STEPS):
            copy(side, source, step).start()

    start_slabs(flag, own, crossed, near, far, start)
    for step in range(OUT_STEPS):
        for side in range(2):
            copy(side, own, step).wait()
        out[:, step * wide : (step + 1) * wide] = jnp.dot(
            act[...],
            buf[:, step * wide : (step + 1) * wide],
            preferred_element_type=jnp.float32,
        ).astype(jnp.bfloat16)


def expert_act(flag, rows_in, own, crossed, near, far):
    count = rows_in.shape[0]
    hf = own[0].shape[2]
    return pl.pallas_call(
        act_kernel,
        out_shape=jax.ShapeDtypeStruct((count, 2 * hf), jnp.bfloat16),
        in_specs=[pl.BlockSpec(memory_space=pltpu.SMEM)]
        + [pl.BlockSpec(memory_space=pltpu.HBM)] * 9,
        out_specs=pl.BlockSpec(memory_space=pltpu.VMEM),
        scratch_shapes=[
            pltpu.VMEM((count, D), jnp.bfloat16),
            pltpu.VMEM((2, D, 2 * hf), jnp.bfloat16),
            pltpu.SemaphoreType.DMA,
            pltpu.SemaphoreType.DMA((2, IN_STEPS, 2)),
        ],
        compiler_params=pltpu.CompilerParams(vmem_limit_bytes=28 * 1024 * 1024),
        cost_estimate=pl.CostEstimate(
            flops=8 * count * D * hf, bytes_accessed=8 * D * hf + 2 * count * D, transcendentals=0
        ),
        name="expert_act",
    )(flag, rows_in, *own, *crossed, *near, *far)


def expert_down(flag, act, own, crossed, near, far):
    count = act.shape[0]
    hf = own.shape[1]
    return pl.pallas_call(
        down_kernel,
        out_shape=jax.ShapeDtypeStruct((count, D), jnp.bfloat16),
        in_specs=[pl.BlockSpec(memory_space=pltpu.SMEM), pl.BlockSpec(memory_space=pltpu.VMEM)]
        + [pl.BlockSpec(memory_space=pltpu.HBM)] * 4,
        out_specs=pl.BlockSpec(memory_space=pltpu.VMEM),
        scratch_shapes=[
            pltpu.VMEM((2 * hf, D), jnp.bfloat16),
            pltpu.SemaphoreType.DMA((2, OUT_STEPS)),
        ],
        compiler_params=pltpu.CompilerParams(vmem_limit_bytes=20 * 1024 * 1024),
        cost_estimate=pl.CostEstimate(
            flops=4 * count * D * hf, bytes_accessed=4 * D * hf + 2 * count * D, transcendentals=0
        ),
        name="expert_down",
    )(flag, act, own, crossed, near, far)


def local(
    resid,
    queries,
    new_keys,
    new_values,
    cache_keys,
    cache_values,
    cache_len,
    out_proj,
    norm_gain,
    router,
    expert_ids,
    gate_slab,
    up_slab,
    down_slab,
):
    rows = resid.shape[0]
    chips = lax.axis_size("chip")
    core = lax.axis_index("core")
    depth = lax.axis_index("dp")
    depths = lax.axis_size("dp")

    other_proj = flipped(out_proj, "core", 1)
    places = [(c, d) for c in range(2) for d in range(depths)]
    across = [(c * depths + d, c * depths + (d ^ 1)) for c, d in places if c != d % 2]
    beside = [(c * depths + d, (1 - c) * depths + d) for c, d in places if c == d % 2]

    def spread_out(slab):
        crossed = lax.ppermute(slab, ("core", "dp"), across)
        return crossed, lax.ppermute(slab, ("core", "dp"), beside)

    def shared(slab, after):
        held, _ = lax.optimization_barrier((slab, after))
        return lax.ppermute(held, ("core", "dp"), beside)

    gate_crossed, gate_near = spread_out(gate_slab)
    up_crossed, up_near = spread_out(up_slab)
    down_crossed, down_near = spread_out(down_slab)
    flag = (core == depth % 2).astype(jnp.int32).reshape(1)
    ids = jnp.concatenate([expert_ids] + [flipped(expert_ids, "dp", m) for m in (1, 2, 3)], axis=0)

    piece = out_proj.shape[0]
    sent = attention(
        core.astype(jnp.int32).reshape(1),
        queries,
        new_keys,
        new_values,
        cache_keys,
        cache_values,
        cache_len,
        chips,
    )
    regrouped = lax.all_to_all(sent, "chip", split_axis=0, concat_axis=0, tiled=True)
    regrouped = regrouped.reshape(chips * rows, 2 * piece)
    partial = jnp.dot(regrouped[:, :piece], out_proj, preferred_element_type=jnp.float32)
    partial = partial + jnp.dot(
        regrouped[:, piece:], other_proj, preferred_element_type=jnp.float32
    )
    partial = partial.astype(jnp.bfloat16)
    gate_far = shared(gate_crossed, partial)
    partial = lax.all_to_all(
        partial.reshape(chips, rows, D),
        "chip",
        split_axis=0,
        concat_axis=0,
        tiled=True,
    )
    hidden = resid.astype(jnp.float32) + jnp.sum(partial.astype(jnp.float32), axis=0)
    meansq = jnp.mean(hidden * hidden, axis=1, keepdims=True)
    normed = (hidden * lax.rsqrt(jnp.maximum(meansq, 0.25)) * norm_gain).astype(jnp.bfloat16)

    tokens = jnp.concatenate([normed] + [flipped(normed, "dp", m) for m in (1, 2, 3)], axis=0)

    count = tokens.shape[0]
    labels = 4 * jnp.arange(chips, dtype=jnp.int32) + 2 * (depth % 2) + depth // 2
    hits = ids.T[:, None, :] == labels[None, :, None]
    member = jnp.any(hits, axis=0)
    at = jnp.arange(count, dtype=jnp.int32)
    before = (at[:, None] < at[None, :]) & (at[:, None] // rows == at[None, :] // rows)
    rank = jnp.dot(
        member.astype(jnp.bfloat16),
        before.astype(jnp.bfloat16),
        preferred_element_type=jnp.float32,
    ).astype(jnp.int32)
    place = jnp.where(member, rank + CAP * (at // rows)[None, :], -1)
    slots = CAP * depths
    dispatch = place[:, None, :] == jnp.arange(slots, dtype=jnp.int32)[None, :, None]
    outgoing = jnp.dot(
        dispatch.reshape(chips * slots, count).astype(jnp.bfloat16),
        tokens,
        preferred_element_type=jnp.float32,
    ).astype(jnp.bfloat16)
    up_far = shared(up_crossed, outgoing)
    incoming = lax.all_to_all(
        outgoing.reshape(chips, slots, D), "chip", split_axis=0, concat_axis=0, tiled=True
    )

    logits = jnp.dot(tokens, router, preferred_element_type=jnp.float32)
    experts = router.shape[1]
    onehot = ids[:, :, None] == jnp.arange(experts, dtype=jnp.int32)[None, None, :]
    chosen = jnp.sum(jnp.where(onehot, logits[:, None, :], 0.0), axis=2)
    peak_logit = jnp.max(chosen, axis=1, keepdims=True)
    exp_logit = jnp.exp(chosen - peak_logit)
    gate_probs = (exp_logit / jnp.sum(exp_logit, axis=1, keepdims=True)).astype(jnp.bfloat16)
    spread = jnp.sum(
        jnp.where(hits, gate_probs.astype(jnp.float32).T[:, None, :], 0.0), axis=0
    )
    combine = jnp.where(dispatch, spread[:, None, :], 0.0).astype(jnp.bfloat16)

    down_far = shared(down_crossed, incoming)
    act = expert_act(
        flag,
        incoming.reshape(chips * slots, D),
        (gate_slab, up_slab),
        (gate_crossed, up_crossed),
        (gate_near, up_near),
        (gate_far, up_far),
    )
    produced = expert_down(flag, act, down_slab, down_crossed, down_near, down_far)
    returned = lax.all_to_all(
        produced.reshape(chips, slots, D), "chip", split_axis=0, concat_axis=0, tiled=True
    )
    mix = lax.dot_general(
        combine.reshape(chips * slots, count),
        returned.reshape(chips * slots, D),
        (((0,), (0,)), ((), ())),
        preferred_element_type=jnp.float32,
    )
    total = hidden + mix[:rows]
    narrow = mix.astype(jnp.bfloat16)
    for m in (1, 2, 3):
        total = total + flipped(narrow[m * rows : (m + 1) * rows], "dp", m).astype(jnp.float32)
    return total


def solution(mesh):
    split = Mesh(mesh.devices.reshape(-1, 2, mesh.shape["dp"]), ALL)
    in_specs = (
        P(ALL, None),
        P(ALL, None),
        P(ALL, None),
        P(ALL, None),
        P(ALL, None, None),
        P(ALL, None, None),
        P(ALL),
        P(EP, None),
        P(),
        P(),
        P(ALL, None),
        P(ALL, None, None),
        P(ALL, None, None),
        P(ALL, None, None),
    )

    return jax.shard_map(
        local, mesh=split, in_specs=in_specs, out_specs=P(ALL, None), check_vma=False
    )
```

time: 218 us -> 274 us (1.26)
  waiting for transfers between devices: 111 us -> 148 us
  starting transfers between devices: 37.8 us -> 69.4 us
  Pallas kernels: 0 us -> 24.9 us
  matrix products: 32.2 us -> 8.33 us
  other arithmetic: 11.4 us -> 2.09 us
  local copies, waits for them, and re-layouts: 7.82 us -> 4.71 us
    ppermute x10, waiting for transfers between devices: 22.3 us -> 85.1 us  [flipped(): return lax.ppermute(value, axis, pairs)]
    all_to_all x3, waiting for transfers between devices: 89.2 us -> 62.7 us  [the longest x1 23 us: local(): lax.all_to_all(produced.reshape(chips, slots, D), 'chip', split_axis=0, c...]
    pallas_call x0 -> x3, Pallas kernels: none -> 24.9 us  [the longest x1 9.56 us: expert_act(): pl.pallas_call(act_kernel, out_shape=jax.ShapeDtypeStruct((count, 2 * hf)...]
    dot_general x10 -> x3, matrix products: 27.5 us -> 3.69 us  [the longest x1 2 us: local(): jnp.dot(dispatch.reshape(chips * slots, count).astype(jnp.bfloat16), toke...]
    ppermute x0 -> x9, starting transfers between devices: none -> 19.2 us  [the longest x3 11.4 us: spread_out(): crossed = lax.ppermute(slab, ('core', 'dp'), across)]
    ppermute x10, starting transfers between devices: 17.5 us -> 33.7 us  [flipped(): return lax.ppermute(value, axis, pairs)]
    all_to_all x3, starting transfers between devices: 20.3 us -> 16.6 us  [the longest x1 6.39 us: local(): lax.all_to_all(produced.reshape(chips, slots, D), 'chip', split_axis=0, c...]
    unnamed x31 -> x18, local copies, waits for them, and re-layouts: 1.05 us -> 4.46 us
  transfers between devices with their start and end apart: 13 -> 22, of which waited for: 11 -> 8; matrix products, arithmetic and copies ran while one was open for 16% -> 2% of each run, Pallas kernels for 0% -> 7%
where the time goes in v2:
time: 274 us; the launch traced here: 273 us
  waiting for transfers between devices  148 us (54%)
  starting transfers between devices  69.4 us (25%)
  Pallas kernels  24.9 us (9%)
  blocking collectives  15.3 us (6%)
  matrix products  8.33 us (3%)
  local copies, waits for them, and re-layouts  4.71 us (2%)
    ppermute x10, waiting for transfers between devices, flipped(): return lax.ppermute(value, axis, pairs)  85.1 us
    ppermute x10, starting transfers between devices, flipped(): return lax.ppermute(value, axis, pairs)  33.7 us
    all_to_all x1, waiting for transfers between devices, local(): lax.all_to_all(produced.reshape(chips, slots, D), 'chip', split_axis=0, c...  23 us
    all_to_all x1, waiting for transfers between devices, local(): lax.all_to_all(partial.reshape(chips, rows, D), 'chip', split_axis=0, con...  20.4 us
    all_to_all x1, waiting for transfers between devices, local(): lax.all_to_all(outgoing.reshape(chips, slots, D), 'chip', split_axis=0, c...  19.3 us
    all_to_all x1, blocking collectives, local(): lax.all_to_all(sent, 'chip', split_axis=0, concat_axis=0, tiled=True)  15.3 us
    ppermute x3, starting transfers between devices, spread_out(): crossed = lax.ppermute(slab, ('core', 'dp'), across)  11.4 us
    pallas_call x1, Pallas kernels, expert_act(): pl.pallas_call(act_kernel, out_shape=jax.ShapeDtypeStruct((count, 2 * hf)...  9.56 us
  transfers between devices with their start and end apart: 22, of which 8 were waited for; matrix products, arithmetic and copies ran while one was open for 2% of the time, Pallas kernels for 7%

profile of v2, /device:TPU:1, one launch (start us, length us, event | category | flops | bytes accessed | tf_op | source)
XLA Modules:
  0.0 273.0 jit_solution(10998751157667186029)
XLA Ops:
  1.4 9.5 %attention.1 = bf16[16,16,512]{2,1,0:T(8,128)(2,1)} custom-call(s32[1]{0:T(128)} %bitcast.swap, s32[16]{0:T(128)} %lengths.1, bf16[16,8192]{1,0:T(8,128)(2,1)} %q_in.1, bf16[16,512]{1,0:T(8,128)(2,1)} %nk_in.1, bf16[16,512]{1,0:T(8,128)(2,1)} %nv_in.1, bf16[16,128,512]{2,1,0:T(8,128)(2,1)} %keys.1, bf16[16,128,512]{2,1,0:T(8,128)(2,1)} %values.1), custom_call_target="tpu_custom_call" | custom-call | flops 134217728 | bytes 4194304 | tf_op jit(solution)/shard_map/attention/pallas_call | solution.py:105
  10.9 15.3 %all_to_all.20 = bf16[16,16,512]{2,1,0:T(8,128)(2,1)S(1)} all-to-all(bf16[16,16,512]{2,1,0:T(8,128)(2,1)} %attention.1), channel_id=1, replica_groups=mesh['chip'=16,'core'=2,'dp'=4] {'chip'}, dimensions={0} | all-to-all | bytes 524288 | tf_op jit(solution)/shard_map/all_to_all | solution.py:304
  27.0 3.7 %fusion = bf16[256,4096]{1,0:T(8,128)(2,1)} fusion(f32[256,4096]{1,0:T(8,128)S(1)} %fusion.7, bf16[256,4096]{1,0:T(8,128)(2,1)} %collective-permute-done, bf16[256,512]{1,0:T(8,128)(2,1)S(1)} %bitcast.24), kind=kOutput, calls=%fused_computation.1 | convolution fusion | flops 538968064 | bytes 8519680 | tf_op jit(solution)/shard_map/dot_general | solution.py:307
  30.7 3.8 %all-to-all-start.1 = ((bf16[16,16,4096]{2,1,0:T(8,128)(2,1)}), bf16[16,16,4096]{2,1,0:T(8,128)(2,1)S(1)}, u32[]{:S(2)}, u32[]{:S(2)}) async-start(bf16[16,16,4096]{2,1,0:T(8,128)(2,1)} %bitcast.22), calls=%async_computation.1 | async-start | bytes 4194304 | tf_op jit(solution)/shard_map/all_to_all | solution.py:312
  36.3 3.3 %collective-permute-start.2 = (s32[16,8]{0,1:T(8,128)S(1)}, s32[16,8]{0,1:T(8,128)S(1)}, u32[]{:S(2)}, u32[]{:S(2)}) collective-permute-start(s32[16,8]{0,1:T(8,128)S(1)} %copy-done.8), channel_id=1, source_target_pairs={{0,2},{1,3},{2,0},{3,1},{4,6},{5,7},{6,4},{7,5},{8,10},{9,11},{10,... | collective-permute-start | bytes 1544 | tf_op jit(solution)/shard_map/ppermute | solution.py:27
  39.6 3.3 %collective-permute-start.8 = (bf16[1,4096,384]{2,1,0:T(8,128)(2,1)}, bf16[1,4096,384]{2,1,0:T(8,128)(2,1)}, u32[]{:S(2)}, u32[]{:S(2)}) collective-permute-start(bf16[1,4096,384]{2,1,0:T(8,128)(2,1)} %refs_1_.1), channel_id=1, source_target_pairs={{1,0},{3,2},{4,5},{6,7},{9,8},{11,10},{12,13},{14,15},{17,16},{19,... | collective-permute-start | bytes 9437192 | tf_op jit(solution)/shard_map/ppermute | solution.py:280
  44.2 20.4 %all-to-all-done.1 = bf16[16,16,4096]{2,1,0:T(8,128)(2,1)S(1)} async-done(((bf16[16,16,4096]{2,1,0:T(8,128)(2,1)}), bf16[16,16,4096]{2,1,0:T(8,128)(2,1)S(1)}, u32[]{:S(2)}, u32[]{:S(2)}) %all-to-all-start.1) | async-done | bytes 2097184 | tf_op jit(solution)/shard_map/all_to_all | solution.py:312
  65.1 5.2 %collective-permute-start.7 = (bf16[1,4096,384]{2,1,0:T(8,128)(2,1)}, bf16[1,4096,384]{2,1,0:T(8,128)(2,1)}, u32[]{:S(2)}, u32[]{:S(2)}) collective-permute-start(bf16[1,4096,384]{2,1,0:T(8,128)(2,1)} %refs_0_.1), channel_id=1, source_target_pairs={{1,0},{3,2},{4,5},{6,7},{9,8},{11,10},{12,13},{14,15},{17,16},{19,... | collective-permute-start | bytes 9437192 | tf_op jit(solution)/shard_map/ppermute | solution.py:280
  70.3 2.9 %collective-permute-start.13 = (bf16[1,384,4096]{2,1,0:T(8,128)(2,1)}, bf16[1,384,4096]{2,1,0:T(8,128)(2,1)}, u32[]{:S(2)}, u32[]{:S(2)}) collective-permute-start(bf16[1,384,4096]{2,1,0:T(8,128)(2,1)} %own.1), channel_id=1, source_target_pairs={{1,0},{3,2},{4,5},{6,7},{9,8},{11,10},{12,13},{14,15},{17,16},{19,... | collective-permute-start | bytes 9437192 | tf_op jit(solution)/shard_map/ppermute | solution.py:280
  73.6 72.3 %collective-permute-done.4 = bf16[16,4096]{1,0:T(8,128)(2,1)S(1)} collective-permute-done((bf16[16,4096]{1,0:T(8,128)(2,1)S(1)}, bf16[16,4096]{1,0:T(8,128)(2,1)S(1)}, u32[]{:S(2)}, u32[]{:S(2)}) %collective-permute-start.4) | collective-permute-done | bytes 131104 | tf_op jit(solution)/shard_map/ppermute | solution.py:27
  145.9 4.1 %collective-permute-start.5 = (bf16[16,4096]{1,0:T(8,128)(2,1)S(1)}, bf16[16,4096]{1,0:T(8,128)(2,1)S(1)}, u32[]{:S(2)}, u32[]{:S(2)}) collective-permute-start(bf16[16,4096]{1,0:T(8,128)(2,1)S(1)} %multiply_convert_fusion), channel_id=1, source_target_pairs={{0,2},{1,3},{2,0},{3,1},{4,6},{5,7},{6,4},{7,5},{8,10},{9,11},{10,... | collective-permute-start | bytes 393224 | tf_op jit(solution)/shard_map/ppermute | solution.py:27
  150.2 2.2 collective-permute-done.5
  152.4 4.9 %collective-permute-start.6 = (bf16[16,4096]{1,0:T(8,128)(2,1)S(1)}, bf16[16,4096]{1,0:T(8,128)(2,1)S(1)}, u32[]{:S(2)}, u32[]{:S(2)}) collective-permute-start(bf16[16,4096]{1,0:T(8,128)(2,1)S(1)} %multiply_convert_fusion), channel_id=1, source_target_pairs={{0,3},{1,2},{2,1},{3,0},{4,7},{5,6},{6,5},{7,4},{8,11},{9,10},{10,... | collective-permute-start | bytes 393224 | tf_op jit(solution)/shard_map/ppermute | solution.py:27
  157.6 2.0 collective-permute-done.6
  162.3 6.3 %all-to-all-start.2 = ((bf16[16,16,4096]{2,1,0:T(8,128)(2,1)}), bf16[16,16,4096]{2,1,0:T(8,128)(2,1)S(1)}, u32[]{:S(2)}, u32[]{:S(2)}) async-start(bf16[16,16,4096]{2,1,0:T(8,128)(2,1)} %bitcast.21), calls=%async_computation.2 | async-start | bytes 4194304 | tf_op jit(solution)/shard_map/all_to_all | solution.py:345
  173.8 19.3 %all-to-all-done.2 = bf16[16,16,4096]{2,1,0:T(8,128)(2,1)S(1)} async-done(((bf16[16,16,4096]{2,1,0:T(8,128)(2,1)}), bf16[16,16,4096]{2,1,0:T(8,128)(2,1)S(1)}, u32[]{:S(2)}, u32[]{:S(2)}) %all-to-all-start.2) | async-done | bytes 2097184 | tf_op jit(solution)/shard_map/all_to_all | solution.py:345
  198.2 9.6 %expert_act.1.act = bf16[256,768]{1,0:T(8,128)(2,1)S(1)} custom-call(s32[1]{0:T(128)} %bitcast.5.flag, bf16[256,4096]{1,0:T(8,128)(2,1)S(1)} %bitcast.20, bf16[1,4096,384]{2,1,0:T(8,128)(2,1)S(1)} %copy-done.1, bf16[1,4096,384]{2,1,0:T(8,128)(2,1)S(1)} %copy-done.2, bf16[1,4096,384]{2,1,0:T(8,128)(2,1)} %collective-permute-done.7.refs_2_, ...), custom_call_target="tpu_custom_call" | custom-call | flops 3221225472 | bytes 14680064 | tf_op jit(solution)/shard_map/expert_act/pallas_call | solution.py:211
  207.8 5.8 %expert_down.1 = bf16[256,4096]{1,0:T(8,128)(2,1)} custom-call(s32[1]{0:T(128)} %bitcast.5.flag, bf16[256,768]{1,0:T(8,128)(2,1)S(1)} %expert_act.1.act, bf16[1,384,4096]{2,1,0:T(8,128)(2,1)S(1)} %copy-done.3, bf16[1,384,4096]{2,1,0:T(8,128)(2,1)} %collective-permute-done.13.crossed, bf16[1,384,4096]{2,1,0:T(8,128)(2,1)} %collective-permute-done.14.near, ...), custom_call_target="tpu_custom_call" | custom-call | flops 1610612736 | bytes 8388608 | tf_op jit(solution)/shard_map/expert_down/pallas_call | solution.py:234
  213.7 6.4 %all-to-all-start.3 = ((bf16[16,16,4096]{2,1,0:T(8,128)(2,1)}), bf16[16,16,4096]{2,1,0:T(8,128)(2,1)S(1)}, u32[]{:S(2)}, u32[]{:S(2)}) async-start(bf16[16,16,4096]{2,1,0:T(8,128)(2,1)} %bitcast.9), calls=%async_computation.3 | async-start | bytes 4194304 | tf_op jit(solution)/shard_map/all_to_all | solution.py:371
  221.9 23.0 %all-to-all-done.3 = bf16[16,16,4096]{2,1,0:T(8,128)(2,1)S(1)} async-done(((bf16[16,16,4096]{2,1,0:T(8,128)(2,1)}), bf16[16,16,4096]{2,1,0:T(8,128)(2,1)S(1)}, u32[]{:S(2)}, u32[]{:S(2)}) %all-to-all-start.3) | async-done | bytes 2097184 | tf_op jit(solution)/shard_map/all_to_all | solution.py:371
  245.5 13.5 %collective-permute-start.16 = (bf16[16,4096]{1,0:T(8,128)(2,1)S(1)}, bf16[16,4096]{1,0:T(8,128)(2,1)S(1)}, u32[]{:S(2)}, u32[]{:S(2)}) collective-permute-start(bf16[16,4096]{1,0:T(8,128)(2,1)S(1)} %get-tuple-element.11), channel_id=1, source_target_pairs={{0,1},{1,0},{2,3},{3,2},{4,5},{5,4},{6,7},{7,6},{8,9},{9,8},{10,11... | collective-permute-start | bytes 393224 | tf_op jit(solution)/shard_map/ppermute | solution.py:27
  258.9 4.7 %collective-permute-start.17 = (bf16[16,4096]{1,0:T(8,128)(2,1)S(1)}, bf16[16,4096]{1,0:T(8,128)(2,1)S(1)}, u32[]{:S(2)}, u32[]{:S(2)}) collective-permute-start(bf16[16,4096]{1,0:T(8,128)(2,1)S(1)} %get-tuple-element.13), channel_id=1, source_target_pairs={{0,2},{1,3},{2,0},{3,1},{4,6},{5,7},{6,4},{7,5},{8,10},{9,11},{10,... | collective-permute-start | bytes 393224 | tf_op jit(solution)/shard_map/ppermute | solution.py:27
  263.7 6.0 %collective-permute-done.17 = bf16[16,4096]{1,0:T(8,128)(2,1)S(1)} collective-permute-done((bf16[16,4096]{1,0:T(8,128)(2,1)S(1)}, bf16[16,4096]{1,0:T(8,128)(2,1)S(1)}, u32[]{:S(2)}, u32[]{:S(2)}) %collective-permute-start.17) | collective-permute-done | bytes 131104 | tf_op jit(solution)/shard_map/ppermute | solution.py:27
  269.7 2.5 collective-permute-done.18
  (68 shorter events, 22.4 us)
Async XLA Ops:
  0.0 220.1 %copy-start = (bf16[4096,64]{0,1:T(8,128)(2,1)S(1)}, bf16[4096,64]{0,1:T(8,128)(2,1)}, u32[]{:S(2)}) copy-start(bf16[4096,64]{0,1:T(8,128)(2,1)} %param.23) | copy-start | bytes 1572868
  0.0 27.0 %collective-permute-start = (bf16[256,4096]{1,0:T(8,128)(2,1)}, bf16[256,4096]{1,0:T(8,128)(2,1)}, u32[]{:S(2)}, u32[]{:S(2)}) collective-permute-start(bf16[256,4096]{1,0:T(8,128)(2,1)} %param.21), channel_id=1, source_target_pairs={{0,4},{4,0},{1,5},{5,1},{2,6},{6,2},{3,7},{7,3},{8,12},{12,8},{9,1... | collective-permute-start | bytes 6291464 | tf_op jit(solution)/shard_map/ppermute | solution.py:27
  30.7 33.9 %all-to-all-start.1 = ((bf16[16,16,4096]{2,1,0:T(8,128)(2,1)}), bf16[16,16,4096]{2,1,0:T(8,128)(2,1)S(1)}, u32[]{:S(2)}, u32[]{:S(2)}) async-start(bf16[16,16,4096]{2,1,0:T(8,128)(2,1)} %bitcast.22), calls=%async_computation.1 | async-start | bytes 4194304 | tf_op jit(solution)/shard_map/all_to_all | solution.py:312
  34.6 38.7 %copy-start.7 = (f32[4096]{0:T(1024)S(1)}, f32[4096]{0:T(1024)}, u32[]{:S(2)}) copy-start(f32[4096]{0:T(1024)} %param.22) | copy-start | bytes 49156
  34.6 30.5 %collective-permute-start.1 = (s32[16,8]{0,1:T(8,128)S(1)}, s32[16,8]{0,1:T(8,128)S(1)}, u32[]{:S(2)}, u32[]{:S(2)}) collective-permute-start(s32[16,8]{0,1:T(8,128)S(1)} %copy-done.8), channel_id=1, source_target_pairs={{0,1},{1,0},{2,3},{3,2},{4,5},{5,4},{6,7},{7,6},{8,9},{9,8},{10,11... | collective-permute-start | bytes 1544 | tf_op jit(solution)/shard_map/ppermute | solution.py:27
  36.3 34.0 %collective-permute-start.2 = (s32[16,8]{0,1:T(8,128)S(1)}, s32[16,8]{0,1:T(8,128)S(1)}, u32[]{:S(2)}, u32[]{:S(2)}) collective-permute-start(s32[16,8]{0,1:T(8,128)S(1)} %copy-done.8), channel_id=1, source_target_pairs={{0,2},{1,3},{2,0},{3,1},{4,6},{5,7},{6,4},{7,5},{8,10},{9,11},{10,... | collective-permute-start | bytes 1544 | tf_op jit(solution)/shard_map/ppermute | solution.py:27
  39.6 33.8 %collective-permute-start.3 = (s32[16,8]{0,1:T(8,128)S(1)}, s32[16,8]{0,1:T(8,128)S(1)}, u32[]{:S(2)}, u32[]{:S(2)}) collective-permute-start(s32[16,8]{0,1:T(8,128)S(1)} %copy-done.8), channel_id=1, source_target_pairs={{0,3},{1,2},{2,1},{3,0},{4,7},{5,6},{6,5},{7,4},{8,11},{9,10},{10,... | collective-permute-start | bytes 1544 | tf_op jit(solution)/shard_map/ppermute | solution.py:27
  39.6 131.6 %collective-permute-start.8 = (bf16[1,4096,384]{2,1,0:T(8,128)(2,1)}, bf16[1,4096,384]{2,1,0:T(8,128)(2,1)}, u32[]{:S(2)}, u32[]{:S(2)}) collective-permute-start(bf16[1,4096,384]{2,1,0:T(8,128)(2,1)} %refs_1_.1), channel_id=1, source_target_pairs={{1,0},{3,2},{4,5},{6,7},{9,8},{11,10},{12,13},{14,15},{17,16},{19,... | collective-permute-start | bytes 9437192 | tf_op jit(solution)/shard_map/ppermute | solution.py:280
  42.9 150.2 %collective-permute-start.10 = (bf16[1,4096,384]{2,1,0:T(8,128)(2,1)}, bf16[1,4096,384]{2,1,0:T(8,128)(2,1)}, u32[]{:S(2)}, u32[]{:S(2)}) collective-permute-start(bf16[1,4096,384]{2,1,0:T(8,128)(2,1)} %refs_1_.1), channel_id=1, source_target_pairs={{0,4},{2,6},{5,1},{7,3},{8,12},{10,14},{13,9},{15,11},{16,20},{18,... | collective-permute-start | bytes 9437192 | tf_op jit(solution)/shard_map/ppermute | solution.py:281
  65.1 104.8 %collective-permute-start.7 = (bf16[1,4096,384]{2,1,0:T(8,128)(2,1)}, bf16[1,4096,384]{2,1,0:T(8,128)(2,1)}, u32[]{:S(2)}, u32[]{:S(2)}) collective-permute-start(bf16[1,4096,384]{2,1,0:T(8,128)(2,1)} %refs_0_.1), channel_id=1, source_target_pairs={{1,0},{3,2},{4,5},{6,7},{9,8},{11,10},{12,13},{14,15},{17,16},{19,... | collective-permute-start | bytes 9437192 | tf_op jit(solution)/shard_map/ppermute | solution.py:280
  70.3 102.2 %collective-permute-start.13 = (bf16[1,384,4096]{2,1,0:T(8,128)(2,1)}, bf16[1,384,4096]{2,1,0:T(8,128)(2,1)}, u32[]{:S(2)}, u32[]{:S(2)}) collective-permute-start(bf16[1,384,4096]{2,1,0:T(8,128)(2,1)} %own.1), channel_id=1, source_target_pairs={{1,0},{3,2},{4,5},{6,7},{9,8},{11,10},{12,13},{14,15},{17,16},{19,... | collective-permute-start | bytes 9437192 | tf_op jit(solution)/shard_map/ppermute | solution.py:280
  73.4 72.5 %collective-permute-start.4 = (bf16[16,4096]{1,0:T(8,128)(2,1)S(1)}, bf16[16,4096]{1,0:T(8,128)(2,1)S(1)}, u32[]{:S(2)}, u32[]{:S(2)}) collective-permute-start(bf16[16,4096]{1,0:T(8,128)(2,1)S(1)} %multiply_convert_fusion), channel_id=1, source_target_pairs={{0,1},{1,0},{2,3},{3,2},{4,5},{5,4},{6,7},{7,6},{8,9},{9,8},{10,11... | collective-permute-start | bytes 393224 | tf_op jit(solution)/shard_map/ppermute | solution.py:27
  145.9 6.5 %collective-permute-start.5 = (bf16[16,4096]{1,0:T(8,128)(2,1)S(1)}, bf16[16,4096]{1,0:T(8,128)(2,1)S(1)}, u32[]{:S(2)}, u32[]{:S(2)}) collective-permute-start(bf16[16,4096]{1,0:T(8,128)(2,1)S(1)} %multiply_convert_fusion), channel_id=1, source_target_pairs={{0,2},{1,3},{2,0},{3,1},{4,6},{5,7},{6,4},{7,5},{8,10},{9,11},{10,... | collective-permute-start | bytes 393224 | tf_op jit(solution)/shard_map/ppermute | solution.py:27
  152.4 7.2 %collective-permute-start.6 = (bf16[16,4096]{1,0:T(8,128)(2,1)S(1)}, bf16[16,4096]{1,0:T(8,128)(2,1)S(1)}, u32[]{:S(2)}, u32[]{:S(2)}) collective-permute-start(bf16[16,4096]{1,0:T(8,128)(2,1)S(1)} %multiply_convert_fusion), channel_id=1, source_target_pairs={{0,3},{1,2},{2,1},{3,0},{4,7},{5,6},{6,5},{7,4},{8,11},{9,10},{10,... | collective-permute-start | bytes 393224 | tf_op jit(solution)/shard_map/ppermute | solution.py:27
  162.3 30.8 %all-to-all-start.2 = ((bf16[16,16,4096]{2,1,0:T(8,128)(2,1)}), bf16[16,16,4096]{2,1,0:T(8,128)(2,1)S(1)}, u32[]{:S(2)}, u32[]{:S(2)}) async-start(bf16[16,16,4096]{2,1,0:T(8,128)(2,1)} %bitcast.21), calls=%async_computation.2 | async-start | bytes 4194304 | tf_op jit(solution)/shard_map/all_to_all | solution.py:345
  168.6 25.8 %collective-permute-start.9 = (bf16[1,4096,384]{2,1,0:T(8,128)(2,1)}, bf16[1,4096,384]{2,1,0:T(8,128)(2,1)}, u32[]{:S(2)}, u32[]{:S(2)}) collective-permute-start(bf16[1,4096,384]{2,1,0:T(8,128)(2,1)} %refs_0_.1), channel_id=1, source_target_pairs={{0,4},{2,6},{5,1},{7,3},{8,12},{10,14},{13,9},{15,11},{16,20},{18,... | collective-permute-start | bytes 9437192 | tf_op jit(solution)/shard_map/ppermute | solution.py:281
  169.9 24.5 %collective-permute-start.11 = (bf16[1,4096,384]{2,1,0:T(8,128)(2,1)}, bf16[1,4096,384]{2,1,0:T(8,128)(2,1)}, u32[]{:S(2)}, u32[]{:S(2)}) collective-permute-start(bf16[1,4096,384]{2,1,0:T(8,128)(2,1)} %collective-permute-done.7.refs_2_), channel_id=1, source_target_pairs={{0,4},{2,6},{5,1},{7,3},{8,12},{10,14},{13,9},{15,11},{16,20},{18,... | collective-permute-start | bytes 9437192 | tf_op jit(solution)/shard_map/ppermute | solution.py:285
  171.2 23.2 %collective-permute-start.12 = (bf16[1,4096,384]{2,1,0:T(8,128)(2,1)}, bf16[1,4096,384]{2,1,0:T(8,128)(2,1)}, u32[]{:S(2)}, u32[]{:S(2)}) collective-permute-start(bf16[1,4096,384]{2,1,0:T(8,128)(2,1)} %collective-permute-done.8.refs_3_), channel_id=1, source_target_pairs={{0,4},{2,6},{5,1},{7,3},{8,12},{10,14},{13,9},{15,11},{16,20},{18,... | collective-permute-start | bytes 9437192 | tf_op jit(solution)/shard_map/ppermute | solution.py:285
  172.5 35.3 %collective-permute-start.14 = (bf16[1,384,4096]{2,1,0:T(8,128)(2,1)}, bf16[1,384,4096]{2,1,0:T(8,128)(2,1)}, u32[]{:S(2)}, u32[]{:S(2)}) collective-permute-start(bf16[1,384,4096]{2,1,0:T(8,128)(2,1)} %own.1), channel_id=1, source_target_pairs={{0,4},{2,6},{5,1},{7,3},{8,12},{10,14},{13,9},{15,11},{16,20},{18,... | collective-permute-start | bytes 9437192 | tf_op jit(solution)/shard_map/ppermute | solution.py:281
  193.1 14.7 %collective-permute-start.15 = (bf16[1,384,4096]{2,1,0:T(8,128)(2,1)}, bf16[1,384,4096]{2,1,0:T(8,128)(2,1)}, u32[]{:S(2)}, u32[]{:S(2)}) collective-permute-start(bf16[1,384,4096]{2,1,0:T(8,128)(2,1)} %collective-permute-done.13.crossed), channel_id=1, source_target_pairs={{0,4},{2,6},{5,1},{7,3},{8,12},{10,14},{13,9},{15,11},{16,20},{18,... | collective-permute-start | bytes 9437192 | tf_op jit(solution)/shard_map/ppermute | solution.py:285
  213.7 31.3 %all-to-all-start.3 = ((bf16[16,16,4096]{2,1,0:T(8,128)(2,1)}), bf16[16,16,4096]{2,1,0:T(8,128)(2,1)S(1)}, u32[]{:S(2)}, u32[]{:S(2)}) async-start(bf16[16,16,4096]{2,1,0:T(8,128)(2,1)} %bitcast.9), calls=%async_computation.3 | async-start | bytes 4194304 | tf_op jit(solution)/shard_map/all_to_all | solution.py:371
  245.5 18.2 %collective-permute-start.16 = (bf16[16,4096]{1,0:T(8,128)(2,1)S(1)}, bf16[16,4096]{1,0:T(8,128)(2,1)S(1)}, u32[]{:S(2)}, u32[]{:S(2)}) collective-permute-start(bf16[16,4096]{1,0:T(8,128)(2,1)S(1)} %get-tuple-element.11), channel_id=1, source_target_pairs={{0,1},{1,0},{2,3},{3,2},{4,5},{5,4},{6,7},{7,6},{8,9},{9,8},{10,11... | collective-permute-start | bytes 393224 | tf_op jit(solution)/shard_map/ppermute | solution.py:27
  258.9 10.8 %collective-permute-start.17 = (bf16[16,4096]{1,0:T(8,128)(2,1)S(1)}, bf16[16,4096]{1,0:T(8,128)(2,1)S(1)}, u32[]{:S(2)}, u32[]{:S(2)}) collective-permute-start(bf16[16,4096]{1,0:T(8,128)(2,1)S(1)} %get-tuple-element.13), channel_id=1, source_target_pairs={{0,2},{1,3},{2,0},{3,1},{4,6},{5,7},{6,4},{7,5},{8,10},{9,11},{10,... | collective-permute-start | bytes 393224 | tf_op jit(solution)/shard_map/ppermute | solution.py:27
  263.7 8.6 %collective-permute-start.18 = (bf16[16,4096]{1,0:T(8,128)(2,1)S(1)}, bf16[16,4096]{1,0:T(8,128)(2,1)S(1)}, u32[]{:S(2)}, u32[]{:S(2)}) collective-permute-start(bf16[16,4096]{1,0:T(8,128)(2,1)S(1)} %get-tuple-element.12), channel_id=1, source_target_pairs={{0,3},{1,2},{2,1},{3,0},{4,7},{5,6},{6,5},{7,4},{8,11},{9,10},{10,... | collective-permute-start | bytes 393224 | tf_op jit(solution)/shard_map/ppermute | solution.py:27
  (7 other events, 73.1 us)

commit v3 on v2

--- a/solution.py
+++ b/solution.py
@@ -14,7 +14,6 @@
 HD = 128
 CAP = 4
 ATTN_STEPS = 2
-IN_STEPS = 4
 OUT_STEPS = 4
 
 
@@ -142,40 +141,32 @@
 
 def act_kernel(flag, rows_in, *refs):
     own, crossed, near, far = refs[0:2], refs[2:4], refs[4:6], refs[6:8]
-    out, x_buf, in_buf, x_sem, in_sem = refs[8:]
+    out, x_buf, buf, x_sem, sem = refs[8:]
     hf = own[0].shape[2]
-    span = D // IN_STEPS
-
-    def copy(side, source, step, part):
+
+    def copy(side, source, part):
         return pltpu.make_async_copy(
-            source[part].at[0, pl.ds(step * span, span)],
-            in_buf.at[side, pl.ds(step * span, span), pl.ds(part * hf, hf)],
-            in_sem.at[side, step, part],
+            source[part].at[0], buf.at[2 * side + part], sem.at[2 * side + part]
         )
 
     def start(side, source):
-        for step in range(IN_STEPS):
-            for part in range(2):
-                copy(side, source, step, part).start()
+        for part in range(2):
+            copy(side, source, part).start()
 
     x_copy = pltpu.make_async_copy(rows_in, x_buf, x_sem)
     x_copy.start()
     start_slabs(flag, own, crossed, near, far, start)
     x_copy.wait()
     for side in range(2):
-        total = None
-        for step in range(IN_STEPS):
-            for part in range(2):
-                copy(side, own, step, part).wait()
-            piece = jnp.dot(
-                x_buf[:, step * span : (step + 1) * span],
-                in_buf[side, step * span : (step + 1) * span],
-                preferred_element_type=jnp.float32,
+        vals = []
+        for part in range(2):
+            copy(side, own, part).wait()
+            vals.append(
+                jnp.dot(x_buf[...], buf[2 * side + part], preferred_element_type=jnp.float32)
             )
-            total = piece if total is None else total + piece
-        gate_val = total[:, :hf]
+        gate_val, up_val = vals
         out[:, side * hf : (side + 1) * hf] = (
-            gate_val / (1.0 + jnp.exp(-gate_val)) * total[:, hf:]
+            gate_val / (1.0 + jnp.exp(-gate_val)) * up_val
         ).astype(jnp.bfloat16)
 
 
@@ -216,11 +207,11 @@
         out_specs=pl.BlockSpec(memory_space=pltpu.VMEM),
         scratch_shapes=[
             pltpu.VMEM((count, D), jnp.bfloat16),
-            pltpu.VMEM((2, D, 2 * hf), jnp.bfloat16),
+            pltpu.VMEM((4, D, hf), jnp.bfloat16),
             pltpu.SemaphoreType.DMA,
-            pltpu.SemaphoreType.DMA((2, IN_STEPS, 2)),
+            pltpu.SemaphoreType.DMA((4,)),
         ],
-        compiler_params=pltpu.CompilerParams(vmem_limit_bytes=28 * 1024 * 1024),
+        compiler_params=pltpu.CompilerParams(vmem_limit_bytes=123 * 512 * 1024),
         cost_estimate=pl.CostEstimate(
             flops=8 * count * D * hf, bytes_accessed=8 * D * hf + 2 * count * D, transcendentals=0
         ),
@@ -276,19 +267,18 @@
     across = [(c * depths + d, c * depths + (d ^ 1)) for c, d in places if c != d % 2]
     beside = [(c * depths + d, (1 - c) * depths + d) for c, d in places if c == d % 2]
 
-    def spread_out(slab):
-        crossed = lax.ppermute(slab, ("core", "dp"), across)
-        return crossed, lax.ppermute(slab, ("core", "dp"), beside)
-
-    def shared(slab, after):
-        held, _ = lax.optimization_barrier((slab, after))
-        return lax.ppermute(held, ("core", "dp"), beside)
-
-    gate_crossed, gate_near = spread_out(gate_slab)
-    up_crossed, up_near = spread_out(up_slab)
-    down_crossed, down_near = spread_out(down_slab)
+    def moved(slab, pairs, after=None):
+        if after is not None:
+            slab, _ = lax.optimization_barrier((slab, after))
+        return lax.ppermute(slab, ("core", "dp"), pairs)
+
+    gate_crossed = moved(gate_slab, across)
+    gate_near = moved(gate_slab, beside)
+    up_near = moved(up_slab, beside)
+    down_near = moved(down_slab, beside)
     flag = (core == depth % 2).astype(jnp.int32).reshape(1)
-    ids = jnp.concatenate([expert_ids] + [flipped(expert_ids, "dp", m) for m in (1, 2, 3)], axis=0)
+    other_ids = [flipped(expert_ids, "dp", m) for m in (1, 2, 3)]
+    ids = jnp.concatenate([expert_ids] + other_ids, axis=0)
 
     piece = out_proj.shape[0]
     sent = attention(
@@ -307,22 +297,7 @@
     partial = partial + jnp.dot(
         regrouped[:, piece:], other_proj, preferred_element_type=jnp.float32
     )
-    partial = partial.astype(jnp.bfloat16)
-    gate_far = shared(gate_crossed, partial)
-    partial = lax.all_to_all(
-        partial.reshape(chips, rows, D),
-        "chip",
-        split_axis=0,
-        concat_axis=0,
-        tiled=True,
-    )
-    hidden = resid.astype(jnp.float32) + jnp.sum(partial.astype(jnp.float32), axis=0)
-    meansq = jnp.mean(hidden * hidden, axis=1, keepdims=True)
-    normed = (hidden * lax.rsqrt(jnp.maximum(meansq, 0.25)) * norm_gain).astype(jnp.bfloat16)
-
-    tokens = jnp.concatenate([normed] + [flipped(normed, "dp", m) for m in (1, 2, 3)], axis=0)
-
-    count = tokens.shape[0]
+    count = ids.shape[0]
     labels = 4 * jnp.arange(chips, dtype=jnp.int32) + 2 * (depth % 2) + depth // 2
     hits = ids.T[:, None, :] == labels[None, :, None]
     member = jnp.any(hits, axis=0)
@@ -336,12 +311,32 @@
     place = jnp.where(member, rank + CAP * (at // rows)[None, :], -1)
     slots = CAP * depths
     dispatch = place[:, None, :] == jnp.arange(slots, dtype=jnp.int32)[None, :, None]
+
+    partial = partial.astype(jnp.bfloat16)
+    gate_far = moved(gate_crossed, beside, partial)
+    up_crossed = moved(up_slab, across, partial)
+    partial = lax.all_to_all(
+        partial.reshape(chips, rows, D),
+        "chip",
+        split_axis=0,
+        concat_axis=0,
+        tiled=True,
+    )
+    partial, dispatch = lax.optimization_barrier((partial, dispatch))
+    hidden = resid.astype(jnp.float32) + jnp.sum(partial.astype(jnp.float32), axis=0)
+    meansq = jnp.mean(hidden * hidden, axis=1, keepdims=True)
+    normed = (hidden * lax.rsqrt(jnp.maximum(meansq, 0.25)) * norm_gain).astype(jnp.bfloat16)
+
+    others = [flipped(normed, "dp", m) for m in (1, 2, 3)]
+    tokens = jnp.concatenate([normed] + others, axis=0)
+    down_crossed = moved(down_slab, across, others)
+
     outgoing = jnp.dot(
         dispatch.reshape(chips * slots, count).astype(jnp.bfloat16),
         tokens,
         preferred_element_type=jnp.float32,
     ).astype(jnp.bfloat16)
-    up_far = shared(up_crossed, outgoing)
+    up_far = moved(up_crossed, beside, outgoing)
     incoming = lax.all_to_all(
         outgoing.reshape(chips, slots, D), "chip", split_axis=0, concat_axis=0, tiled=True
     )
@@ -358,7 +353,7 @@
     )
     combine = jnp.where(dispatch, spread[:, None, :], 0.0).astype(jnp.bfloat16)
 
-    down_far = shared(down_crossed, incoming)
+    down_far = moved(down_crossed, beside, incoming)
     act = expert_act(
         flag,
         incoming.reshape(chips * slots, D),

time: 274 us -> 232 us (0.85)
  waiting for transfers between devices: 148 us -> 116 us
  starting transfers between devices: 69.4 us -> 62.1 us
  local copies, waits for them, and re-layouts: 4.71 us -> 1.2 us
    ppermute x10, waiting for transfers between devices: 85.1 us -> 53.9 us  [flipped(): return lax.ppermute(value, axis, pairs)]
    ppermute x9, waiting for transfers between devices: 0.02 us -> 21.4 us  [moved(): return lax.ppermute(slab, ('core', 'dp'), pairs)]
    all_to_all x1, waiting for transfers between devices: 19.3 us -> 1.03 us  [local(): lax.all_to_all(outgoing.reshape(chips, slots, D), 'chip', split_axis=0, c...]
    ppermute x10, starting transfers between devices: 33.7 us -> 26 us  [flipped(): return lax.ppermute(value, axis, pairs)]
    unnamed x18 -> x14, local copies, waits for them, and re-layouts: 4.46 us -> 1.02 us
  transfers between devices with their start and end apart: 22 -> 22, of which waited for: 8 -> 9; matrix products, arithmetic and copies ran while one was open for 2% -> 2% of each run, Pallas kernels for 7% -> 9%
where the time goes in v3:
time: 232 us; the launch traced here: 231 us
  waiting for transfers between devices  116 us (50%)
  starting transfers between devices  62.1 us (27%)
  Pallas kernels  25.6 us (11%)
  blocking collectives  15.3 us (7%)
  matrix products  8.36 us (4%)
    ppermute x10, waiting for transfers between devices, flipped(): return lax.ppermute(value, axis, pairs)  53.9 us
    ppermute x10, starting transfers between devices, flipped(): return lax.ppermute(value, axis, pairs)  26 us
    all_to_all x1, waiting for transfers between devices, local(): lax.all_to_all(produced.reshape(chips, slots, D), 'chip', split_axis=0, c...  22.2 us
    ppermute x9, waiting for transfers between devices, moved(): return lax.ppermute(slab, ('core', 'dp'), pairs)  21.4 us
    ppermute x9, starting transfers between devices, moved(): return lax.ppermute(slab, ('core', 'dp'), pairs)  18.7 us
    all_to_all x1, waiting for transfers between devices, local(): lax.all_to_all(partial.reshape(chips, rows, D), 'chip', split_axis=0, con...  17.7 us
    all_to_all x1, blocking collectives, local(): lax.all_to_all(sent, 'chip', split_axis=0, concat_axis=0, tiled=True)  15.3 us
    pallas_call x1, Pallas kernels, expert_act(): pl.pallas_call(act_kernel, out_shape=jax.ShapeDtypeStruct((count, 2 * hf)...  10.2 us
  transfers between devices with their start and end apart: 22, of which 9 were waited for; matrix products, arithmetic and copies ran while one was open for 2% of the time, Pallas kernels for 9%

profile of v3, /device:TPU:1, one launch (start us, length us, event | category | flops | bytes accessed | tf_op | source)
XLA Modules:
  0.0 231.1 jit_solution(13682717140541168147)
XLA Ops:
  1.4 9.5 %attention.1 = bf16[16,16,512]{2,1,0:T(8,128)(2,1)} custom-call(s32[1]{0:T(128)} %bitcast.swap, s32[16]{0:T(128)} %lengths.1, bf16[16,8192]{1,0:T(8,128)(2,1)} %q_in.1, bf16[16,512]{1,0:T(8,128)(2,1)} %nk_in.1, bf16[16,512]{1,0:T(8,128)(2,1)} %nv_in.1, bf16[16,128,512]{2,1,0:T(8,128)(2,1)} %keys.1, bf16[16,128,512]{2,1,0:T(8,128)(2,1)} %values.1), custom_call_target="tpu_custom_call" | custom-call | flops 134217728 | bytes 4194304 | tf_op jit(solution)/shard_map/attention/pallas_call | solution.py:104
  10.9 15.3 %all_to_all.20 = bf16[16,16,512]{2,1,0:T(8,128)(2,1)S(1)} all-to-all(bf16[16,16,512]{2,1,0:T(8,128)(2,1)} %attention.1), channel_id=1, replica_groups=mesh['chip'=16,'core'=2,'dp'=4] {'chip'}, dimensions={0} | all-to-all | bytes 524288 | tf_op jit(solution)/shard_map/all_to_all | solution.py:294
  27.0 3.7 %fusion = bf16[256,4096]{1,0:T(8,128)(2,1)} fusion(f32[256,4096]{1,0:T(8,128)S(1)} %fusion.7, bf16[256,4096]{1,0:T(8,128)(2,1)} %collective-permute-done, bf16[256,512]{1,0:T(8,128)(2,1)S(1)} %bitcast.21), kind=kOutput, calls=%fused_computation.1 | convolution fusion | flops 538968064 | bytes 8519680 | tf_op jit(solution)/shard_map/dot_general | solution.py:297
  30.7 3.8 %all-to-all-start.1 = ((bf16[16,16,4096]{2,1,0:T(8,128)(2,1)}), bf16[16,16,4096]{2,1,0:T(8,128)(2,1)S(1)}, u32[]{:S(2)}, u32[]{:S(2)}) async-start(bf16[16,16,4096]{2,1,0:T(8,128)(2,1)} %bitcast.19), calls=%async_computation.1 | async-start | bytes 4194304 | tf_op jit(solution)/shard_map/all_to_all | solution.py:318
  34.6 3.8 %collective-permute-start.3 = (s32[16,8]{0,1:T(8,128)S(1)}, s32[16,8]{0,1:T(8,128)S(1)}, u32[]{:S(2)}, u32[]{:S(2)}) collective-permute-start(s32[16,8]{0,1:T(8,128)S(1)} %copy-done.6), channel_id=1, source_target_pairs={{0,3},{1,2},{2,1},{3,0},{4,7},{5,6},{6,5},{7,4},{8,11},{9,10},{10,... | collective-permute-start | bytes 1544 | tf_op jit(solution)/shard_map/ppermute | solution.py:26
  39.1 4.4 %collective-permute-start.7 = (bf16[1,4096,384]{2,1,0:T(8,128)(2,1)}, bf16[1,4096,384]{2,1,0:T(8,128)(2,1)}, u32[]{:S(2)}, u32[]{:S(2)}) collective-permute-start(bf16[1,4096,384]{2,1,0:T(8,128)(2,1)} %refs_0_.1), channel_id=1, source_target_pairs={{1,0},{3,2},{4,5},{6,7},{9,8},{11,10},{12,13},{14,15},{17,16},{19,... | collective-permute-start | bytes 9437192 | tf_op jit(solution)/shard_map/ppermute | solution.py:273
  43.9 3.0 %collective-permute-start.8 = (bf16[1,4096,384]{2,1,0:T(8,128)(2,1)}, bf16[1,4096,384]{2,1,0:T(8,128)(2,1)}, u32[]{:S(2)}, u32[]{:S(2)}) collective-permute-start(bf16[1,4096,384]{2,1,0:T(8,128)(2,1)} %refs_1_.1), channel_id=1, source_target_pairs={{1,0},{3,2},{4,5},{6,7},{9,8},{11,10},{12,13},{14,15},{17,16},{19,... | collective-permute-start | bytes 9437192 | tf_op jit(solution)/shard_map/ppermute | solution.py:273
  46.9 17.7 %all-to-all-done.1 = bf16[16,16,4096]{2,1,0:T(8,128)(2,1)S(1)} async-done(((bf16[16,16,4096]{2,1,0:T(8,128)(2,1)}), bf16[16,16,4096]{2,1,0:T(8,128)(2,1)S(1)}, u32[]{:S(2)}, u32[]{:S(2)}) %all-to-all-start.1) | async-done | bytes 2097184 | tf_op jit(solution)/shard_map/all_to_all | solution.py:318
  65.2 3.8 %collective-permute-start.6 = (bf16[16,4096]{1,0:T(8,128)(2,1)S(1)}, bf16[16,4096]{1,0:T(8,128)(2,1)S(1)}, u32[]{:S(2)}, u32[]{:S(2)}) collective-permute-start(bf16[16,4096]{1,0:T(8,128)(2,1)S(1)} %multiply_convert_fusion), channel_id=1, source_target_pairs={{0,3},{1,2},{2,1},{3,0},{4,7},{5,6},{6,5},{7,4},{8,11},{9,10},{10,... | collective-permute-start | bytes 393224 | tf_op jit(solution)/shard_map/ppermute | solution.py:26
  69.7 2.1 collective-permute-done.6
  71.8 45.7 %collective-permute-done.5 = bf16[16,4096]{1,0:T(8,128)(2,1)S(1)} collective-permute-done((bf16[16,4096]{1,0:T(8,128)(2,1)S(1)}, bf16[16,4096]{1,0:T(8,128)(2,1)S(1)}, u32[]{:S(2)}, u32[]{:S(2)}) %collective-permute-start.5) | collective-permute-done | bytes 131104 | tf_op jit(solution)/shard_map/ppermute | solution.py:26
  117.6 3.4 %collective-permute-start.13 = (bf16[1,384,4096]{2,1,0:T(8,128)(2,1)}, bf16[1,384,4096]{2,1,0:T(8,128)(2,1)}, u32[]{:S(2)}, u32[]{:S(2)}) collective-permute-start(bf16[1,384,4096]{2,1,0:T(8,128)(2,1)} %own.1), channel_id=1, source_target_pairs={{1,0},{3,2},{4,5},{6,7},{9,8},{11,10},{12,13},{14,15},{17,16},{19,... | collective-permute-start | bytes 9437192 | tf_op jit(solution)/shard_map/ppermute | solution.py:273
  122.3 2.0 convolution_convert_fusion
  124.3 6.6 %all-to-all-start.2 = ((bf16[16,16,4096]{2,1,0:T(8,128)(2,1)}), bf16[16,16,4096]{2,1,0:T(8,128)(2,1)}, u32[]{:S(2)}, u32[]{:S(2)}) async-start(bf16[16,16,4096]{2,1,0:T(8,128)(2,1)} %bitcast.7), calls=%async_computation.2 | async-start | bytes 4194304 | tf_op jit(solution)/shard_map/all_to_all | solution.py:340
  134.9 19.0 %collective-permute-done.13.crossed = bf16[1,384,4096]{2,1,0:T(8,128)(2,1)} collective-permute-done((bf16[1,384,4096]{2,1,0:T(8,128)(2,1)}, bf16[1,384,4096]{2,1,0:T(8,128)(2,1)}, u32[]{:S(2)}, u32[]{:S(2)}) %collective-permute-start.13) | collective-permute-done | bytes 3145760 | tf_op jit(solution)/shard_map/ppermute | solution.py:273
  156.2 1.5 collective-permute-start.15
  157.7 10.2 %expert_act.1.act = bf16[256,768]{1,0:T(8,128)(2,1)} custom-call(s32[1]{0:T(128)} %bitcast.5.flag, bf16[256,4096]{1,0:T(8,128)(2,1)} %bitcast.8.rows_in, bf16[1,4096,384]{2,1,0:T(8,128)(2,1)} %refs_0_.1, bf16[1,4096,384]{2,1,0:T(8,128)(2,1)} %refs_1_.1, bf16[1,4096,384]{2,1,0:T(8,128)(2,1)} %collective-permute-done.7.refs_2_, ...), custom_call_target="tpu_custom_call" | custom-call | flops 3221225472 | bytes 14680064 | tf_op jit(solution)/shard_map/expert_act/pallas_call | solution.py:202
  167.9 2.3 %collective-permute-done.15.far = bf16[1,384,4096]{2,1,0:T(8,128)(2,1)} collective-permute-done((bf16[1,384,4096]{2,1,0:T(8,128)(2,1)}, bf16[1,384,4096]{2,1,0:T(8,128)(2,1)}, u32[]{:S(2)}, u32[]{:S(2)}) %collective-permute-start.15) | collective-permute-done | bytes 3145760 | tf_op jit(solution)/shard_map/ppermute | solution.py:273
  171.3 5.8 %expert_down.1 = bf16[256,4096]{1,0:T(8,128)(2,1)} custom-call(s32[1]{0:T(128)} %bitcast.5.flag, bf16[256,768]{1,0:T(8,128)(2,1)S(1)} %copy-done.1, bf16[1,384,4096]{2,1,0:T(8,128)(2,1)} %own.1, bf16[1,384,4096]{2,1,0:T(8,128)(2,1)} %collective-permute-done.13.crossed, bf16[1,384,4096]{2,1,0:T(8,128)(2,1)} %collective-permute-done.14.near, ...), custom_call_target="tpu_custom_call" | custom-call | flops 1610612736 | bytes 8388608 | tf_op jit(solution)/shard_map/expert_down/pallas_call | solution.py:225
  177.1 6.9 %all-to-all-start.3 = ((bf16[16,16,4096]{2,1,0:T(8,128)(2,1)}), bf16[16,16,4096]{2,1,0:T(8,128)(2,1)S(1)}, u32[]{:S(2)}, u32[]{:S(2)}) async-start(bf16[16,16,4096]{2,1,0:T(8,128)(2,1)} %bitcast.9), calls=%async_computation.3 | async-start | bytes 4194304 | tf_op jit(solution)/shard_map/all_to_all | solution.py:366
  185.8 22.2 %all-to-all-done.3 = bf16[16,16,4096]{2,1,0:T(8,128)(2,1)S(1)} async-done(((bf16[16,16,4096]{2,1,0:T(8,128)(2,1)}), bf16[16,16,4096]{2,1,0:T(8,128)(2,1)S(1)}, u32[]{:S(2)}, u32[]{:S(2)}) %all-to-all-start.3) | async-done | bytes 2097184 | tf_op jit(solution)/shard_map/all_to_all | solution.py:366
  208.6 15.0 %collective-permute-start.18 = (bf16[16,4096]{1,0:T(8,128)(2,1)S(1)}, bf16[16,4096]{1,0:T(8,128)(2,1)S(1)}, u32[]{:S(2)}, u32[]{:S(2)}) collective-permute-start(bf16[16,4096]{1,0:T(8,128)(2,1)S(1)} %get-tuple-element.20), channel_id=1, source_target_pairs={{0,3},{1,2},{2,1},{3,0},{4,7},{5,6},{6,5},{7,4},{8,11},{9,10},{10,... | collective-permute-start | bytes 393224 | tf_op jit(solution)/shard_map/ppermute | solution.py:26
  224.2 3.8 %collective-permute-done.18 = bf16[16,4096]{1,0:T(8,128)(2,1)S(1)} collective-permute-done((bf16[16,4096]{1,0:T(8,128)(2,1)S(1)}, bf16[16,4096]{1,0:T(8,128)(2,1)S(1)}, u32[]{:S(2)}, u32[]{:S(2)}) %collective-permute-start.18) | collective-permute-done | bytes 131104 | tf_op jit(solution)/shard_map/ppermute | solution.py:26
  228.0 2.2 collective-permute-done.17
  (62 shorter events, 16.7 us)
Async XLA Ops:
  0.0 184.1 %copy-start = (bf16[4096,64]{0,1:T(8,128)(2,1)S(1)}, bf16[4096,64]{0,1:T(8,128)(2,1)}, u32[]{:S(2)}) copy-start(bf16[4096,64]{0,1:T(8,128)(2,1)} %param.23) | copy-start | bytes 1572868
  0.0 27.0 %collective-permute-start = (bf16[256,4096]{1,0:T(8,128)(2,1)}, bf16[256,4096]{1,0:T(8,128)(2,1)}, u32[]{:S(2)}, u32[]{:S(2)}) collective-permute-start(bf16[256,4096]{1,0:T(8,128)(2,1)} %param.21), channel_id=1, source_target_pairs={{0,4},{4,0},{1,5},{5,1},{2,6},{6,2},{3,7},{7,3},{8,12},{12,8},{9,1... | collective-permute-start | bytes 6291464 | tf_op jit(solution)/shard_map/ppermute | solution.py:26
  30.7 33.9 %all-to-all-start.1 = ((bf16[16,16,4096]{2,1,0:T(8,128)(2,1)}), bf16[16,16,4096]{2,1,0:T(8,128)(2,1)S(1)}, u32[]{:S(2)}, u32[]{:S(2)}) async-start(bf16[16,16,4096]{2,1,0:T(8,128)(2,1)} %bitcast.19), calls=%async_computation.1 | async-start | bytes 4194304 | tf_op jit(solution)/shard_map/all_to_all | solution.py:318
  34.6 30.5 %copy-start.5 = (f32[4096]{0:T(1024)S(1)}, f32[4096]{0:T(1024)}, u32[]{:S(2)}) copy-start(f32[4096]{0:T(1024)} %param.22) | copy-start | bytes 49156
  34.6 8.9 %collective-permute-start.3 = (s32[16,8]{0,1:T(8,128)S(1)}, s32[16,8]{0,1:T(8,128)S(1)}, u32[]{:S(2)}, u32[]{:S(2)}) collective-permute-start(s32[16,8]{0,1:T(8,128)S(1)} %copy-done.6), channel_id=1, source_target_pairs={{0,3},{1,2},{2,1},{3,0},{4,7},{5,6},{6,5},{7,4},{8,11},{9,10},{10,... | collective-permute-start | bytes 1544 | tf_op jit(solution)/shard_map/ppermute | solution.py:26
  38.5 5.1 %collective-permute-start.2 = (s32[16,8]{0,1:T(8,128)S(1)}, s32[16,8]{0,1:T(8,128)S(1)}, u32[]{:S(2)}, u32[]{:S(2)}) collective-permute-start(s32[16,8]{0,1:T(8,128)S(1)} %copy-done.6), channel_id=1, source_target_pairs={{0,2},{1,3},{2,0},{3,1},{4,6},{5,7},{6,4},{7,5},{8,10},{9,11},{10,... | collective-permute-start | bytes 1544 | tf_op jit(solution)/shard_map/ppermute | solution.py:26
  38.5 5.1 %collective-permute-start.1 = (s32[16,8]{0,1:T(8,128)S(1)}, s32[16,8]{0,1:T(8,128)S(1)}, u32[]{:S(2)}, u32[]{:S(2)}) collective-permute-start(s32[16,8]{0,1:T(8,128)S(1)} %copy-done.6), channel_id=1, source_target_pairs={{0,1},{1,0},{2,3},{3,2},{4,5},{5,4},{6,7},{7,6},{8,9},{9,8},{10,11... | collective-permute-start | bytes 1544 | tf_op jit(solution)/shard_map/ppermute | solution.py:26
  39.1 93.1 %collective-permute-start.7 = (bf16[1,4096,384]{2,1,0:T(8,128)(2,1)}, bf16[1,4096,384]{2,1,0:T(8,128)(2,1)}, u32[]{:S(2)}, u32[]{:S(2)}) collective-permute-start(bf16[1,4096,384]{2,1,0:T(8,128)(2,1)} %refs_0_.1), channel_id=1, source_target_pairs={{1,0},{3,2},{4,5},{6,7},{9,8},{11,10},{12,13},{14,15},{17,16},{19,... | collective-permute-start | bytes 9437192 | tf_op jit(solution)/shard_map/ppermute | solution.py:273
  43.9 89.6 %collective-permute-start.8 = (bf16[1,4096,384]{2,1,0:T(8,128)(2,1)}, bf16[1,4096,384]{2,1,0:T(8,128)(2,1)}, u32[]{:S(2)}, u32[]{:S(2)}) collective-permute-start(bf16[1,4096,384]{2,1,0:T(8,128)(2,1)} %refs_1_.1), channel_id=1, source_target_pairs={{1,0},{3,2},{4,5},{6,7},{9,8},{11,10},{12,13},{14,15},{17,16},{19,... | collective-permute-start | bytes 9437192 | tf_op jit(solution)/shard_map/ppermute | solution.py:273
  65.2 6.6 %collective-permute-start.6 = (bf16[16,4096]{1,0:T(8,128)(2,1)S(1)}, bf16[16,4096]{1,0:T(8,128)(2,1)S(1)}, u32[]{:S(2)}, u32[]{:S(2)}) collective-permute-start(bf16[16,4096]{1,0:T(8,128)(2,1)S(1)} %multiply_convert_fusion), channel_id=1, source_target_pairs={{0,3},{1,2},{2,1},{3,0},{4,7},{5,6},{6,5},{7,4},{8,11},{9,10},{10,... | collective-permute-start | bytes 393224 | tf_op jit(solution)/shard_map/ppermute | solution.py:26
  69.1 48.5 %collective-permute-start.5 = (bf16[16,4096]{1,0:T(8,128)(2,1)S(1)}, bf16[16,4096]{1,0:T(8,128)(2,1)S(1)}, u32[]{:S(2)}, u32[]{:S(2)}) collective-permute-start(bf16[16,4096]{1,0:T(8,128)(2,1)S(1)} %multiply_convert_fusion), channel_id=1, source_target_pairs={{0,2},{1,3},{2,0},{3,1},{4,6},{5,7},{6,4},{7,5},{8,10},{9,11},{10,... | collective-permute-start | bytes 393224 | tf_op jit(solution)/shard_map/ppermute | solution.py:26
  69.1 48.5 %collective-permute-start.4 = (bf16[16,4096]{1,0:T(8,128)(2,1)S(1)}, bf16[16,4096]{1,0:T(8,128)(2,1)S(1)}, u32[]{:S(2)}, u32[]{:S(2)}) collective-permute-start(bf16[16,4096]{1,0:T(8,128)(2,1)S(1)} %multiply_convert_fusion), channel_id=1, source_target_pairs={{0,1},{1,0},{2,3},{3,2},{4,5},{5,4},{6,7},{7,6},{8,9},{9,8},{10,11... | collective-permute-start | bytes 393224 | tf_op jit(solution)/shard_map/ppermute | solution.py:26
  117.6 36.3 %collective-permute-start.13 = (bf16[1,384,4096]{2,1,0:T(8,128)(2,1)}, bf16[1,384,4096]{2,1,0:T(8,128)(2,1)}, u32[]{:S(2)}, u32[]{:S(2)}) collective-permute-start(bf16[1,384,4096]{2,1,0:T(8,128)(2,1)} %own.1), channel_id=1, source_target_pairs={{1,0},{3,2},{4,5},{6,7},{9,8},{11,10},{12,13},{14,15},{17,16},{19,... | collective-permute-start | bytes 9437192 | tf_op jit(solution)/shard_map/ppermute | solution.py:273
  121.0 35.2 %collective-permute-start.9 = (bf16[1,4096,384]{2,1,0:T(8,128)(2,1)}, bf16[1,4096,384]{2,1,0:T(8,128)(2,1)}, u32[]{:S(2)}, u32[]{:S(2)}) collective-permute-start(bf16[1,4096,384]{2,1,0:T(8,128)(2,1)} %refs_0_.1), channel_id=1, source_target_pairs={{0,4},{2,6},{5,1},{7,3},{8,12},{10,14},{13,9},{15,11},{16,20},{18,... | collective-permute-start | bytes 9437192 | tf_op jit(solution)/shard_map/ppermute | solution.py:273
  124.3 31.9 %all-to-all-start.2 = ((bf16[16,16,4096]{2,1,0:T(8,128)(2,1)}), bf16[16,16,4096]{2,1,0:T(8,128)(2,1)}, u32[]{:S(2)}, u32[]{:S(2)}) async-start(bf16[16,16,4096]{2,1,0:T(8,128)(2,1)} %bitcast.7), calls=%async_computation.2 | async-start | bytes 4194304 | tf_op jit(solution)/shard_map/all_to_all | solution.py:340
  131.0 26.7 %collective-permute-start.10 = (bf16[1,4096,384]{2,1,0:T(8,128)(2,1)}, bf16[1,4096,384]{2,1,0:T(8,128)(2,1)}, u32[]{:S(2)}, u32[]{:S(2)}) collective-permute-start(bf16[1,4096,384]{2,1,0:T(8,128)(2,1)} %refs_1_.1), channel_id=1, source_target_pairs={{0,4},{2,6},{5,1},{7,3},{8,12},{10,14},{13,9},{15,11},{16,20},{18,... | collective-permute-start | bytes 9437192 | tf_op jit(solution)/shard_map/ppermute | solution.py:273
  132.3 25.4 %collective-permute-start.11 = (bf16[1,4096,384]{2,1,0:T(8,128)(2,1)}, bf16[1,4096,384]{2,1,0:T(8,128)(2,1)}, u32[]{:S(2)}, u32[]{:S(2)}) collective-permute-start(bf16[1,4096,384]{2,1,0:T(8,128)(2,1)} %collective-permute-done.7.refs_2_), channel_id=1, source_target_pairs={{0,4},{2,6},{5,1},{7,3},{8,12},{10,14},{13,9},{15,11},{16,20},{18,... | collective-permute-start | bytes 9437192 | tf_op jit(solution)/shard_map/ppermute | solution.py:273
  133.6 24.1 %collective-permute-start.12 = (bf16[1,4096,384]{2,1,0:T(8,128)(2,1)}, bf16[1,4096,384]{2,1,0:T(8,128)(2,1)}, u32[]{:S(2)}, u32[]{:S(2)}) collective-permute-start(bf16[1,4096,384]{2,1,0:T(8,128)(2,1)} %collective-permute-done.8.refs_3_), channel_id=1, source_target_pairs={{0,4},{2,6},{5,1},{7,3},{8,12},{10,14},{13,9},{15,11},{16,20},{18,... | collective-permute-start | bytes 9437192 | tf_op jit(solution)/shard_map/ppermute | solution.py:273
  153.9 14.1 %collective-permute-start.14 = (bf16[1,384,4096]{2,1,0:T(8,128)(2,1)}, bf16[1,384,4096]{2,1,0:T(8,128)(2,1)}, u32[]{:S(2)}, u32[]{:S(2)}) collective-permute-start(bf16[1,384,4096]{2,1,0:T(8,128)(2,1)} %own.1), channel_id=1, source_target_pairs={{0,4},{2,6},{5,1},{7,3},{8,12},{10,14},{13,9},{15,11},{16,20},{18,... | collective-permute-start | bytes 9437192 | tf_op jit(solution)/shard_map/ppermute | solution.py:273
  156.2 14.1 %collective-permute-start.15 = (bf16[1,384,4096]{2,1,0:T(8,128)(2,1)}, bf16[1,384,4096]{2,1,0:T(8,128)(2,1)}, u32[]{:S(2)}, u32[]{:S(2)}) collective-permute-start(bf16[1,384,4096]{2,1,0:T(8,128)(2,1)} %collective-permute-done.13.crossed), channel_id=1, source_target_pairs={{0,4},{2,6},{5,1},{7,3},{8,12},{10,14},{13,9},{15,11},{16,20},{18,... | collective-permute-start | bytes 9437192 | tf_op jit(solution)/shard_map/ppermute | solution.py:273
  177.1 30.9 %all-to-all-start.3 = ((bf16[16,16,4096]{2,1,0:T(8,128)(2,1)}), bf16[16,16,4096]{2,1,0:T(8,128)(2,1)S(1)}, u32[]{:S(2)}, u32[]{:S(2)}) async-start(bf16[16,16,4096]{2,1,0:T(8,128)(2,1)} %bitcast.9), calls=%async_computation.3 | async-start | bytes 4194304 | tf_op jit(solution)/shard_map/all_to_all | solution.py:366
  208.6 19.4 %collective-permute-start.18 = (bf16[16,4096]{1,0:T(8,128)(2,1)S(1)}, bf16[16,4096]{1,0:T(8,128)(2,1)S(1)}, u32[]{:S(2)}, u32[]{:S(2)}) collective-permute-start(bf16[16,4096]{1,0:T(8,128)(2,1)S(1)} %get-tuple-element.20), channel_id=1, source_target_pairs={{0,3},{1,2},{2,1},{3,0},{4,7},{5,6},{6,5},{7,4},{8,11},{9,10},{10,... | collective-permute-start | bytes 393224 | tf_op jit(solution)/shard_map/ppermute | solution.py:26
  223.5 6.7 %collective-permute-start.17 = (bf16[16,4096]{1,0:T(8,128)(2,1)S(1)}, bf16[16,4096]{1,0:T(8,128)(2,1)S(1)}, u32[]{:S(2)}, u32[]{:S(2)}) collective-permute-start(bf16[16,4096]{1,0:T(8,128)(2,1)S(1)} %get-tuple-element.21), channel_id=1, source_target_pairs={{0,2},{1,3},{2,0},{3,1},{4,6},{5,7},{6,4},{7,5},{8,10},{9,11},{10,... | collective-permute-start | bytes 393224 | tf_op jit(solution)/shard_map/ppermute | solution.py:26
  223.8 6.5 %collective-permute-start.16 = (bf16[16,4096]{1,0:T(8,128)(2,1)S(1)}, bf16[16,4096]{1,0:T(8,128)(2,1)S(1)}, u32[]{:S(2)}, u32[]{:S(2)}) collective-permute-start(bf16[16,4096]{1,0:T(8,128)(2,1)S(1)} %get-tuple-element.19), channel_id=1, source_target_pairs={{0,1},{1,0},{2,3},{3,2},{4,5},{5,4},{6,7},{7,6},{8,9},{9,8},{10,11... | collective-permute-start | bytes 393224 | tf_op jit(solution)/shard_map/ppermute | solution.py:26
  (5 other events, 64.8 us)

commit v4 on v3

--- a/solution.py
+++ b/solution.py
@@ -263,9 +263,9 @@
     depths = lax.axis_size("dp")
 
     other_proj = flipped(out_proj, "core", 1)
-    places = [(c, d) for c in range(2) for d in range(depths)]
-    across = [(c * depths + d, c * depths + (d ^ 1)) for c, d in places if c != d % 2]
-    beside = [(c * depths + d, (1 - c) * depths + d) for c, d in places if c == d % 2]
+    spots = [(c, d) for c in range(2) for d in range(depths)]
+    across = [(c * depths + d, c * depths + (d ^ 1)) for c, d in spots if c != d % 2]
+    beside = [(c * depths + d, (1 - c) * depths + d) for c, d in spots if c == d % 2]
 
     def moved(slab, pairs, after=None):
         if after is not None:
@@ -277,8 +277,16 @@
     up_near = moved(up_slab, beside)
     down_near = moved(down_slab, beside)
     flag = (core == depth % 2).astype(jnp.int32).reshape(1)
-    other_ids = [flipped(expert_ids, "dp", m) for m in (1, 2, 3)]
-    ids = jnp.concatenate([expert_ids] + other_ids, axis=0)
+    ring = [(c * depths + d, c * depths + (d + 1 - 2 * c) % depths) for c, d in spots]
+
+    def gathered(value):
+        blocks = [value]
+        for _ in range(depths - 1):
+            blocks.append(lax.ppermute(blocks[-1], ("core", "dp"), ring))
+        return blocks
+
+    id_blocks = gathered(expert_ids)
+    ids = jnp.concatenate(id_blocks, axis=0)
 
     piece = out_proj.shape[0]
     sent = attention(
@@ -313,8 +321,8 @@
     dispatch = place[:, None, :] == jnp.arange(slots, dtype=jnp.int32)[None, :, None]
 
     partial = partial.astype(jnp.bfloat16)
-    gate_far = moved(gate_crossed, beside, partial)
     up_crossed = moved(up_slab, across, partial)
+    down_crossed = moved(down_slab, across, partial)
     partial = lax.all_to_all(
         partial.reshape(chips, rows, D),
         "chip",
@@ -327,16 +335,15 @@
     meansq = jnp.mean(hidden * hidden, axis=1, keepdims=True)
     normed = (hidden * lax.rsqrt(jnp.maximum(meansq, 0.25)) * norm_gain).astype(jnp.bfloat16)
 
-    others = [flipped(normed, "dp", m) for m in (1, 2, 3)]
-    tokens = jnp.concatenate([normed] + others, axis=0)
-    down_crossed = moved(down_slab, across, others)
-
+    tokens = jnp.concatenate(gathered(normed), axis=0)
     outgoing = jnp.dot(
         dispatch.reshape(chips * slots, count).astype(jnp.bfloat16),
         tokens,
         preferred_element_type=jnp.float32,
     ).astype(jnp.bfloat16)
+    gate_far = moved(gate_crossed, beside, outgoing)
     up_far = moved(up_crossed, beside, outgoing)
+    down_far = moved(down_crossed, beside, outgoing)
     incoming = lax.all_to_all(
         outgoing.reshape(chips, slots, D), "chip", split_axis=0, concat_axis=0, tiled=True
     )
@@ -353,7 +360,6 @@
     )
     combine = jnp.where(dispatch, spread[:, None, :], 0.0).astype(jnp.bfloat16)
 
-    down_far = moved(down_crossed, beside, incoming)
     act = expert_act(
         flag,
         incoming.reshape(chips * slots, D),
@@ -374,8 +380,10 @@
     )
     total = hidden + mix[:rows]
     narrow = mix.astype(jnp.bfloat16)
-    for m in (1, 2, 3):
-        total = total + flipped(narrow[m * rows : (m + 1) * rows], "dp", m).astype(jnp.float32)
+    for m in range(1, depths):
+        home = [(c * depths + d, c * depths + (d + (2 * c - 1) * m) % depths) for c, d in spots]
+        part = lax.ppermute(narrow[m * rows : (m + 1) * rows], ("core", "dp"), home)
+        total = total + part.astype(jnp.float32)
     return total
 
 

time: 232 us -> 253 us (1.091)
  starting transfers between devices: 62.1 us -> 79.7 us
  waiting for transfers between devices: 116 us -> 119 us
    ppermute x10 -> x1, waiting for transfers between devices: 53.9 us -> 0.01 us  [flipped(): return lax.ppermute(value, axis, pairs)]
    ppermute x0 -> x9, starting transfers between devices: none -> 43.7 us  [the longest x3 22.2 us: local(): part = lax.ppermute(narrow[m * rows:(m + 1) * rows], ('core', 'dp'), home)]
    ppermute x9, waiting for transfers between devices: 21.4 us -> 56.4 us  [moved(): return lax.ppermute(slab, ('core', 'dp'), pairs)]
    ppermute x10 -> x1, starting transfers between devices: 26 us -> 1.38 us  [flipped(): return lax.ppermute(value, axis, pairs)]
    all_to_all x1, waiting for transfers between devices: 1.03 us -> 23.8 us  [local(): lax.all_to_all(outgoing.reshape(chips, slots, D), 'chip', split_axis=0, c...]
    ppermute x0 -> x9, waiting for transfers between devices: none -> 14.4 us  [the longest x6 9.41 us: gathered(): blocks.append(lax.ppermute(blocks[-1], ('core', 'dp'), ring))]
    all_to_all x1, waiting for transfers between devices: 17.7 us -> 3.28 us  [local(): lax.all_to_all(partial.reshape(chips, rows, D), 'chip', split_axis=0, con...]
  transfers between devices with their start and end apart: 22 -> 22, of which waited for: 9 -> 13; matrix products, arithmetic and copies ran while one was open for 2% -> 2% of each run, Pallas kernels for 9% -> 8%
where the time goes in v4:
time: 253 us; the launch traced here: 251 us
  waiting for transfers between devices  119 us (47%)
  starting transfers between devices  79.7 us (32%)
  Pallas kernels  25.5 us (10%)
  blocking collectives  15.3 us (6%)
  matrix products  8.36 us (3%)
    ppermute x9, waiting for transfers between devices, moved(): return lax.ppermute(slab, ('core', 'dp'), pairs)  56.4 us
    all_to_all x1, waiting for transfers between devices, local(): lax.all_to_all(outgoing.reshape(chips, slots, D), 'chip', split_axis=0, c...  23.8 us
    ppermute x3, starting transfers between devices, local(): part = lax.ppermute(narrow[m * rows:(m + 1) * rows], ('core', 'dp'), home)  22.2 us
    ppermute x6, starting transfers between devices, gathered(): blocks.append(lax.ppermute(blocks[-1], ('core', 'dp'), ring))  21.6 us
    all_to_all x1, waiting for transfers between devices, local(): lax.all_to_all(produced.reshape(chips, slots, D), 'chip', split_axis=0, c...  20.9 us
    ppermute x9, starting transfers between devices, moved(): return lax.ppermute(slab, ('core', 'dp'), pairs)  18.9 us
    all_to_all x1, blocking collectives, local(): lax.all_to_all(sent, 'chip', split_axis=0, concat_axis=0, tiled=True)  15.3 us
    pallas_call x1, Pallas kernels, expert_act(): pl.pallas_call(act_kernel, out_shape=jax.ShapeDtypeStruct((count, 2 * hf)...  10.2 us
  transfers between devices with their start and end apart: 22, of which 13 were waited for; matrix products, arithmetic and copies ran while one was open for 2% of the time, Pallas kernels for 8%

profile of v4, /device:TPU:1, one launch (start us, length us, event | category | flops | bytes accessed | tf_op | source)
XLA Modules:
  0.0 251.2 jit_solution(10368432349845597658)
XLA Ops:
  1.4 9.5 %attention.1 = bf16[16,16,512]{2,1,0:T(8,128)(2,1)} custom-call(s32[1]{0:T(128)} %bitcast.swap, s32[16]{0:T(128)} %lengths.1, bf16[16,8192]{1,0:T(8,128)(2,1)} %q_in.1, bf16[16,512]{1,0:T(8,128)(2,1)} %nk_in.1, bf16[16,512]{1,0:T(8,128)(2,1)} %nv_in.1, bf16[16,128,512]{2,1,0:T(8,128)(2,1)} %keys.1, bf16[16,128,512]{2,1,0:T(8,128)(2,1)} %values.1), custom_call_target="tpu_custom_call" | custom-call | flops 134217728 | bytes 4194304 | tf_op jit(solution)/shard_map/attention/pallas_call | solution.py:104
  10.9 15.3 %all_to_all.20 = bf16[16,16,512]{2,1,0:T(8,128)(2,1)S(1)} all-to-all(bf16[16,16,512]{2,1,0:T(8,128)(2,1)} %attention.1), channel_id=1, replica_groups=mesh['chip'=16,'core'=2,'dp'=4] {'chip'}, dimensions={0} | all-to-all | bytes 524288 | tf_op jit(solution)/shard_map/all_to_all | solution.py:302
  27.0 3.8 %fusion = bf16[256,4096]{1,0:T(8,128)(2,1)} fusion(f32[256,4096]{1,0:T(8,128)S(1)} %fusion.7, bf16[256,4096]{1,0:T(8,128)(2,1)} %collective-permute-done, bf16[256,512]{1,0:T(8,128)(2,1)S(1)} %bitcast.21), kind=kOutput, calls=%fused_computation.1 | convolution fusion | flops 538968064 | bytes 8519680 | tf_op jit(solution)/shard_map/dot_general | solution.py:305
  30.8 3.8 %all-to-all-start.1 = ((bf16[16,16,4096]{2,1,0:T(8,128)(2,1)}), bf16[16,16,4096]{2,1,0:T(8,128)(2,1)S(1)}, u32[]{:S(2)}, u32[]{:S(2)}) async-start(bf16[16,16,4096]{2,1,0:T(8,128)(2,1)} %bitcast.19), calls=%async_computation.1 | async-start | bytes 4194304 | tf_op jit(solution)/shard_map/all_to_all | solution.py:326
  34.6 5.3 %collective-permute-start.7 = (bf16[1,4096,384]{2,1,0:T(8,128)(2,1)}, bf16[1,4096,384]{2,1,0:T(8,128)(2,1)}, u32[]{:S(2)}, u32[]{:S(2)}) collective-permute-start(bf16[1,4096,384]{2,1,0:T(8,128)(2,1)} %refs_0_.1), channel_id=1, source_target_pairs={{1,0},{3,2},{4,5},{6,7},{9,8},{11,10},{12,13},{14,15},{17,16},{19,... | collective-permute-start | bytes 9437192 | tf_op jit(solution)/shard_map/ppermute | solution.py:273
  40.0 2.9 %collective-permute-start.8 = (bf16[1,4096,384]{2,1,0:T(8,128)(2,1)}, bf16[1,4096,384]{2,1,0:T(8,128)(2,1)}, u32[]{:S(2)}, u32[]{:S(2)}) collective-permute-start(bf16[1,4096,384]{2,1,0:T(8,128)(2,1)} %refs_1_.1), channel_id=1, source_target_pairs={{1,0},{3,2},{4,5},{6,7},{9,8},{11,10},{12,13},{14,15},{17,16},{19,... | collective-permute-start | bytes 9437192 | tf_op jit(solution)/shard_map/ppermute | solution.py:273
  44.2 6.0 %collective-permute-start.1 = (s32[16,8]{0,1:T(8,128)S(1)}, s32[16,8]{0,1:T(8,128)S(1)}, u32[]{:S(2)}, u32[]{:S(2)}) collective-permute-start(s32[16,8]{0,1:T(8,128)S(1)} %copy-done.6), channel_id=1, source_target_pairs={{0,1},{1,2},{2,3},{3,0},{4,7},{5,4},{6,5},{7,6},{8,9},{9,10},{10,1... | collective-permute-start | bytes 1544 | tf_op jit(solution)/shard_map/ppermute | solution.py:285
  50.9 3.2 %collective-permute-start.2 = (s32[16,8]{0,1:T(8,128)S(1)}, s32[16,8]{0,1:T(8,128)S(1)}, u32[]{:S(2)}, u32[]{:S(2)}) collective-permute-start(s32[16,8]{0,1:T(8,128)S(1)} %collective-permute-done.1), channel_id=1, source_target_pairs={{0,1},{1,2},{2,3},{3,0},{4,7},{5,4},{6,5},{7,6},{8,9},{9,10},{10,1... | collective-permute-start | bytes 1544 | tf_op jit(solution)/shard_map/ppermute | solution.py:285
  54.9 3.2 %collective-permute-start.3 = (s32[16,8]{0,1:T(8,128)S(1)}, s32[16,8]{0,1:T(8,128)S(1)}, u32[]{:S(2)}, u32[]{:S(2)}) collective-permute-start(s32[16,8]{0,1:T(8,128)S(1)} %collective-permute-done.2), channel_id=1, source_target_pairs={{0,1},{1,2},{2,3},{3,0},{4,7},{5,4},{6,5},{7,6},{8,9},{9,10},{10,1... | collective-permute-start | bytes 1544 | tf_op jit(solution)/shard_map/ppermute | solution.py:285
  61.4 3.3 %all-to-all-done.1 = bf16[16,16,4096]{2,1,0:T(8,128)(2,1)S(1)} async-done(((bf16[16,16,4096]{2,1,0:T(8,128)(2,1)}), bf16[16,16,4096]{2,1,0:T(8,128)(2,1)S(1)}, u32[]{:S(2)}, u32[]{:S(2)}) %all-to-all-start.1) | async-done | bytes 2097184 | tf_op jit(solution)/shard_map/all_to_all | solution.py:326
  65.3 3.8 %collective-permute-start.4 = (bf16[16,4096]{1,0:T(8,128)(2,1)S(1)}, bf16[16,4096]{1,0:T(8,128)(2,1)S(1)}, u32[]{:S(2)}, u32[]{:S(2)}) collective-permute-start(bf16[16,4096]{1,0:T(8,128)(2,1)S(1)} %multiply_convert_fusion), channel_id=1, source_target_pairs={{0,1},{1,2},{2,3},{3,0},{4,7},{5,4},{6,5},{7,6},{8,9},{9,10},{10,1... | collective-permute-start | bytes 393224 | tf_op jit(solution)/shard_map/ppermute | solution.py:285
  71.1 3.0 %collective-permute-start.5 = (bf16[16,4096]{1,0:T(8,128)(2,1)S(1)}, bf16[16,4096]{1,0:T(8,128)(2,1)S(1)}, u32[]{:S(2)}, u32[]{:S(2)}) collective-permute-start(bf16[16,4096]{1,0:T(8,128)(2,1)S(1)} %collective-permute-done.4), channel_id=1, source_target_pairs={{0,1},{1,2},{2,3},{3,0},{4,7},{5,4},{6,5},{7,6},{8,9},{9,10},{10,1... | collective-permute-start | bytes 393224 | tf_op jit(solution)/shard_map/ppermute | solution.py:285
  79.1 3.2 %collective-permute-done.6 = bf16[16,4096]{1,0:T(8,128)(2,1)S(1)} collective-permute-done((bf16[16,4096]{1,0:T(8,128)(2,1)S(1)}, bf16[16,4096]{1,0:T(8,128)(2,1)S(1)}, u32[]{:S(2)}, u32[]{:S(2)}) %collective-permute-start.6) | collective-permute-done | bytes 131104 | tf_op jit(solution)/shard_map/ppermute | solution.py:285
  87.0 23.9 %collective-permute-done.8.refs_3_ = bf16[1,4096,384]{2,1,0:T(8,128)(2,1)} collective-permute-done((bf16[1,4096,384]{2,1,0:T(8,128)(2,1)}, bf16[1,4096,384]{2,1,0:T(8,128)(2,1)}, u32[]{:S(2)}, u32[]{:S(2)}) %collective-permute-start.8) | collective-permute-done | bytes 3145760 | tf_op jit(solution)/shard_map/ppermute | solution.py:273
  112.2 32.4 %collective-permute-done.13.crossed = bf16[1,384,4096]{2,1,0:T(8,128)(2,1)} collective-permute-done((bf16[1,384,4096]{2,1,0:T(8,128)(2,1)}, bf16[1,384,4096]{2,1,0:T(8,128)(2,1)}, u32[]{:S(2)}, u32[]{:S(2)}) %collective-permute-start.13) | collective-permute-done | bytes 3145760 | tf_op jit(solution)/shard_map/ppermute | solution.py:273
  147.2 6.7 %all-to-all-start.2 = ((bf16[16,16,4096]{2,1,0:T(8,128)(2,1)}), bf16[16,16,4096]{2,1,0:T(8,128)(2,1)}, u32[]{:S(2)}, u32[]{:S(2)}) async-start(bf16[16,16,4096]{2,1,0:T(8,128)(2,1)} %bitcast.7), calls=%async_computation.2 | async-start | bytes 4194304 | tf_op jit(solution)/shard_map/all_to_all | solution.py:347
  153.9 23.8 %all-to-all-done.2 = bf16[16,16,4096]{2,1,0:T(8,128)(2,1)} async-done(((bf16[16,16,4096]{2,1,0:T(8,128)(2,1)}), bf16[16,16,4096]{2,1,0:T(8,128)(2,1)}, u32[]{:S(2)}, u32[]{:S(2)}) %all-to-all-start.2) | async-done | bytes 2097184 | tf_op jit(solution)/shard_map/all_to_all | solution.py:347
  177.6 10.2 %expert_act.1.act = bf16[256,768]{1,0:T(8,128)(2,1)} custom-call(s32[1]{0:T(128)} %bitcast.5.flag, bf16[256,4096]{1,0:T(8,128)(2,1)} %bitcast.8.rows_in, bf16[1,4096,384]{2,1,0:T(8,128)(2,1)} %refs_0_.1, bf16[1,4096,384]{2,1,0:T(8,128)(2,1)} %refs_1_.1, bf16[1,4096,384]{2,1,0:T(8,128)(2,1)} %collective-permute-done.7.refs_2_, ...), custom_call_target="tpu_custom_call" | custom-call | flops 3221225472 | bytes 14680064 | tf_op jit(solution)/shard_map/expert_act/pallas_call | solution.py:202
  188.9 5.8 %expert_down.1 = bf16[256,4096]{1,0:T(8,128)(2,1)} custom-call(s32[1]{0:T(128)} %bitcast.5.flag, bf16[256,768]{1,0:T(8,128)(2,1)S(1)} %copy-done.1, bf16[1,384,4096]{2,1,0:T(8,128)(2,1)} %own.1, bf16[1,384,4096]{2,1,0:T(8,128)(2,1)} %collective-permute-done.13.crossed, bf16[1,384,4096]{2,1,0:T(8,128)(2,1)} %collective-permute-done.14.near, ...), custom_call_target="tpu_custom_call" | custom-call | flops 1610612736 | bytes 8388608 | tf_op jit(solution)/shard_map/expert_down/pallas_call | solution.py:225
  194.7 5.2 %all-to-all-start.3 = ((bf16[16,16,4096]{2,1,0:T(8,128)(2,1)}), bf16[16,16,4096]{2,1,0:T(8,128)(2,1)S(1)}, u32[]{:S(2)}, u32[]{:S(2)}) async-start(bf16[16,16,4096]{2,1,0:T(8,128)(2,1)} %bitcast.9), calls=%async_computation.3 | async-start | bytes 4194304 | tf_op jit(solution)/shard_map/all_to_all | solution.py:372
  201.7 20.9 %all-to-all-done.3 = bf16[16,16,4096]{2,1,0:T(8,128)(2,1)S(1)} async-done(((bf16[16,16,4096]{2,1,0:T(8,128)(2,1)}), bf16[16,16,4096]{2,1,0:T(8,128)(2,1)S(1)}, u32[]{:S(2)}, u32[]{:S(2)}) %all-to-all-start.3) | async-done | bytes 2097184 | tf_op jit(solution)/shard_map/all_to_all | solution.py:372
  223.1 18.6 %collective-permute-start.16 = (bf16[16,4096]{1,0:T(8,128)(2,1)S(1)}, bf16[16,4096]{1,0:T(8,128)(2,1)S(1)}, u32[]{:S(2)}, u32[]{:S(2)}) collective-permute-start(bf16[16,4096]{1,0:T(8,128)(2,1)S(1)} %get-tuple-element.19), channel_id=1, source_target_pairs={{0,3},{1,0},{2,1},{3,2},{4,5},{5,6},{6,7},{7,4},{8,11},{9,8},{10,9... | collective-permute-start | bytes 393224 | tf_op jit(solution)/shard_map/ppermute | solution.py:385
  241.7 3.6 %collective-permute-start.17 = (bf16[16,4096]{1,0:T(8,128)(2,1)S(1)}, bf16[16,4096]{1,0:T(8,128)(2,1)S(1)}, u32[]{:S(2)}, u32[]{:S(2)}) collective-permute-start(bf16[16,4096]{1,0:T(8,128)(2,1)S(1)} %get-tuple-element.21), channel_id=1, source_target_pairs={{0,2},{1,3},{2,0},{3,1},{4,6},{5,7},{6,4},{7,5},{8,10},{9,11},{10,... | collective-permute-start | bytes 393224 | tf_op jit(solution)/shard_map/ppermute | solution.py:385
  246.5 3.5 %collective-permute-done.17 = bf16[16,4096]{1,0:T(8,128)(2,1)S(1)} collective-permute-done((bf16[16,4096]{1,0:T(8,128)(2,1)S(1)}, bf16[16,4096]{1,0:T(8,128)(2,1)S(1)}, u32[]{:S(2)}, u32[]{:S(2)}) %collective-permute-start.17) | collective-permute-done | bytes 131104 | tf_op jit(solution)/shard_map/ppermute | solution.py:385
  (62 shorter events, 29.9 us)
Async XLA Ops:
  0.0 200.0 %copy-start = (bf16[4096,64]{0,1:T(8,128)(2,1)S(1)}, bf16[4096,64]{0,1:T(8,128)(2,1)}, u32[]{:S(2)}) copy-start(bf16[4096,64]{0,1:T(8,128)(2,1)} %param.23) | copy-start | bytes 1572868
  0.0 27.0 %collective-permute-start = (bf16[256,4096]{1,0:T(8,128)(2,1)}, bf16[256,4096]{1,0:T(8,128)(2,1)}, u32[]{:S(2)}, u32[]{:S(2)}) collective-permute-start(bf16[256,4096]{1,0:T(8,128)(2,1)} %param.21), channel_id=1, source_target_pairs={{0,4},{4,0},{1,5},{5,1},{2,6},{6,2},{3,7},{7,3},{8,12},{12,8},{9,1... | collective-permute-start | bytes 6291464 | tf_op jit(solution)/shard_map/ppermute | solution.py:26
  30.8 33.9 %all-to-all-start.1 = ((bf16[16,16,4096]{2,1,0:T(8,128)(2,1)}), bf16[16,16,4096]{2,1,0:T(8,128)(2,1)S(1)}, u32[]{:S(2)}, u32[]{:S(2)}) async-start(bf16[16,16,4096]{2,1,0:T(8,128)(2,1)} %bitcast.19), calls=%async_computation.1 | async-start | bytes 4194304 | tf_op jit(solution)/shard_map/all_to_all | solution.py:326
  34.6 30.5 %copy-start.5 = (f32[4096]{0:T(1024)S(1)}, f32[4096]{0:T(1024)}, u32[]{:S(2)}) copy-start(f32[4096]{0:T(1024)} %param.22) | copy-start | bytes 49156
  34.6 51.0 %collective-permute-start.7 = (bf16[1,4096,384]{2,1,0:T(8,128)(2,1)}, bf16[1,4096,384]{2,1,0:T(8,128)(2,1)}, u32[]{:S(2)}, u32[]{:S(2)}) collective-permute-start(bf16[1,4096,384]{2,1,0:T(8,128)(2,1)} %refs_0_.1), channel_id=1, source_target_pairs={{1,0},{3,2},{4,5},{6,7},{9,8},{11,10},{12,13},{14,15},{17,16},{19,... | collective-permute-start | bytes 9437192 | tf_op jit(solution)/shard_map/ppermute | solution.py:273
  40.0 70.9 %collective-permute-start.8 = (bf16[1,4096,384]{2,1,0:T(8,128)(2,1)}, bf16[1,4096,384]{2,1,0:T(8,128)(2,1)}, u32[]{:S(2)}, u32[]{:S(2)}) collective-permute-start(bf16[1,4096,384]{2,1,0:T(8,128)(2,1)} %refs_1_.1), channel_id=1, source_target_pairs={{1,0},{3,2},{4,5},{6,7},{9,8},{11,10},{12,13},{14,15},{17,16},{19,... | collective-permute-start | bytes 9437192 | tf_op jit(solution)/shard_map/ppermute | solution.py:273
  42.9 103.0 %collective-permute-start.10 = (bf16[1,4096,384]{2,1,0:T(8,128)(2,1)}, bf16[1,4096,384]{2,1,0:T(8,128)(2,1)}, u32[]{:S(2)}, u32[]{:S(2)}) collective-permute-start(bf16[1,4096,384]{2,1,0:T(8,128)(2,1)} %refs_1_.1), channel_id=1, source_target_pairs={{0,4},{2,6},{5,1},{7,3},{8,12},{10,14},{13,9},{15,11},{16,20},{18,... | collective-permute-start | bytes 9437192 | tf_op jit(solution)/shard_map/ppermute | solution.py:273
  44.2 6.7 %collective-permute-start.1 = (s32[16,8]{0,1:T(8,128)S(1)}, s32[16,8]{0,1:T(8,128)S(1)}, u32[]{:S(2)}, u32[]{:S(2)}) collective-permute-start(s32[16,8]{0,1:T(8,128)S(1)} %copy-done.6), channel_id=1, source_target_pairs={{0,1},{1,2},{2,3},{3,0},{4,7},{5,4},{6,5},{7,6},{8,9},{9,10},{10,1... | collective-permute-start | bytes 1544 | tf_op jit(solution)/shard_map/ppermute | solution.py:285
  50.9 4.0 %collective-permute-start.2 = (s32[16,8]{0,1:T(8,128)S(1)}, s32[16,8]{0,1:T(8,128)S(1)}, u32[]{:S(2)}, u32[]{:S(2)}) collective-permute-start(s32[16,8]{0,1:T(8,128)S(1)} %collective-permute-done.1), channel_id=1, source_target_pairs={{0,1},{1,2},{2,3},{3,0},{4,7},{5,4},{6,5},{7,6},{8,9},{9,10},{10,1... | collective-permute-start | bytes 1544 | tf_op jit(solution)/shard_map/ppermute | solution.py:285
  54.9 6.1 %collective-permute-start.3 = (s32[16,8]{0,1:T(8,128)S(1)}, s32[16,8]{0,1:T(8,128)S(1)}, u32[]{:S(2)}, u32[]{:S(2)}) collective-permute-start(s32[16,8]{0,1:T(8,128)S(1)} %collective-permute-done.2), channel_id=1, source_target_pairs={{0,1},{1,2},{2,3},{3,0},{4,7},{5,4},{6,5},{7,6},{8,9},{9,10},{10,1... | collective-permute-start | bytes 1544 | tf_op jit(solution)/shard_map/ppermute | solution.py:285
  58.1 86.5 %collective-permute-start.13 = (bf16[1,384,4096]{2,1,0:T(8,128)(2,1)}, bf16[1,384,4096]{2,1,0:T(8,128)(2,1)}, u32[]{:S(2)}, u32[]{:S(2)}) collective-permute-start(bf16[1,384,4096]{2,1,0:T(8,128)(2,1)} %own.1), channel_id=1, source_target_pairs={{1,0},{3,2},{4,5},{6,7},{9,8},{11,10},{12,13},{14,15},{17,16},{19,... | collective-permute-start | bytes 9437192 | tf_op jit(solution)/shard_map/ppermute | solution.py:273
  65.3 5.9 %collective-permute-start.4 = (bf16[16,4096]{1,0:T(8,128)(2,1)S(1)}, bf16[16,4096]{1,0:T(8,128)(2,1)S(1)}, u32[]{:S(2)}, u32[]{:S(2)}) collective-permute-start(bf16[16,4096]{1,0:T(8,128)(2,1)S(1)} %multiply_convert_fusion), channel_id=1, source_target_pairs={{0,1},{1,2},{2,3},{3,0},{4,7},{5,4},{6,5},{7,6},{8,9},{9,10},{10,1... | collective-permute-start | bytes 393224 | tf_op jit(solution)/shard_map/ppermute | solution.py:285
  71.1 5.6 %collective-permute-start.5 = (bf16[16,4096]{1,0:T(8,128)(2,1)S(1)}, bf16[16,4096]{1,0:T(8,128)(2,1)S(1)}, u32[]{:S(2)}, u32[]{:S(2)}) collective-permute-start(bf16[16,4096]{1,0:T(8,128)(2,1)S(1)} %collective-permute-done.4), channel_id=1, source_target_pairs={{0,1},{1,2},{2,3},{3,0},{4,7},{5,4},{6,5},{7,6},{8,9},{9,10},{10,1... | collective-permute-start | bytes 393224 | tf_op jit(solution)/shard_map/ppermute | solution.py:285
  76.7 5.6 %collective-permute-start.6 = (bf16[16,4096]{1,0:T(8,128)(2,1)S(1)}, bf16[16,4096]{1,0:T(8,128)(2,1)S(1)}, u32[]{:S(2)}, u32[]{:S(2)}) collective-permute-start(bf16[16,4096]{1,0:T(8,128)(2,1)S(1)} %collective-permute-done.5), channel_id=1, source_target_pairs={{0,1},{1,2},{2,3},{3,0},{4,7},{5,4},{6,5},{7,6},{8,9},{9,10},{10,1... | collective-permute-start | bytes 393224 | tf_op jit(solution)/shard_map/ppermute | solution.py:285
  82.4 71.5 %collective-permute-start.9 = (bf16[1,4096,384]{2,1,0:T(8,128)(2,1)}, bf16[1,4096,384]{2,1,0:T(8,128)(2,1)}, u32[]{:S(2)}, u32[]{:S(2)}) collective-permute-start(bf16[1,4096,384]{2,1,0:T(8,128)(2,1)} %refs_0_.1), channel_id=1, source_target_pairs={{0,4},{2,6},{5,1},{7,3},{8,12},{10,14},{13,9},{15,11},{16,20},{18,... | collective-permute-start | bytes 9437192 | tf_op jit(solution)/shard_map/ppermute | solution.py:273
  85.7 92.0 %collective-permute-start.11 = (bf16[1,4096,384]{2,1,0:T(8,128)(2,1)}, bf16[1,4096,384]{2,1,0:T(8,128)(2,1)}, u32[]{:S(2)}, u32[]{:S(2)}) collective-permute-start(bf16[1,4096,384]{2,1,0:T(8,128)(2,1)} %collective-permute-done.7.refs_2_), channel_id=1, source_target_pairs={{0,4},{2,6},{5,1},{7,3},{8,12},{10,14},{13,9},{15,11},{16,20},{18,... | collective-permute-start | bytes 9437192 | tf_op jit(solution)/shard_map/ppermute | solution.py:273
  110.9 66.8 %collective-permute-start.12 = (bf16[1,4096,384]{2,1,0:T(8,128)(2,1)}, bf16[1,4096,384]{2,1,0:T(8,128)(2,1)}, u32[]{:S(2)}, u32[]{:S(2)}) collective-permute-start(bf16[1,4096,384]{2,1,0:T(8,128)(2,1)} %collective-permute-done.8.refs_3_), channel_id=1, source_target_pairs={{0,4},{2,6},{5,1},{7,3},{8,12},{10,14},{13,9},{15,11},{16,20},{18,... | collective-permute-start | bytes 9437192 | tf_op jit(solution)/shard_map/ppermute | solution.py:273
  144.6 43.3 %collective-permute-start.14 = (bf16[1,384,4096]{2,1,0:T(8,128)(2,1)}, bf16[1,384,4096]{2,1,0:T(8,128)(2,1)}, u32[]{:S(2)}, u32[]{:S(2)}) collective-permute-start(bf16[1,384,4096]{2,1,0:T(8,128)(2,1)} %own.1), channel_id=1, source_target_pairs={{0,4},{2,6},{5,1},{7,3},{8,12},{10,14},{13,9},{15,11},{16,20},{18,... | collective-permute-start | bytes 9437192 | tf_op jit(solution)/shard_map/ppermute | solution.py:273
  145.9 42.0 %collective-permute-start.15 = (bf16[1,384,4096]{2,1,0:T(8,128)(2,1)}, bf16[1,384,4096]{2,1,0:T(8,128)(2,1)}, u32[]{:S(2)}, u32[]{:S(2)}) collective-permute-start(bf16[1,384,4096]{2,1,0:T(8,128)(2,1)} %collective-permute-done.13.crossed), channel_id=1, source_target_pairs={{0,4},{2,6},{5,1},{7,3},{8,12},{10,14},{13,9},{15,11},{16,20},{18,... | collective-permute-start | bytes 9437192 | tf_op jit(solution)/shard_map/ppermute | solution.py:273
  147.2 30.4 %all-to-all-start.2 = ((bf16[16,16,4096]{2,1,0:T(8,128)(2,1)}), bf16[16,16,4096]{2,1,0:T(8,128)(2,1)}, u32[]{:S(2)}, u32[]{:S(2)}) async-start(bf16[16,16,4096]{2,1,0:T(8,128)(2,1)} %bitcast.7), calls=%async_computation.2 | async-start | bytes 4194304 | tf_op jit(solution)/shard_map/all_to_all | solution.py:347
  194.7 27.9 %all-to-all-start.3 = ((bf16[16,16,4096]{2,1,0:T(8,128)(2,1)}), bf16[16,16,4096]{2,1,0:T(8,128)(2,1)S(1)}, u32[]{:S(2)}, u32[]{:S(2)}) async-start(bf16[16,16,4096]{2,1,0:T(8,128)(2,1)} %bitcast.9), calls=%async_computation.3 | async-start | bytes 4194304 | tf_op jit(solution)/shard_map/all_to_all | solution.py:372
  223.1 23.3 %collective-permute-start.16 = (bf16[16,4096]{1,0:T(8,128)(2,1)S(1)}, bf16[16,4096]{1,0:T(8,128)(2,1)S(1)}, u32[]{:S(2)}, u32[]{:S(2)}) collective-permute-start(bf16[16,4096]{1,0:T(8,128)(2,1)S(1)} %get-tuple-element.19), channel_id=1, source_target_pairs={{0,3},{1,0},{2,1},{3,2},{4,5},{5,6},{6,7},{7,4},{8,11},{9,8},{10,9... | collective-permute-start | bytes 393224 | tf_op jit(solution)/shard_map/ppermute | solution.py:385
  241.7 8.3 %collective-permute-start.17 = (bf16[16,4096]{1,0:T(8,128)(2,1)S(1)}, bf16[16,4096]{1,0:T(8,128)(2,1)S(1)}, u32[]{:S(2)}, u32[]{:S(2)}) collective-permute-start(bf16[16,4096]{1,0:T(8,128)(2,1)S(1)} %get-tuple-element.21), channel_id=1, source_target_pairs={{0,2},{1,3},{2,0},{3,1},{4,6},{5,7},{6,4},{7,5},{8,10},{9,11},{10,... | collective-permute-start | bytes 393224 | tf_op jit(solution)/shard_map/ppermute | solution.py:385
  245.3 5.0 %collective-permute-start.18 = (bf16[16,4096]{1,0:T(8,128)(2,1)S(1)}, bf16[16,4096]{1,0:T(8,128)(2,1)S(1)}, u32[]{:S(2)}, u32[]{:S(2)}) collective-permute-start(bf16[16,4096]{1,0:T(8,128)(2,1)S(1)} %get-tuple-element.20), channel_id=1, source_target_pairs={{0,1},{1,2},{2,3},{3,0},{4,7},{5,4},{6,5},{7,6},{8,9},{9,10},{10,1... | collective-permute-start | bytes 393224 | tf_op jit(solution)/shard_map/ppermute | solution.py:385
  (5 other events, 71.0 us)

commit v5 on v4

--- a/solution.py
+++ b/solution.py
@@ -14,7 +14,9 @@
 HD = 128
 CAP = 4
 ATTN_STEPS = 2
-OUT_STEPS = 4
+OUT_STEPS = 2
+CUTS = 8
+X_CUTS = 4
 
 
 EP = ("chip", "core")
@@ -127,117 +129,109 @@
     )(swap, cache_len, queries, new_keys, new_values, cache_keys, cache_values)
 
 
-def start_slabs(flag, own, crossed, near, far, start):
+def ffn_kernel(flag, rows_in, *refs):
+    own, crossed, near, far = refs[0:3], refs[3:6], refs[6:9], refs[9:12]
+    out, x_buf, in_buf, down_buf, y_buf, x_sem, in_sem, down_sem, y_sem = refs[12:]
+    hf = own[0].shape[2]
+    deep = D // CUTS
+    wide = D // OUT_STEPS
+
+    def x_copy(cut):
+        part = pl.ds(cut * rows_in.shape[0] // X_CUTS, rows_in.shape[0] // X_CUTS)
+        return pltpu.make_async_copy(rows_in.at[part], x_buf.at[part], x_sem.at[cut])
+
+    def in_copy(side, source, part, cut):
+        return pltpu.make_async_copy(
+            source[part].at[0, pl.ds(cut * deep, deep)],
+            in_buf.at[2 * side + part, pl.ds(cut * deep, deep)],
+            in_sem.at[2 * side + part, cut],
+        )
+
+    def down_copy(side, source, step):
+        return pltpu.make_async_copy(
+            source[2].at[0, :, pl.ds(step * wide, wide)],
+            down_buf.at[pl.ds(side * hf, hf), pl.ds(step * wide, wide)],
+            down_sem.at[side, step],
+        )
+
+    def start(first, second):
+        for side, source in ((0, first), (1, second)):
+            for part in range(2):
+                for cut in range(CUTS):
+                    in_copy(side, source, part, cut).start()
+        for step in range(OUT_STEPS):
+            down_copy(0, first, step).start()
+            down_copy(1, second, step).start()
+
+    for cut in range(X_CUTS):
+        x_copy(cut).start()
+
     @pl.when(flag[0] == 1)
     def _():
-        start(0, own)
-        start(1, crossed)
+        start(own, crossed)
 
     @pl.when(flag[0] != 1)
     def _():
-        start(0, near)
-        start(1, far)
-
-
-def act_kernel(flag, rows_in, *refs):
-    own, crossed, near, far = refs[0:2], refs[2:4], refs[4:6], refs[6:8]
-    out, x_buf, buf, x_sem, sem = refs[8:]
-    hf = own[0].shape[2]
-
-    def copy(side, source, part):
-        return pltpu.make_async_copy(
-            source[part].at[0], buf.at[2 * side + part], sem.at[2 * side + part]
-        )
-
-    def start(side, source):
-        for part in range(2):
-            copy(side, source, part).start()
-
-    x_copy = pltpu.make_async_copy(rows_in, x_buf, x_sem)
-    x_copy.start()
-    start_slabs(flag, own, crossed, near, far, start)
-    x_copy.wait()
+        start(near, far)
+
+    for cut in range(X_CUTS):
+        x_copy(cut).wait()
+    acts = []
     for side in range(2):
         vals = []
         for part in range(2):
-            copy(side, own, part).wait()
+            for cut in range(CUTS):
+                in_copy(side, own, part, cut).wait()
             vals.append(
-                jnp.dot(x_buf[...], buf[2 * side + part], preferred_element_type=jnp.float32)
+                jnp.dot(x_buf[...], in_buf[2 * side + part], preferred_element_type=jnp.float32)
             )
         gate_val, up_val = vals
-        out[:, side * hf : (side + 1) * hf] = (
-            gate_val / (1.0 + jnp.exp(-gate_val)) * up_val
+        acts.append((gate_val / (1.0 + jnp.exp(-gate_val)) * up_val).astype(jnp.bfloat16))
+    act = jnp.concatenate(acts, axis=1)
+    copies = []
+    for step in range(OUT_STEPS):
+        columns = slice(step * wide, (step + 1) * wide)
+        for side in range(2):
+            down_copy(side, own, step).wait()
+        y_buf[:, columns] = jnp.dot(
+            act, down_buf[:, columns], preferred_element_type=jnp.float32
         ).astype(jnp.bfloat16)
-
-
-def down_kernel(flag, act, own, crossed, near, far, out, buf, sem):
-    hf = own.shape[1]
-    wide = D // OUT_STEPS
-
-    def copy(side, source, step):
-        return pltpu.make_async_copy(
-            source.at[0, :, pl.ds(step * wide, wide)],
-            buf.at[pl.ds(side * hf, hf), pl.ds(step * wide, wide)],
-            sem.at[side, step],
-        )
-
-    def start(side, source):
-        for step in range(OUT_STEPS):
-            copy(side, source, step).start()
-
-    start_slabs(flag, own, crossed, near, far, start)
-    for step in range(OUT_STEPS):
-        for side in range(2):
-            copy(side, own, step).wait()
-        out[:, step * wide : (step + 1) * wide] = jnp.dot(
-            act[...],
-            buf[:, step * wide : (step + 1) * wide],
-            preferred_element_type=jnp.float32,
-        ).astype(jnp.bfloat16)
-
-
-def expert_act(flag, rows_in, own, crossed, near, far):
+        copy = pltpu.make_async_copy(
+            y_buf.at[:, pl.ds(step * wide, wide)],
+            out.at[:, pl.ds(step * wide, wide)],
+            y_sem.at[step],
+        )
+        copy.start()
+        copies.append(copy)
+    for copy in copies:
+        copy.wait()
+
+
+def expert_ffn(flag, rows_in, own, crossed, near, far):
     count = rows_in.shape[0]
     hf = own[0].shape[2]
     return pl.pallas_call(
-        act_kernel,
-        out_shape=jax.ShapeDtypeStruct((count, 2 * hf), jnp.bfloat16),
+        ffn_kernel,
+        out_shape=jax.ShapeDtypeStruct((count, D), jnp.bfloat16),
         in_specs=[pl.BlockSpec(memory_space=pltpu.SMEM)]
-        + [pl.BlockSpec(memory_space=pltpu.HBM)] * 9,
-        out_specs=pl.BlockSpec(memory_space=pltpu.VMEM),
+        + [pl.BlockSpec(memory_space=pltpu.HBM)] * 13,
+        out_specs=pl.BlockSpec(memory_space=pltpu.HBM),
         scratch_shapes=[
             pltpu.VMEM((count, D), jnp.bfloat16),
             pltpu.VMEM((4, D, hf), jnp.bfloat16),
-            pltpu.SemaphoreType.DMA,
-            pltpu.SemaphoreType.DMA((4,)),
+            pltpu.VMEM((2 * hf, D), jnp.bfloat16),
+            pltpu.VMEM((count, D), jnp.bfloat16),
+            pltpu.SemaphoreType.DMA((X_CUTS,)),
+            pltpu.SemaphoreType.DMA((4, CUTS)),
+            pltpu.SemaphoreType.DMA((2, OUT_STEPS)),
+            pltpu.SemaphoreType.DMA((OUT_STEPS,)),
         ],
         compiler_params=pltpu.CompilerParams(vmem_limit_bytes=123 * 512 * 1024),
         cost_estimate=pl.CostEstimate(
-            flops=8 * count * D * hf, bytes_accessed=8 * D * hf + 2 * count * D, transcendentals=0
+            flops=12 * count * D * hf, bytes_accessed=12 * D * hf + 4 * count * D, transcendentals=0
         ),
-        name="expert_act",
+        name="expert_ffn",
     )(flag, rows_in, *own, *crossed, *near, *far)
-
-
-def expert_down(flag, act, own, crossed, near, far):
-    count = act.shape[0]
-    hf = own.shape[1]
-    return pl.pallas_call(
-        down_kernel,
-        out_shape=jax.ShapeDtypeStruct((count, D), jnp.bfloat16),
-        in_specs=[pl.BlockSpec(memory_space=pltpu.SMEM), pl.BlockSpec(memory_space=pltpu.VMEM)]
-        + [pl.BlockSpec(memory_space=pltpu.HBM)] * 4,
-        out_specs=pl.BlockSpec(memory_space=pltpu.VMEM),
-        scratch_shapes=[
-            pltpu.VMEM((2 * hf, D), jnp.bfloat16),
-            pltpu.SemaphoreType.DMA((2, OUT_STEPS)),
-        ],
-        compiler_params=pltpu.CompilerParams(vmem_limit_bytes=20 * 1024 * 1024),
-        cost_estimate=pl.CostEstimate(
-            flops=4 * count * D * hf, bytes_accessed=4 * D * hf + 2 * count * D, transcendentals=0
-        ),
-        name="expert_down",
-    )(flag, act, own, crossed, near, far)
 
 
 def local(
@@ -360,15 +354,14 @@
     )
     combine = jnp.where(dispatch, spread[:, None, :], 0.0).astype(jnp.bfloat16)
 
-    act = expert_act(
+    produced = expert_ffn(
         flag,
         incoming.reshape(chips * slots, D),
-        (gate_slab, up_slab),
-        (gate_crossed, up_crossed),
-        (gate_near, up_near),
-        (gate_far, up_far),
-    )
-    produced = expert_down(flag, act, down_slab, down_crossed, down_near, down_far)
+        (gate_slab, up_slab, down_slab),
+        (gate_crossed, up_crossed, down_crossed),
+        (gate_near, up_near, down_near),
+        (gate_far, up_far, down_far),
+    )
     returned = lax.all_to_all(
         produced.reshape(chips, slots, D), "chip", split_axis=0, concat_axis=0, tiled=True
     )

time: 253 us -> 249 us (0.984)
  Pallas kernels: 25.5 us -> 20.6 us
    pallas_call x2 -> x1, Pallas kernels: 16 us -> 11.1 us  [expert_ffn(): pl.pallas_call(ffn_kernel, out_shape=jax.ShapeDtypeStruct((count, D), jnp...]
  transfers between devices with their start and end apart: 22 -> 22, of which waited for: 13 -> 14; matrix products, arithmetic and copies ran while one was open for 2% -> 2% of each run, Pallas kernels for 8% -> 4%
where the time goes in v5:
time: 249 us; the launch traced here: 248 us
  waiting for transfers between devices  120 us (48%)
  starting transfers between devices  80.5 us (32%)
  Pallas kernels  20.6 us (8%)
  blocking collectives  15.3 us (6%)
  matrix products  8.33 us (3%)
    ppermute x9, waiting for transfers between devices, moved(): return lax.ppermute(slab, ('core', 'dp'), pairs)  56.4 us
    all_to_all x1, waiting for transfers between devices, local(): lax.all_to_all(outgoing.reshape(chips, slots, D), 'chip', split_axis=0, c...  23.8 us
    ppermute x3, starting transfers between devices, local(): part = lax.ppermute(narrow[m * rows:(m + 1) * rows], ('core', 'dp'), home)  22.8 us
    all_to_all x1, waiting for transfers between devices, local(): lax.all_to_all(produced.reshape(chips, slots, D), 'chip', split_axis=0, c...  21.7 us
    ppermute x6, starting transfers between devices, gathered(): blocks.append(lax.ppermute(blocks[-1], ('core', 'dp'), ring))  21.6 us
    ppermute x9, starting transfers between devices, moved(): return lax.ppermute(slab, ('core', 'dp'), pairs)  19 us
    all_to_all x1, blocking collectives, local(): lax.all_to_all(sent, 'chip', split_axis=0, concat_axis=0, tiled=True)  15.3 us
    pallas_call x1, Pallas kernels, expert_ffn(): pl.pallas_call(ffn_kernel, out_shape=jax.ShapeDtypeStruct((count, D), jnp...  11.1 us
  transfers between devices with their start and end apart: 22, of which 14 were waited for; matrix products, arithmetic and copies ran while one was open for 2% of the time, Pallas kernels for 4%

profile of v5, /device:TPU:1, one launch (start us, length us, event | category | flops | bytes accessed | tf_op | source)
XLA Modules:
  0.0 247.5 jit_solution(7029590853295062669)
XLA Ops:
  1.4 9.5 %attention.1 = bf16[16,16,512]{2,1,0:T(8,128)(2,1)} custom-call(s32[1]{0:T(128)} %bitcast.swap, s32[16]{0:T(128)} %lengths.1, bf16[16,8192]{1,0:T(8,128)(2,1)} %q_in.1, bf16[16,512]{1,0:T(8,128)(2,1)} %nk_in.1, bf16[16,512]{1,0:T(8,128)(2,1)} %nv_in.1, bf16[16,128,512]{2,1,0:T(8,128)(2,1)} %keys.1, bf16[16,128,512]{2,1,0:T(8,128)(2,1)} %values.1), custom_call_target="tpu_custom_call" | custom-call | flops 134217728 | bytes 4194304 | tf_op jit(solution)/shard_map/attention/pallas_call | solution.py:106
  10.9 15.3 %all_to_all.20 = bf16[16,16,512]{2,1,0:T(8,128)(2,1)S(1)} all-to-all(bf16[16,16,512]{2,1,0:T(8,128)(2,1)} %attention.1), channel_id=1, replica_groups=mesh['chip'=16,'core'=2,'dp'=4] {'chip'}, dimensions={0} | all-to-all | bytes 524288 | tf_op jit(solution)/shard_map/all_to_all | solution.py:296
  27.0 3.7 %fusion = bf16[256,4096]{1,0:T(8,128)(2,1)} fusion(f32[256,4096]{1,0:T(8,128)S(1)} %fusion.7, bf16[256,4096]{1,0:T(8,128)(2,1)} %collective-permute-done, bf16[256,512]{1,0:T(8,128)(2,1)S(1)} %bitcast.22), kind=kOutput, calls=%fused_computation.1 | convolution fusion | flops 538968064 | bytes 8519680 | tf_op jit(solution)/shard_map/dot_general | solution.py:299
  30.7 3.8 %all-to-all-start.1 = ((bf16[16,16,4096]{2,1,0:T(8,128)(2,1)}), bf16[16,16,4096]{2,1,0:T(8,128)(2,1)S(1)}, u32[]{:S(2)}, u32[]{:S(2)}) async-start(bf16[16,16,4096]{2,1,0:T(8,128)(2,1)} %bitcast.20), calls=%async_computation.1 | async-start | bytes 4194304 | tf_op jit(solution)/shard_map/all_to_all | solution.py:320
  34.6 5.3 %collective-permute-start.7 = (bf16[1,4096,384]{2,1,0:T(8,128)(2,1)}, bf16[1,4096,384]{2,1,0:T(8,128)(2,1)}, u32[]{:S(2)}, u32[]{:S(2)}) collective-permute-start(bf16[1,4096,384]{2,1,0:T(8,128)(2,1)} %refs_0_.1), channel_id=1, source_target_pairs={{1,0},{3,2},{4,5},{6,7},{9,8},{11,10},{12,13},{14,15},{17,16},{19,... | collective-permute-start | bytes 9437192 | tf_op jit(solution)/shard_map/ppermute | solution.py:267
  39.9 3.0 %collective-permute-start.8 = (bf16[1,4096,384]{2,1,0:T(8,128)(2,1)}, bf16[1,4096,384]{2,1,0:T(8,128)(2,1)}, u32[]{:S(2)}, u32[]{:S(2)}) collective-permute-start(bf16[1,4096,384]{2,1,0:T(8,128)(2,1)} %refs_1_.1), channel_id=1, source_target_pairs={{1,0},{3,2},{4,5},{6,7},{9,8},{11,10},{12,13},{14,15},{17,16},{19,... | collective-permute-start | bytes 9437192 | tf_op jit(solution)/shard_map/ppermute | solution.py:267
  42.9 3.0 %collective-permute-start.9 = (bf16[1,384,4096]{2,1,0:T(8,128)(2,1)}, bf16[1,384,4096]{2,1,0:T(8,128)(2,1)}, u32[]{:S(2)}, u32[]{:S(2)}) collective-permute-start(bf16[1,384,4096]{2,1,0:T(8,128)(2,1)} %refs_2_.1), channel_id=1, source_target_pairs={{1,0},{3,2},{4,5},{6,7},{9,8},{11,10},{12,13},{14,15},{17,16},{19,... | collective-permute-start | bytes 9437192 | tf_op jit(solution)/shard_map/ppermute | solution.py:267
  47.2 6.0 %collective-permute-start.1 = (s32[16,8]{0,1:T(8,128)S(1)}, s32[16,8]{0,1:T(8,128)S(1)}, u32[]{:S(2)}, u32[]{:S(2)}) collective-permute-start(s32[16,8]{0,1:T(8,128)S(1)} %copy-done.5), channel_id=1, source_target_pairs={{0,1},{1,2},{2,3},{3,0},{4,7},{5,4},{6,5},{7,6},{8,9},{9,10},{10,1... | collective-permute-start | bytes 1544 | tf_op jit(solution)/shard_map/ppermute | solution.py:279
  53.9 3.2 %collective-permute-start.2 = (s32[16,8]{0,1:T(8,128)S(1)}, s32[16,8]{0,1:T(8,128)S(1)}, u32[]{:S(2)}, u32[]{:S(2)}) collective-permute-start(s32[16,8]{0,1:T(8,128)S(1)} %collective-permute-done.1), channel_id=1, source_target_pairs={{0,1},{1,2},{2,3},{3,0},{4,7},{5,4},{6,5},{7,6},{8,9},{9,10},{10,1... | collective-permute-start | bytes 1544 | tf_op jit(solution)/shard_map/ppermute | solution.py:279
  57.9 3.2 %collective-permute-start.3 = (s32[16,8]{0,1:T(8,128)S(1)}, s32[16,8]{0,1:T(8,128)S(1)}, u32[]{:S(2)}, u32[]{:S(2)}) collective-permute-start(s32[16,8]{0,1:T(8,128)S(1)} %collective-permute-done.2), channel_id=1, source_target_pairs={{0,1},{1,2},{2,3},{3,0},{4,7},{5,4},{6,5},{7,6},{8,9},{9,10},{10,1... | collective-permute-start | bytes 1544 | tf_op jit(solution)/shard_map/ppermute | solution.py:279
  65.2 3.8 %collective-permute-start.4 = (bf16[16,4096]{1,0:T(8,128)(2,1)S(1)}, bf16[16,4096]{1,0:T(8,128)(2,1)S(1)}, u32[]{:S(2)}, u32[]{:S(2)}) collective-permute-start(bf16[16,4096]{1,0:T(8,128)(2,1)S(1)} %multiply_convert_fusion), channel_id=1, source_target_pairs={{0,1},{1,2},{2,3},{3,0},{4,7},{5,4},{6,5},{7,6},{8,9},{9,10},{10,1... | collective-permute-start | bytes 393224 | tf_op jit(solution)/shard_map/ppermute | solution.py:279
  71.1 3.0 %collective-permute-start.5 = (bf16[16,4096]{1,0:T(8,128)(2,1)S(1)}, bf16[16,4096]{1,0:T(8,128)(2,1)S(1)}, u32[]{:S(2)}, u32[]{:S(2)}) collective-permute-start(bf16[16,4096]{1,0:T(8,128)(2,1)S(1)} %collective-permute-done.4), channel_id=1, source_target_pairs={{0,1},{1,2},{2,3},{3,0},{4,7},{5,4},{6,5},{7,6},{8,9},{9,10},{10,1... | collective-permute-start | bytes 393224 | tf_op jit(solution)/shard_map/ppermute | solution.py:279
  74.1 2.6 %collective-permute-done.5 = bf16[16,4096]{1,0:T(8,128)(2,1)S(1)} collective-permute-done((bf16[16,4096]{1,0:T(8,128)(2,1)S(1)}, bf16[16,4096]{1,0:T(8,128)(2,1)S(1)}, u32[]{:S(2)}, u32[]{:S(2)}) %collective-permute-start.5) | collective-permute-done | bytes 131104 | tf_op jit(solution)/shard_map/ppermute | solution.py:279
  79.1 3.2 %collective-permute-done.6 = bf16[16,4096]{1,0:T(8,128)(2,1)S(1)} collective-permute-done((bf16[16,4096]{1,0:T(8,128)(2,1)S(1)}, bf16[16,4096]{1,0:T(8,128)(2,1)S(1)}, u32[]{:S(2)}, u32[]{:S(2)}) %collective-permute-start.6) | collective-permute-done | bytes 131104 | tf_op jit(solution)/shard_map/ppermute | solution.py:279
  86.9 23.9 %collective-permute-done.8.refs_4_ = bf16[1,4096,384]{2,1,0:T(8,128)(2,1)} collective-permute-done((bf16[1,4096,384]{2,1,0:T(8,128)(2,1)}, bf16[1,4096,384]{2,1,0:T(8,128)(2,1)}, u32[]{:S(2)}, u32[]{:S(2)}) %collective-permute-start.8) | collective-permute-done | bytes 3145760 | tf_op jit(solution)/shard_map/ppermute | solution.py:267
  112.1 32.4 %collective-permute-done.9.refs_5_ = bf16[1,384,4096]{2,1,0:T(8,128)(2,1)} collective-permute-done((bf16[1,384,4096]{2,1,0:T(8,128)(2,1)}, bf16[1,384,4096]{2,1,0:T(8,128)(2,1)}, u32[]{:S(2)}, u32[]{:S(2)}) %collective-permute-start.9) | collective-permute-done | bytes 3145760 | tf_op jit(solution)/shard_map/ppermute | solution.py:267
  147.2 6.7 %all-to-all-start.2 = ((bf16[16,16,4096]{2,1,0:T(8,128)(2,1)}), bf16[16,16,4096]{2,1,0:T(8,128)(2,1)}, u32[]{:S(2)}, u32[]{:S(2)}) async-start(bf16[16,16,4096]{2,1,0:T(8,128)(2,1)} %bitcast.7), calls=%async_computation.2 | async-start | bytes 4194304 | tf_op jit(solution)/shard_map/all_to_all | solution.py:341
  153.8 23.8 %all-to-all-done.2 = bf16[16,16,4096]{2,1,0:T(8,128)(2,1)} async-done(((bf16[16,16,4096]{2,1,0:T(8,128)(2,1)}), bf16[16,16,4096]{2,1,0:T(8,128)(2,1)}, u32[]{:S(2)}, u32[]{:S(2)}) %all-to-all-start.2) | async-done | bytes 2097184 | tf_op jit(solution)/shard_map/all_to_all | solution.py:341
  177.6 11.1 %expert_ffn.1 = bf16[256,4096]{1,0:T(8,128)(2,1)} custom-call(s32[1]{0:T(128)} %bitcast.5.flag, bf16[256,4096]{1,0:T(8,128)(2,1)} %bitcast.8.rows_in, bf16[1,4096,384]{2,1,0:T(8,128)(2,1)} %refs_0_.1, bf16[1,4096,384]{2,1,0:T(8,128)(2,1)} %refs_1_.1, bf16[1,384,4096]{2,1,0:T(8,128)(2,1)} %refs_2_.1, bf16[1,4096,384]{2,1,0:T(8,128)(2,1)} %collective-permute-done.7.refs_3_, ...), custom_call_target="tpu_custom_call" | custom-call | flops 4831838208 | bytes 23068672 | tf_op jit(solution)/shard_map/expert_ffn/pallas_call | solution.py:213
  188.7 5.2 %all-to-all-start.3 = ((bf16[16,16,4096]{2,1,0:T(8,128)(2,1)}), bf16[16,16,4096]{2,1,0:T(8,128)(2,1)S(1)}, u32[]{:S(2)}, u32[]{:S(2)}) async-start(bf16[16,16,4096]{2,1,0:T(8,128)(2,1)} %bitcast.19), calls=%async_computation.3 | async-start | bytes 4194304 | tf_op jit(solution)/shard_map/all_to_all | solution.py:365
  195.7 21.7 %all-to-all-done.3 = bf16[16,16,4096]{2,1,0:T(8,128)(2,1)S(1)} async-done(((bf16[16,16,4096]{2,1,0:T(8,128)(2,1)}), bf16[16,16,4096]{2,1,0:T(8,128)(2,1)S(1)}, u32[]{:S(2)}, u32[]{:S(2)}) %all-to-all-start.3) | async-done | bytes 2097184 | tf_op jit(solution)/shard_map/all_to_all | solution.py:365
  218.0 19.2 %collective-permute-start.16 = (bf16[16,4096]{1,0:T(8,128)(2,1)S(1)}, bf16[16,4096]{1,0:T(8,128)(2,1)S(1)}, u32[]{:S(2)}, u32[]{:S(2)}) collective-permute-start(bf16[16,4096]{1,0:T(8,128)(2,1)S(1)} %get-tuple-element.19), channel_id=1, source_target_pairs={{0,3},{1,0},{2,1},{3,2},{4,5},{5,6},{6,7},{7,4},{8,11},{9,8},{10,9... | collective-permute-start | bytes 393224 | tf_op jit(solution)/shard_map/ppermute | solution.py:378
  237.2 2.5 %collective-permute-start.18 = (bf16[16,4096]{1,0:T(8,128)(2,1)S(1)}, bf16[16,4096]{1,0:T(8,128)(2,1)S(1)}, u32[]{:S(2)}, u32[]{:S(2)}) collective-permute-start(bf16[16,4096]{1,0:T(8,128)(2,1)S(1)} %get-tuple-element.20), channel_id=1, source_target_pairs={{0,1},{1,2},{2,3},{3,0},{4,7},{5,4},{6,5},{7,6},{8,9},{9,10},{10,1... | collective-permute-start | bytes 393224 | tf_op jit(solution)/shard_map/ppermute | solution.py:378
  242.1 4.6 %collective-permute-done.17 = bf16[16,4096]{1,0:T(8,128)(2,1)S(1)} collective-permute-done((bf16[16,4096]{1,0:T(8,128)(2,1)S(1)}, bf16[16,4096]{1,0:T(8,128)(2,1)S(1)}, u32[]{:S(2)}, u32[]{:S(2)}) %collective-permute-start.17) | collective-permute-done | bytes 131104 | tf_op jit(solution)/shard_map/ppermute | solution.py:378
  (59 shorter events, 27.4 us)
Async XLA Ops:
  0.0 194.0 %copy-start = (bf16[4096,64]{0,1:T(8,128)(2,1)S(1)}, bf16[4096,64]{0,1:T(8,128)(2,1)}, u32[]{:S(2)}) copy-start(bf16[4096,64]{0,1:T(8,128)(2,1)} %param.23) | copy-start | bytes 1572868
  0.0 27.0 %collective-permute-start = (bf16[256,4096]{1,0:T(8,128)(2,1)}, bf16[256,4096]{1,0:T(8,128)(2,1)}, u32[]{:S(2)}, u32[]{:S(2)}) collective-permute-start(bf16[256,4096]{1,0:T(8,128)(2,1)} %param.21), channel_id=1, source_target_pairs={{0,4},{4,0},{1,5},{5,1},{2,6},{6,2},{3,7},{7,3},{8,12},{12,8},{9,1... | collective-permute-start | bytes 6291464 | tf_op jit(solution)/shard_map/ppermute | solution.py:28
  30.7 33.9 %all-to-all-start.1 = ((bf16[16,16,4096]{2,1,0:T(8,128)(2,1)}), bf16[16,16,4096]{2,1,0:T(8,128)(2,1)S(1)}, u32[]{:S(2)}, u32[]{:S(2)}) async-start(bf16[16,16,4096]{2,1,0:T(8,128)(2,1)} %bitcast.20), calls=%async_computation.1 | async-start | bytes 4194304 | tf_op jit(solution)/shard_map/all_to_all | solution.py:320
  34.6 30.5 %copy-start.4 = (f32[4096]{0:T(1024)S(1)}, f32[4096]{0:T(1024)}, u32[]{:S(2)}) copy-start(f32[4096]{0:T(1024)} %param.22) | copy-start | bytes 49156
  34.6 51.0 %collective-permute-start.7 = (bf16[1,4096,384]{2,1,0:T(8,128)(2,1)}, bf16[1,4096,384]{2,1,0:T(8,128)(2,1)}, u32[]{:S(2)}, u32[]{:S(2)}) collective-permute-start(bf16[1,4096,384]{2,1,0:T(8,128)(2,1)} %refs_0_.1), channel_id=1, source_target_pairs={{1,0},{3,2},{4,5},{6,7},{9,8},{11,10},{12,13},{14,15},{17,16},{19,... | collective-permute-start | bytes 9437192 | tf_op jit(solution)/shard_map/ppermute | solution.py:267
  39.9 70.9 %collective-permute-start.8 = (bf16[1,4096,384]{2,1,0:T(8,128)(2,1)}, bf16[1,4096,384]{2,1,0:T(8,128)(2,1)}, u32[]{:S(2)}, u32[]{:S(2)}) collective-permute-start(bf16[1,4096,384]{2,1,0:T(8,128)(2,1)} %refs_1_.1), channel_id=1, source_target_pairs={{1,0},{3,2},{4,5},{6,7},{9,8},{11,10},{12,13},{14,15},{17,16},{19,... | collective-permute-start | bytes 9437192 | tf_op jit(solution)/shard_map/ppermute | solution.py:267
  42.9 101.7 %collective-permute-start.9 = (bf16[1,384,4096]{2,1,0:T(8,128)(2,1)}, bf16[1,384,4096]{2,1,0:T(8,128)(2,1)}, u32[]{:S(2)}, u32[]{:S(2)}) collective-permute-start(bf16[1,384,4096]{2,1,0:T(8,128)(2,1)} %refs_2_.1), channel_id=1, source_target_pairs={{1,0},{3,2},{4,5},{6,7},{9,8},{11,10},{12,13},{14,15},{17,16},{19,... | collective-permute-start | bytes 9437192 | tf_op jit(solution)/shard_map/ppermute | solution.py:267
  45.9 100.0 %collective-permute-start.10 = (bf16[1,4096,384]{2,1,0:T(8,128)(2,1)}, bf16[1,4096,384]{2,1,0:T(8,128)(2,1)}, u32[]{:S(2)}, u32[]{:S(2)}) collective-permute-start(bf16[1,4096,384]{2,1,0:T(8,128)(2,1)} %refs_0_.1), channel_id=1, source_target_pairs={{0,4},{2,6},{5,1},{7,3},{8,12},{10,14},{13,9},{15,11},{16,20},{18,... | collective-permute-start | bytes 9437192 | tf_op jit(solution)/shard_map/ppermute | solution.py:267
  47.2 6.7 %collective-permute-start.1 = (s32[16,8]{0,1:T(8,128)S(1)}, s32[16,8]{0,1:T(8,128)S(1)}, u32[]{:S(2)}, u32[]{:S(2)}) collective-permute-start(s32[16,8]{0,1:T(8,128)S(1)} %copy-done.5), channel_id=1, source_target_pairs={{0,1},{1,2},{2,3},{3,0},{4,7},{5,4},{6,5},{7,6},{8,9},{9,10},{10,1... | collective-permute-start | bytes 1544 | tf_op jit(solution)/shard_map/ppermute | solution.py:279
  53.9 4.0 %collective-permute-start.2 = (s32[16,8]{0,1:T(8,128)S(1)}, s32[16,8]{0,1:T(8,128)S(1)}, u32[]{:S(2)}, u32[]{:S(2)}) collective-permute-start(s32[16,8]{0,1:T(8,128)S(1)} %collective-permute-done.1), channel_id=1, source_target_pairs={{0,1},{1,2},{2,3},{3,0},{4,7},{5,4},{6,5},{7,6},{8,9},{9,10},{10,1... | collective-permute-start | bytes 1544 | tf_op jit(solution)/shard_map/ppermute | solution.py:279
  57.9 4.0 %collective-permute-start.3 = (s32[16,8]{0,1:T(8,128)S(1)}, s32[16,8]{0,1:T(8,128)S(1)}, u32[]{:S(2)}, u32[]{:S(2)}) collective-permute-start(s32[16,8]{0,1:T(8,128)S(1)} %collective-permute-done.2), channel_id=1, source_target_pairs={{0,1},{1,2},{2,3},{3,0},{4,7},{5,4},{6,5},{7,6},{8,9},{9,10},{10,1... | collective-permute-start | bytes 1544 | tf_op jit(solution)/shard_map/ppermute | solution.py:279
  65.2 5.9 %collective-permute-start.4 = (bf16[16,4096]{1,0:T(8,128)(2,1)S(1)}, bf16[16,4096]{1,0:T(8,128)(2,1)S(1)}, u32[]{:S(2)}, u32[]{:S(2)}) collective-permute-start(bf16[16,4096]{1,0:T(8,128)(2,1)S(1)} %multiply_convert_fusion), channel_id=1, source_target_pairs={{0,1},{1,2},{2,3},{3,0},{4,7},{5,4},{6,5},{7,6},{8,9},{9,10},{10,1... | collective-permute-start | bytes 393224 | tf_op jit(solution)/shard_map/ppermute | solution.py:279
  71.1 5.6 %collective-permute-start.5 = (bf16[16,4096]{1,0:T(8,128)(2,1)S(1)}, bf16[16,4096]{1,0:T(8,128)(2,1)S(1)}, u32[]{:S(2)}, u32[]{:S(2)}) collective-permute-start(bf16[16,4096]{1,0:T(8,128)(2,1)S(1)} %collective-permute-done.4), channel_id=1, source_target_pairs={{0,1},{1,2},{2,3},{3,0},{4,7},{5,4},{6,5},{7,6},{8,9},{9,10},{10,1... | collective-permute-start | bytes 393224 | tf_op jit(solution)/shard_map/ppermute | solution.py:279
  76.7 5.6 %collective-permute-start.6 = (bf16[16,4096]{1,0:T(8,128)(2,1)S(1)}, bf16[16,4096]{1,0:T(8,128)(2,1)S(1)}, u32[]{:S(2)}, u32[]{:S(2)}) collective-permute-start(bf16[16,4096]{1,0:T(8,128)(2,1)S(1)} %collective-permute-done.5), channel_id=1, source_target_pairs={{0,1},{1,2},{2,3},{3,0},{4,7},{5,4},{6,5},{7,6},{8,9},{9,10},{10,1... | collective-permute-start | bytes 393224 | tf_op jit(solution)/shard_map/ppermute | solution.py:279
  82.3 71.5 %collective-permute-start.11 = (bf16[1,4096,384]{2,1,0:T(8,128)(2,1)}, bf16[1,4096,384]{2,1,0:T(8,128)(2,1)}, u32[]{:S(2)}, u32[]{:S(2)}) collective-permute-start(bf16[1,4096,384]{2,1,0:T(8,128)(2,1)} %refs_1_.1), channel_id=1, source_target_pairs={{0,4},{2,6},{5,1},{7,3},{8,12},{10,14},{13,9},{15,11},{16,20},{18,... | collective-permute-start | bytes 9437192 | tf_op jit(solution)/shard_map/ppermute | solution.py:267
  85.6 68.2 %collective-permute-start.12 = (bf16[1,384,4096]{2,1,0:T(8,128)(2,1)}, bf16[1,384,4096]{2,1,0:T(8,128)(2,1)}, u32[]{:S(2)}, u32[]{:S(2)}) collective-permute-start(bf16[1,384,4096]{2,1,0:T(8,128)(2,1)} %refs_2_.1), channel_id=1, source_target_pairs={{0,4},{2,6},{5,1},{7,3},{8,12},{10,14},{13,9},{15,11},{16,20},{18,... | collective-permute-start | bytes 9437192 | tf_op jit(solution)/shard_map/ppermute | solution.py:267
  110.8 66.8 %collective-permute-start.13 = (bf16[1,4096,384]{2,1,0:T(8,128)(2,1)}, bf16[1,4096,384]{2,1,0:T(8,128)(2,1)}, u32[]{:S(2)}, u32[]{:S(2)}) collective-permute-start(bf16[1,4096,384]{2,1,0:T(8,128)(2,1)} %collective-permute-done.7.refs_3_), channel_id=1, source_target_pairs={{0,4},{2,6},{5,1},{7,3},{8,12},{10,14},{13,9},{15,11},{16,20},{18,... | collective-permute-start | bytes 9437192 | tf_op jit(solution)/shard_map/ppermute | solution.py:267
  144.6 33.1 %collective-permute-start.14 = (bf16[1,4096,384]{2,1,0:T(8,128)(2,1)}, bf16[1,4096,384]{2,1,0:T(8,128)(2,1)}, u32[]{:S(2)}, u32[]{:S(2)}) collective-permute-start(bf16[1,4096,384]{2,1,0:T(8,128)(2,1)} %collective-permute-done.8.refs_4_), channel_id=1, source_target_pairs={{0,4},{2,6},{5,1},{7,3},{8,12},{10,14},{13,9},{15,11},{16,20},{18,... | collective-permute-start | bytes 9437192 | tf_op jit(solution)/shard_map/ppermute | solution.py:267
  145.9 31.8 %collective-permute-start.15 = (bf16[1,384,4096]{2,1,0:T(8,128)(2,1)}, bf16[1,384,4096]{2,1,0:T(8,128)(2,1)}, u32[]{:S(2)}, u32[]{:S(2)}) collective-permute-start(bf16[1,384,4096]{2,1,0:T(8,128)(2,1)} %collective-permute-done.9.refs_5_), channel_id=1, source_target_pairs={{0,4},{2,6},{5,1},{7,3},{8,12},{10,14},{13,9},{15,11},{16,20},{18,... | collective-permute-start | bytes 9437192 | tf_op jit(solution)/shard_map/ppermute | solution.py:267
  147.2 30.5 %all-to-all-start.2 = ((bf16[16,16,4096]{2,1,0:T(8,128)(2,1)}), bf16[16,16,4096]{2,1,0:T(8,128)(2,1)}, u32[]{:S(2)}, u32[]{:S(2)}) async-start(bf16[16,16,4096]{2,1,0:T(8,128)(2,1)} %bitcast.7), calls=%async_computation.2 | async-start | bytes 4194304 | tf_op jit(solution)/shard_map/all_to_all | solution.py:341
  188.7 28.7 %all-to-all-start.3 = ((bf16[16,16,4096]{2,1,0:T(8,128)(2,1)}), bf16[16,16,4096]{2,1,0:T(8,128)(2,1)S(1)}, u32[]{:S(2)}, u32[]{:S(2)}) async-start(bf16[16,16,4096]{2,1,0:T(8,128)(2,1)} %bitcast.19), calls=%async_computation.3 | async-start | bytes 4194304 | tf_op jit(solution)/shard_map/all_to_all | solution.py:365
  218.0 24.0 %collective-permute-start.16 = (bf16[16,4096]{1,0:T(8,128)(2,1)S(1)}, bf16[16,4096]{1,0:T(8,128)(2,1)S(1)}, u32[]{:S(2)}, u32[]{:S(2)}) collective-permute-start(bf16[16,4096]{1,0:T(8,128)(2,1)S(1)} %get-tuple-element.19), channel_id=1, source_target_pairs={{0,3},{1,0},{2,1},{3,2},{4,5},{5,6},{6,7},{7,4},{8,11},{9,8},{10,9... | collective-permute-start | bytes 393224 | tf_op jit(solution)/shard_map/ppermute | solution.py:378
  237.2 4.9 %collective-permute-start.18 = (bf16[16,4096]{1,0:T(8,128)(2,1)S(1)}, bf16[16,4096]{1,0:T(8,128)(2,1)S(1)}, u32[]{:S(2)}, u32[]{:S(2)}) collective-permute-start(bf16[16,4096]{1,0:T(8,128)(2,1)S(1)} %get-tuple-element.20), channel_id=1, source_target_pairs={{0,1},{1,2},{2,3},{3,0},{4,7},{5,4},{6,5},{7,6},{8,9},{9,10},{10,1... | collective-permute-start | bytes 393224 | tf_op jit(solution)/shard_map/ppermute | solution.py:378
  239.7 7.0 %collective-permute-start.17 = (bf16[16,4096]{1,0:T(8,128)(2,1)S(1)}, bf16[16,4096]{1,0:T(8,128)(2,1)S(1)}, u32[]{:S(2)}, u32[]{:S(2)}) collective-permute-start(bf16[16,4096]{1,0:T(8,128)(2,1)S(1)} %get-tuple-element.21), channel_id=1, source_target_pairs={{0,2},{1,3},{2,0},{3,1},{4,6},{5,7},{6,4},{7,5},{8,10},{9,11},{10,... | collective-permute-start | bytes 393224 | tf_op jit(solution)/shard_map/ppermute | solution.py:378
  (4 other events, 73.0 us)

commit v6 on v5

--- a/solution.py
+++ b/solution.py
@@ -17,6 +17,7 @@
 OUT_STEPS = 2
 CUTS = 8
 X_CUTS = 4
+COMBINE_STEPS = 4
 
 
 EP = ("chip", "core")
@@ -193,12 +194,14 @@
         columns = slice(step * wide, (step + 1) * wide)
         for side in range(2):
             down_copy(side, own, step).wait()
-        y_buf[:, columns] = jnp.dot(
-            act, down_buf[:, columns], preferred_element_type=jnp.float32
-        ).astype(jnp.bfloat16)
+        rows_out = jnp.dot(act, down_buf[:, columns], preferred_element_type=jnp.float32)
+        for chunk in range(out.shape[0]):
+            y_buf[chunk, :, columns] = rows_out[chunk * CAP : (chunk + 1) * CAP].astype(
+                jnp.bfloat16
+            )
         copy = pltpu.make_async_copy(
-            y_buf.at[:, pl.ds(step * wide, wide)],
-            out.at[:, pl.ds(step * wide, wide)],
+            y_buf.at[:, :, pl.ds(step * wide, wide)],
+            out.at[:, :, pl.ds(step * wide, wide)],
             y_sem.at[step],
         )
         copy.start()
@@ -212,7 +215,7 @@
     hf = own[0].shape[2]
     return pl.pallas_call(
         ffn_kernel,
-        out_shape=jax.ShapeDtypeStruct((count, D), jnp.bfloat16),
+        out_shape=jax.ShapeDtypeStruct((count // CAP, CAP, D), jnp.bfloat16),
         in_specs=[pl.BlockSpec(memory_space=pltpu.SMEM)]
         + [pl.BlockSpec(memory_space=pltpu.HBM)] * 13,
         out_specs=pl.BlockSpec(memory_space=pltpu.HBM),
@@ -220,7 +223,7 @@
             pltpu.VMEM((count, D), jnp.bfloat16),
             pltpu.VMEM((4, D, hf), jnp.bfloat16),
             pltpu.VMEM((2 * hf, D), jnp.bfloat16),
-            pltpu.VMEM((count, D), jnp.bfloat16),
+            pltpu.VMEM((count // CAP, CAP, D), jnp.bfloat16),
             pltpu.SemaphoreType.DMA((X_CUTS,)),
             pltpu.SemaphoreType.DMA((4, CUTS)),
             pltpu.SemaphoreType.DMA((2, OUT_STEPS)),
@@ -232,6 +235,35 @@
         ),
         name="expert_ffn",
     )(flag, rows_in, *own, *crossed, *near, *far)
+
+
+def combine_kernel(weights, rows_in, hidden, out):
+    flat = jnp.concatenate([rows_in[chunk] for chunk in range(rows_in.shape[0])], axis=0)
+    out[...] = hidden[...] + jnp.dot(weights[...], flat, preferred_element_type=jnp.float32)
+
+
+def combined(weights, rows_in, hidden):
+    chunks, each, _ = rows_in.shape
+    rows = hidden.shape[0]
+    wide = D // COMBINE_STEPS
+    return pl.pallas_call(
+        combine_kernel,
+        grid=(COMBINE_STEPS,),
+        out_shape=jax.ShapeDtypeStruct((rows, D), jnp.float32),
+        in_specs=[
+            pl.BlockSpec((rows, chunks * each), lambda i: (0, 0)),
+            pl.BlockSpec((chunks, each, wide), lambda i: (0, 0, i)),
+            pl.BlockSpec((rows, wide), lambda i: (0, i)),
+        ],
+        out_specs=pl.BlockSpec((rows, wide), lambda i: (0, i)),
+        compiler_params=pltpu.CompilerParams(
+            dimension_semantics=("arbitrary",), vmem_limit_bytes=123 * 512 * 1024
+        ),
+        cost_estimate=pl.CostEstimate(
+            flops=2 * rows * chunks * each * D, bytes_accessed=2 * chunks * each * D, transcendentals=0
+        ),
+        name="combined",
+    )(weights, rows_in, hidden)
 
 
 def local(
@@ -310,9 +342,23 @@
         before.astype(jnp.bfloat16),
         preferred_element_type=jnp.float32,
     ).astype(jnp.int32)
-    place = jnp.where(member, rank + CAP * (at // rows)[None, :], -1)
+    source = (depth + depths + (2 * core - 1) * (at // rows)) % depths
+    place = jnp.where(member, rank + CAP * source[None, :], -1)
     slots = CAP * depths
     dispatch = place[:, None, :] == jnp.arange(slots, dtype=jnp.int32)[None, :, None]
+
+    chunk = jnp.arange(chips * depths, dtype=jnp.int32)
+    homes = 4 * (chunk // depths) + 2 * (chunk % 2) + (chunk % depths) // 2
+    own_hits = expert_ids[:, :, None] == homes[None, None, :]
+    own_member = jnp.any(own_hits, axis=1)
+    turn = jnp.arange(rows, dtype=jnp.int32)
+    own_rank = jnp.dot(
+        (turn[None, :] < turn[:, None]).astype(jnp.bfloat16),
+        own_member.astype(jnp.bfloat16),
+        preferred_element_type=jnp.float32,
+    ).astype(jnp.int32)
+    own_rank = jnp.where(own_member, own_rank, -1)
+    own_slots = own_rank[:, :, None] == jnp.arange(CAP, dtype=jnp.int32)[None, None, :]
 
     partial = partial.astype(jnp.bfloat16)
     up_crossed = moved(up_slab, across, partial)
@@ -324,7 +370,7 @@
         concat_axis=0,
         tiled=True,
     )
-    partial, dispatch = lax.optimization_barrier((partial, dispatch))
+    partial, dispatch, own_slots = lax.optimization_barrier((partial, dispatch, own_slots))
     hidden = resid.astype(jnp.float32) + jnp.sum(partial.astype(jnp.float32), axis=0)
     meansq = jnp.mean(hidden * hidden, axis=1, keepdims=True)
     normed = (hidden * lax.rsqrt(jnp.maximum(meansq, 0.25)) * norm_gain).astype(jnp.bfloat16)
@@ -342,17 +388,15 @@
         outgoing.reshape(chips, slots, D), "chip", split_axis=0, concat_axis=0, tiled=True
     )
 
-    logits = jnp.dot(tokens, router, preferred_element_type=jnp.float32)
+    logits = jnp.dot(normed, router, preferred_element_type=jnp.float32)
     experts = router.shape[1]
-    onehot = ids[:, :, None] == jnp.arange(experts, dtype=jnp.int32)[None, None, :]
+    onehot = expert_ids[:, :, None] == jnp.arange(experts, dtype=jnp.int32)[None, None, :]
     chosen = jnp.sum(jnp.where(onehot, logits[:, None, :], 0.0), axis=2)
     peak_logit = jnp.max(chosen, axis=1, keepdims=True)
     exp_logit = jnp.exp(chosen - peak_logit)
     gate_probs = (exp_logit / jnp.sum(exp_logit, axis=1, keepdims=True)).astype(jnp.bfloat16)
-    spread = jnp.sum(
-        jnp.where(hits, gate_probs.astype(jnp.float32).T[:, None, :], 0.0), axis=0
-    )
-    combine = jnp.where(dispatch, spread[:, None, :], 0.0).astype(jnp.bfloat16)
+    spread = jnp.sum(jnp.where(own_hits, gate_probs.astype(jnp.float32)[:, :, None], 0.0), axis=1)
+    combine = jnp.where(own_slots, spread[:, :, None], 0.0).astype(jnp.bfloat16)
 
     produced = expert_ffn(
         flag,
@@ -362,22 +406,8 @@
         (gate_near, up_near, down_near),
         (gate_far, up_far, down_far),
     )
-    returned = lax.all_to_all(
-        produced.reshape(chips, slots, D), "chip", split_axis=0, concat_axis=0, tiled=True
-    )
-    mix = lax.dot_general(
-        combine.reshape(chips * slots, count),
-        returned.reshape(chips * slots, D),
-        (((0,), (0,)), ((), ())),
-        preferred_element_type=jnp.float32,
-    )
-    total = hidden + mix[:rows]
-    narrow = mix.astype(jnp.bfloat16)
-    for m in range(1, depths):
-        home = [(c * depths + d, c * depths + (d + (2 * c - 1) * m) % depths) for c, d in spots]
-        part = lax.ppermute(narrow[m * rows : (m + 1) * rows], ("core", "dp"), home)
-        total = total + part.astype(jnp.float32)
-    return total
+    returned = lax.all_to_all(produced, ("chip", "dp"), split_axis=0, concat_axis=0, tiled=True)
+    return combined(combine.reshape(rows, chips * depths * CAP), returned, hidden)
 
 
 def solution(mesh):

time: 249 us -> 238 us (0.956)
  starting transfers between devices: 80.5 us -> 62.9 us
  waiting for transfers between devices: 120 us -> 124 us
  Pallas kernels: 20.6 us -> 24.4 us
    ppermute x3 -> x0, starting transfers between devices: 22.8 us -> none  [local(): part = lax.ppermute(narrow[m * rows:(m + 1) * rows], ('core', 'dp'), home)]
    all_to_all x1, starting transfers between devices: 5.19 us -> 15.8 us  [local(): lax.all_to_all(produced, ('chip', 'dp'), split_axis=0, concat_axis=0, til...]
    ppermute x3 -> x0, waiting for transfers between devices: 5.91 us -> none  [local(): part = lax.ppermute(narrow[m * rows:(m + 1) * rows], ('core', 'dp'), home)]
    ppermute x6, starting transfers between devices: 21.6 us -> 16.4 us  [gathered(): blocks.append(lax.ppermute(blocks[-1], ('core', 'dp'), ring))]
    all_to_all x1, waiting for transfers between devices: 21.7 us -> 26.3 us  [local(): lax.all_to_all(produced, ('chip', 'dp'), split_axis=0, concat_axis=0, til...]
    pallas_call x1 -> x2, Pallas kernels: 11.1 us -> 15 us  [the longest x1 11.1 us: expert_ffn(): pl.pallas_call(ffn_kernel, out_shape=jax.ShapeDtypeStruct((count // CAP,...]
  transfers between devices with their start and end apart: 22 -> 19, of which waited for: 14 -> 10; matrix products, arithmetic and copies ran while one was open for 2% -> 2% of each run, Pallas kernels for 4% -> 4%
where the time goes in v6:
time: 238 us; the launch traced here: 236 us
  waiting for transfers between devices  124 us (52%)
  starting transfers between devices  62.9 us (26%)
  Pallas kernels  24.4 us (10%)
  blocking collectives  15.3 us (6%)
  matrix products  7.01 us (3%)
    ppermute x9, waiting for transfers between devices, moved(): return lax.ppermute(slab, ('core', 'dp'), pairs)  56.5 us
    all_to_all x1, waiting for transfers between devices, local(): lax.all_to_all(produced, ('chip', 'dp'), split_axis=0, concat_axis=0, til...  26.3 us
    all_to_all x1, waiting for transfers between devices, local(): lax.all_to_all(outgoing.reshape(chips, slots, D), 'chip', split_axis=0, c...  23.6 us
    ppermute x9, starting transfers between devices, moved(): return lax.ppermute(slab, ('core', 'dp'), pairs)  18.9 us
    ppermute x6, starting transfers between devices, gathered(): blocks.append(lax.ppermute(blocks[-1], ('core', 'dp'), ring))  16.4 us
    all_to_all x1, starting transfers between devices, local(): lax.all_to_all(produced, ('chip', 'dp'), split_axis=0, concat_axis=0, til...  15.8 us
    all_to_all x1, blocking collectives, local(): lax.all_to_all(sent, 'chip', split_axis=0, concat_axis=0, tiled=True)  15.3 us
    ppermute x6, waiting for transfers between devices, gathered(): blocks.append(lax.ppermute(blocks[-1], ('core', 'dp'), ring))  12.6 us
  transfers between devices with their start and end apart: 19, of which 10 were waited for; matrix products, arithmetic and copies ran while one was open for 2% of the time, Pallas kernels for 4%

profile of v6, /device:TPU:1, one launch (start us, length us, event | category | flops | bytes accessed | tf_op | source)
XLA Modules:
  0.0 235.9 jit_solution(8026576423255399272)
XLA Ops:
  1.4 9.4 %attention.1 = bf16[16,16,512]{2,1,0:T(8,128)(2,1)} custom-call(s32[1]{0:T(128)} %bitcast.swap, s32[16]{0:T(128)} %lengths.1, bf16[16,8192]{1,0:T(8,128)(2,1)} %q_in.1, bf16[16,512]{1,0:T(8,128)(2,1)} %nk_in.1, bf16[16,512]{1,0:T(8,128)(2,1)} %nv_in.1, bf16[16,128,512]{2,1,0:T(8,128)(2,1)} %keys.1, bf16[16,128,512]{2,1,0:T(8,128)(2,1)} %values.1), custom_call_target="tpu_custom_call" | custom-call | flops 134217728 | bytes 4194304 | tf_op jit(solution)/shard_map/attention/pallas_call | solution.py:107
  10.8 15.3 %all_to_all.20 = bf16[16,16,512]{2,1,0:T(8,128)(2,1)S(1)} all-to-all(bf16[16,16,512]{2,1,0:T(8,128)(2,1)} %attention.1), channel_id=1, replica_groups=mesh['chip'=16,'core'=2,'dp'=4] {'chip'}, dimensions={0} | all-to-all | bytes 524288 | tf_op jit(solution)/shard_map/all_to_all | solution.py:328
  26.8 3.7 %fusion = bf16[256,4096]{1,0:T(8,128)(2,1)} fusion(f32[256,4096]{1,0:T(8,128)S(1)} %fusion.12, bf16[256,4096]{1,0:T(8,128)(2,1)} %collective-permute-done, bf16[256,512]{1,0:T(8,128)(2,1)S(1)} %bitcast.19), kind=kOutput, calls=%fused_computation.1 | convolution fusion | flops 538968064 | bytes 8519680 | tf_op jit(solution)/shard_map/dot_general | solution.py:331
  30.5 3.8 %all-to-all-start.1 = ((bf16[16,16,4096]{2,1,0:T(8,128)(2,1)}), bf16[16,16,4096]{2,1,0:T(8,128)(2,1)S(1)}, u32[]{:S(2)}, u32[]{:S(2)}) async-start(bf16[16,16,4096]{2,1,0:T(8,128)(2,1)} %bitcast.17), calls=%async_computation.1 | async-start | bytes 4194304 | tf_op jit(solution)/shard_map/all_to_all | solution.py:366
  34.4 5.2 %collective-permute-start.7 = (bf16[1,4096,384]{2,1,0:T(8,128)(2,1)}, bf16[1,4096,384]{2,1,0:T(8,128)(2,1)}, u32[]{:S(2)}, u32[]{:S(2)}) collective-permute-start(bf16[1,4096,384]{2,1,0:T(8,128)(2,1)} %refs_0_.1), channel_id=1, source_target_pairs={{1,0},{3,2},{4,5},{6,7},{9,8},{11,10},{12,13},{14,15},{17,16},{19,... | collective-permute-start | bytes 9437192 | tf_op jit(solution)/shard_map/ppermute | solution.py:299
  40.9 6.0 %collective-permute-start.1 = (s32[16,8]{0,1:T(8,128)S(1)}, s32[16,8]{0,1:T(8,128)S(1)}, u32[]{:S(2)}, u32[]{:S(2)}) collective-permute-start(s32[16,8]{0,1:T(8,128)S(1)} %copy-done.5), channel_id=1, source_target_pairs={{0,1},{1,2},{2,3},{3,0},{4,7},{5,4},{6,5},{7,6},{8,9},{9,10},{10,1... | collective-permute-start | bytes 1544 | tf_op jit(solution)/shard_map/ppermute | solution.py:311
  47.4 3.0 %collective-permute-start.8 = (bf16[1,4096,384]{2,1,0:T(8,128)(2,1)}, bf16[1,4096,384]{2,1,0:T(8,128)(2,1)}, u32[]{:S(2)}, u32[]{:S(2)}) collective-permute-start(bf16[1,4096,384]{2,1,0:T(8,128)(2,1)} %refs_1_.1), channel_id=1, source_target_pairs={{1,0},{3,2},{4,5},{6,7},{9,8},{11,10},{12,13},{14,15},{17,16},{19,... | collective-permute-start | bytes 9437192 | tf_op jit(solution)/shard_map/ppermute | solution.py:299
  50.4 3.0 %collective-permute-start.9 = (bf16[1,384,4096]{2,1,0:T(8,128)(2,1)}, bf16[1,384,4096]{2,1,0:T(8,128)(2,1)}, u32[]{:S(2)}, u32[]{:S(2)}) collective-permute-start(bf16[1,384,4096]{2,1,0:T(8,128)(2,1)} %refs_2_.1), channel_id=1, source_target_pairs={{1,0},{3,2},{4,5},{6,7},{9,8},{11,10},{12,13},{14,15},{17,16},{19,... | collective-permute-start | bytes 9437192 | tf_op jit(solution)/shard_map/ppermute | solution.py:299
  53.5 2.9 %collective-permute-done.2 = s32[16,8]{0,1:T(8,128)S(1)} collective-permute-done((s32[16,8]{0,1:T(8,128)S(1)}, s32[16,8]{0,1:T(8,128)S(1)}, u32[]{:S(2)}, u32[]{:S(2)}) %collective-permute-start.2) | collective-permute-done | bytes 544 | tf_op jit(solution)/shard_map/ppermute | solution.py:311
  59.7 4.5 %all-to-all-done.1 = bf16[16,16,4096]{2,1,0:T(8,128)(2,1)S(1)} async-done(((bf16[16,16,4096]{2,1,0:T(8,128)(2,1)}), bf16[16,16,4096]{2,1,0:T(8,128)(2,1)S(1)}, u32[]{:S(2)}, u32[]{:S(2)}) %all-to-all-start.1) | async-done | bytes 2097184 | tf_op jit(solution)/shard_map/all_to_all | solution.py:366
  64.8 3.8 %collective-permute-start.4 = (bf16[16,4096]{1,0:T(8,128)(2,1)S(1)}, bf16[16,4096]{1,0:T(8,128)(2,1)S(1)}, u32[]{:S(2)}, u32[]{:S(2)}) collective-permute-start(bf16[16,4096]{1,0:T(8,128)(2,1)S(1)} %multiply_convert_fusion), channel_id=1, source_target_pairs={{0,1},{1,2},{2,3},{3,0},{4,7},{5,4},{6,5},{7,6},{8,9},{9,10},{10,1... | collective-permute-start | bytes 393224 | tf_op jit(solution)/shard_map/ppermute | solution.py:311
  68.6 2.0 collective-permute-done.4
  70.7 3.0 %collective-permute-start.5 = (bf16[16,4096]{1,0:T(8,128)(2,1)S(1)}, bf16[16,4096]{1,0:T(8,128)(2,1)S(1)}, u32[]{:S(2)}, u32[]{:S(2)}) collective-permute-start(bf16[16,4096]{1,0:T(8,128)(2,1)S(1)} %collective-permute-done.4), channel_id=1, source_target_pairs={{0,1},{1,2},{2,3},{3,0},{4,7},{5,4},{6,5},{7,6},{8,9},{9,10},{10,1... | collective-permute-start | bytes 393224 | tf_op jit(solution)/shard_map/ppermute | solution.py:311
  73.7 2.6 %collective-permute-done.5 = bf16[16,4096]{1,0:T(8,128)(2,1)S(1)} collective-permute-done((bf16[16,4096]{1,0:T(8,128)(2,1)S(1)}, bf16[16,4096]{1,0:T(8,128)(2,1)S(1)}, u32[]{:S(2)}, u32[]{:S(2)}) %collective-permute-start.5) | collective-permute-done | bytes 131104 | tf_op jit(solution)/shard_map/ppermute | solution.py:311
  76.3 2.4 %collective-permute-start.6 = (bf16[16,4096]{1,0:T(8,128)(2,1)S(1)}, bf16[16,4096]{1,0:T(8,128)(2,1)S(1)}, u32[]{:S(2)}, u32[]{:S(2)}) collective-permute-start(bf16[16,4096]{1,0:T(8,128)(2,1)S(1)} %collective-permute-done.5), channel_id=1, source_target_pairs={{0,1},{1,2},{2,3},{3,0},{4,7},{5,4},{6,5},{7,6},{8,9},{9,10},{10,1... | collective-permute-start | bytes 393224 | tf_op jit(solution)/shard_map/ppermute | solution.py:311
  78.7 3.2 %collective-permute-done.6 = bf16[16,4096]{1,0:T(8,128)(2,1)S(1)} collective-permute-done((bf16[16,4096]{1,0:T(8,128)(2,1)S(1)}, bf16[16,4096]{1,0:T(8,128)(2,1)S(1)}, u32[]{:S(2)}, u32[]{:S(2)}) %collective-permute-start.6) | collective-permute-done | bytes 131104 | tf_op jit(solution)/shard_map/ppermute | solution.py:311
  86.5 24.0 %collective-permute-done.8.refs_4_ = bf16[1,4096,384]{2,1,0:T(8,128)(2,1)} collective-permute-done((bf16[1,4096,384]{2,1,0:T(8,128)(2,1)}, bf16[1,4096,384]{2,1,0:T(8,128)(2,1)}, u32[]{:S(2)}, u32[]{:S(2)}) %collective-permute-start.8) | collective-permute-done | bytes 3145760 | tf_op jit(solution)/shard_map/ppermute | solution.py:299
  111.8 32.4 %collective-permute-done.9.refs_5_ = bf16[1,384,4096]{2,1,0:T(8,128)(2,1)} collective-permute-done((bf16[1,384,4096]{2,1,0:T(8,128)(2,1)}, bf16[1,384,4096]{2,1,0:T(8,128)(2,1)}, u32[]{:S(2)}, u32[]{:S(2)}) %collective-permute-start.9) | collective-permute-done | bytes 3145760 | tf_op jit(solution)/shard_map/ppermute | solution.py:299
  146.8 6.6 %all-to-all-start.2 = ((bf16[16,16,4096]{2,1,0:T(8,128)(2,1)}), bf16[16,16,4096]{2,1,0:T(8,128)(2,1)}, u32[]{:S(2)}, u32[]{:S(2)}) async-start(bf16[16,16,4096]{2,1,0:T(8,128)(2,1)} %bitcast.7), calls=%async_computation.2 | async-start | bytes 4194304 | tf_op jit(solution)/shard_map/all_to_all | solution.py:387
  153.5 23.6 %all-to-all-done.2 = bf16[16,16,4096]{2,1,0:T(8,128)(2,1)} async-done(((bf16[16,16,4096]{2,1,0:T(8,128)(2,1)}), bf16[16,16,4096]{2,1,0:T(8,128)(2,1)}, u32[]{:S(2)}, u32[]{:S(2)}) %all-to-all-start.2) | async-done | bytes 2097184 | tf_op jit(solution)/shard_map/all_to_all | solution.py:387
  177.1 11.1 %expert_ffn.1 = bf16[64,4,4096]{2,1,0:T(4,128)(2,1)} custom-call(s32[1]{0:T(128)} %bitcast.5.flag, bf16[256,4096]{1,0:T(8,128)(2,1)} %bitcast.8.rows_in, bf16[1,4096,384]{2,1,0:T(8,128)(2,1)} %refs_0_.1, bf16[1,4096,384]{2,1,0:T(8,128)(2,1)} %refs_1_.1, bf16[1,384,4096]{2,1,0:T(8,128)(2,1)} %refs_2_.1, bf16[1,4096,384]{2,1,0:T(8,128)(2,1)} %collective-permute-done.7.refs_3_, ...), custom_call_target="tpu_custom_call" | custom-call | flops 4831838208 | bytes 23068672 | tf_op jit(solution)/shard_map/expert_ffn/pallas_call | solution.py:216
  188.3 15.8 %all-to-all-start.3 = ((bf16[64,4,4096]{2,1,0:T(4,128)(2,1)}), bf16[64,4,4096]{2,1,0:T(4,128)(2,1)}, u32[]{:S(2)}, u32[]{:S(2)}) async-start(bf16[64,4,4096]{2,1,0:T(4,128)(2,1)} %expert_ffn.1), calls=%async_computation.3 | async-start | bytes 4194304 | tf_op jit(solution)/shard_map/all_to_all | solution.py:409
  205.7 26.3 %all-to-all-done.3.rows_in = bf16[64,4,4096]{2,1,0:T(4,128)(2,1)} async-done(((bf16[64,4,4096]{2,1,0:T(4,128)(2,1)}), bf16[64,4,4096]{2,1,0:T(4,128)(2,1)}, u32[]{:S(2)}, u32[]{:S(2)}) %all-to-all-start.3) | async-done | bytes 2097184 | tf_op jit(solution)/shard_map/all_to_all | solution.py:409
  232.0 3.9 %combined.1 = f32[16,4096]{1,0:T(8,128)} custom-call(bf16[16,256]{1,0:T(8,128)(2,1)} %copy.31.weights, bf16[64,4,4096]{2,1,0:T(4,128)(2,1)} %all-to-all-done.3.rows_in, f32[16,4096]{1,0:T(8,128)} %copy-done.1), custom_call_target="tpu_custom_call" | custom-call | flops 33554432 | bytes 2097152 | tf_op jit(solution)/shard_map/combined/pallas_call | solution.py:249
  (60 shorter events, 17.9 us)
Async XLA Ops:
  0.0 204.0 %copy-start = (bf16[4096,64]{0,1:T(8,128)(2,1)S(1)}, bf16[4096,64]{0,1:T(8,128)(2,1)}, u32[]{:S(2)}) copy-start(bf16[4096,64]{0,1:T(8,128)(2,1)} %param.23) | copy-start | bytes 1572868
  0.0 26.1 %copy-start.2 = (bf16[256,4096]{1,0:T(8,128)(2,1)S(1)}, bf16[256,4096]{1,0:T(8,128)(2,1)}, u32[]{:S(2)}) copy-start(bf16[256,4096]{1,0:T(8,128)(2,1)} %param.21) | copy-start | bytes 6291460
  0.0 26.8 %collective-permute-start = (bf16[256,4096]{1,0:T(8,128)(2,1)}, bf16[256,4096]{1,0:T(8,128)(2,1)}, u32[]{:S(2)}, u32[]{:S(2)}) collective-permute-start(bf16[256,4096]{1,0:T(8,128)(2,1)} %param.21), channel_id=1, source_target_pairs={{0,4},{4,0},{1,5},{5,1},{2,6},{6,2},{3,7},{7,3},{8,12},{12,8},{9,1... | collective-permute-start | bytes 6291464 | tf_op jit(solution)/shard_map/ppermute | solution.py:29
  30.5 34.0 %copy-start.3 = (bf16[16,4096]{1,0:T(8,128)(2,1)S(1)}, bf16[16,4096]{1,0:T(8,128)(2,1)}, u32[]{:S(2)}) copy-start(bf16[16,4096]{1,0:T(8,128)(2,1)} %param.14) | copy-start | bytes 393220
  30.5 34.2 %copy-start.4 = (f32[4096]{0:T(1024)S(1)}, f32[4096]{0:T(1024)}, u32[]{:S(2)}) copy-start(f32[4096]{0:T(1024)} %param.22) | copy-start | bytes 49156
  30.5 33.7 %all-to-all-start.1 = ((bf16[16,16,4096]{2,1,0:T(8,128)(2,1)}), bf16[16,16,4096]{2,1,0:T(8,128)(2,1)S(1)}, u32[]{:S(2)}, u32[]{:S(2)}) async-start(bf16[16,16,4096]{2,1,0:T(8,128)(2,1)} %bitcast.17), calls=%async_computation.1 | async-start | bytes 4194304 | tf_op jit(solution)/shard_map/all_to_all | solution.py:366
  34.4 50.8 %collective-permute-start.7 = (bf16[1,4096,384]{2,1,0:T(8,128)(2,1)}, bf16[1,4096,384]{2,1,0:T(8,128)(2,1)}, u32[]{:S(2)}, u32[]{:S(2)}) collective-permute-start(bf16[1,4096,384]{2,1,0:T(8,128)(2,1)} %refs_0_.1), channel_id=1, source_target_pairs={{1,0},{3,2},{4,5},{6,7},{9,8},{11,10},{12,13},{14,15},{17,16},{19,... | collective-permute-start | bytes 9437192 | tf_op jit(solution)/shard_map/ppermute | solution.py:299
  39.6 105.9 %collective-permute-start.10 = (bf16[1,4096,384]{2,1,0:T(8,128)(2,1)}, bf16[1,4096,384]{2,1,0:T(8,128)(2,1)}, u32[]{:S(2)}, u32[]{:S(2)}) collective-permute-start(bf16[1,4096,384]{2,1,0:T(8,128)(2,1)} %refs_0_.1), channel_id=1, source_target_pairs={{0,4},{2,6},{5,1},{7,3},{8,12},{10,14},{13,9},{15,11},{16,20},{18,... | collective-permute-start | bytes 9437192 | tf_op jit(solution)/shard_map/ppermute | solution.py:299
  40.9 12.5 %collective-permute-start.1 = (s32[16,8]{0,1:T(8,128)S(1)}, s32[16,8]{0,1:T(8,128)S(1)}, u32[]{:S(2)}, u32[]{:S(2)}) collective-permute-start(s32[16,8]{0,1:T(8,128)S(1)} %copy-done.5), channel_id=1, source_target_pairs={{0,1},{1,2},{2,3},{3,0},{4,7},{5,4},{6,5},{7,6},{8,9},{9,10},{10,1... | collective-permute-start | bytes 1544 | tf_op jit(solution)/shard_map/ppermute | solution.py:311
  47.4 63.1 %collective-permute-start.8 = (bf16[1,4096,384]{2,1,0:T(8,128)(2,1)}, bf16[1,4096,384]{2,1,0:T(8,128)(2,1)}, u32[]{:S(2)}, u32[]{:S(2)}) collective-permute-start(bf16[1,4096,384]{2,1,0:T(8,128)(2,1)} %refs_1_.1), channel_id=1, source_target_pairs={{1,0},{3,2},{4,5},{6,7},{9,8},{11,10},{12,13},{14,15},{17,16},{19,... | collective-permute-start | bytes 9437192 | tf_op jit(solution)/shard_map/ppermute | solution.py:299
  50.4 93.8 %collective-permute-start.9 = (bf16[1,384,4096]{2,1,0:T(8,128)(2,1)}, bf16[1,384,4096]{2,1,0:T(8,128)(2,1)}, u32[]{:S(2)}, u32[]{:S(2)}) collective-permute-start(bf16[1,384,4096]{2,1,0:T(8,128)(2,1)} %refs_2_.1), channel_id=1, source_target_pairs={{1,0},{3,2},{4,5},{6,7},{9,8},{11,10},{12,13},{14,15},{17,16},{19,... | collective-permute-start | bytes 9437192 | tf_op jit(solution)/shard_map/ppermute | solution.py:299
  53.4 3.0 %collective-permute-start.2 = (s32[16,8]{0,1:T(8,128)S(1)}, s32[16,8]{0,1:T(8,128)S(1)}, u32[]{:S(2)}, u32[]{:S(2)}) collective-permute-start(s32[16,8]{0,1:T(8,128)S(1)} %collective-permute-done.1), channel_id=1, source_target_pairs={{0,1},{1,2},{2,3},{3,0},{4,7},{5,4},{6,5},{7,6},{8,9},{9,10},{10,1... | collective-permute-start | bytes 1544 | tf_op jit(solution)/shard_map/ppermute | solution.py:311
  56.4 2.9 %collective-permute-start.3 = (s32[16,8]{0,1:T(8,128)S(1)}, s32[16,8]{0,1:T(8,128)S(1)}, u32[]{:S(2)}, u32[]{:S(2)}) collective-permute-start(s32[16,8]{0,1:T(8,128)S(1)} %collective-permute-done.2), channel_id=1, source_target_pairs={{0,1},{1,2},{2,3},{3,0},{4,7},{5,4},{6,5},{7,6},{8,9},{9,10},{10,1... | collective-permute-start | bytes 1544 | tf_op jit(solution)/shard_map/ppermute | solution.py:311
  64.7 82.1 %copy-start.1 = (f32[16,4096]{1,0:T(8,128)}, f32[16,4096]{1,0:T(8,128)S(1)}, u32[]{:S(2)}) copy-start(f32[16,4096]{1,0:T(8,128)S(1)} %get-tuple-element.22.hidden) | copy-start | bytes 786436
  64.8 5.9 %collective-permute-start.4 = (bf16[16,4096]{1,0:T(8,128)(2,1)S(1)}, bf16[16,4096]{1,0:T(8,128)(2,1)S(1)}, u32[]{:S(2)}, u32[]{:S(2)}) collective-permute-start(bf16[16,4096]{1,0:T(8,128)(2,1)S(1)} %multiply_convert_fusion), channel_id=1, source_target_pairs={{0,1},{1,2},{2,3},{3,0},{4,7},{5,4},{6,5},{7,6},{8,9},{9,10},{10,1... | collective-permute-start | bytes 393224 | tf_op jit(solution)/shard_map/ppermute | solution.py:311
  70.7 5.6 %collective-permute-start.5 = (bf16[16,4096]{1,0:T(8,128)(2,1)S(1)}, bf16[16,4096]{1,0:T(8,128)(2,1)S(1)}, u32[]{:S(2)}, u32[]{:S(2)}) collective-permute-start(bf16[16,4096]{1,0:T(8,128)(2,1)S(1)} %collective-permute-done.4), channel_id=1, source_target_pairs={{0,1},{1,2},{2,3},{3,0},{4,7},{5,4},{6,5},{7,6},{8,9},{9,10},{10,1... | collective-permute-start | bytes 393224 | tf_op jit(solution)/shard_map/ppermute | solution.py:311
  76.3 5.6 %collective-permute-start.6 = (bf16[16,4096]{1,0:T(8,128)(2,1)S(1)}, bf16[16,4096]{1,0:T(8,128)(2,1)S(1)}, u32[]{:S(2)}, u32[]{:S(2)}) collective-permute-start(bf16[16,4096]{1,0:T(8,128)(2,1)S(1)} %collective-permute-done.5), channel_id=1, source_target_pairs={{0,1},{1,2},{2,3},{3,0},{4,7},{5,4},{6,5},{7,6},{8,9},{9,10},{10,1... | collective-permute-start | bytes 393224 | tf_op jit(solution)/shard_map/ppermute | solution.py:311
  81.9 71.6 %collective-permute-start.11 = (bf16[1,4096,384]{2,1,0:T(8,128)(2,1)}, bf16[1,4096,384]{2,1,0:T(8,128)(2,1)}, u32[]{:S(2)}, u32[]{:S(2)}) collective-permute-start(bf16[1,4096,384]{2,1,0:T(8,128)(2,1)} %refs_1_.1), channel_id=1, source_target_pairs={{0,4},{2,6},{5,1},{7,3},{8,12},{10,14},{13,9},{15,11},{16,20},{18,... | collective-permute-start | bytes 9437192 | tf_op jit(solution)/shard_map/ppermute | solution.py:299
  85.2 68.3 %collective-permute-start.12 = (bf16[1,384,4096]{2,1,0:T(8,128)(2,1)}, bf16[1,384,4096]{2,1,0:T(8,128)(2,1)}, u32[]{:S(2)}, u32[]{:S(2)}) collective-permute-start(bf16[1,384,4096]{2,1,0:T(8,128)(2,1)} %refs_2_.1), channel_id=1, source_target_pairs={{0,4},{2,6},{5,1},{7,3},{8,12},{10,14},{13,9},{15,11},{16,20},{18,... | collective-permute-start | bytes 9437192 | tf_op jit(solution)/shard_map/ppermute | solution.py:299
  110.5 66.6 %collective-permute-start.13 = (bf16[1,4096,384]{2,1,0:T(8,128)(2,1)}, bf16[1,4096,384]{2,1,0:T(8,128)(2,1)}, u32[]{:S(2)}, u32[]{:S(2)}) collective-permute-start(bf16[1,4096,384]{2,1,0:T(8,128)(2,1)} %collective-permute-done.7.refs_3_), channel_id=1, source_target_pairs={{0,4},{2,6},{5,1},{7,3},{8,12},{10,14},{13,9},{15,11},{16,20},{18,... | collective-permute-start | bytes 9437192 | tf_op jit(solution)/shard_map/ppermute | solution.py:299
  144.2 32.9 %collective-permute-start.14 = (bf16[1,4096,384]{2,1,0:T(8,128)(2,1)}, bf16[1,4096,384]{2,1,0:T(8,128)(2,1)}, u32[]{:S(2)}, u32[]{:S(2)}) collective-permute-start(bf16[1,4096,384]{2,1,0:T(8,128)(2,1)} %collective-permute-done.8.refs_4_), channel_id=1, source_target_pairs={{0,4},{2,6},{5,1},{7,3},{8,12},{10,14},{13,9},{15,11},{16,20},{18,... | collective-permute-start | bytes 9437192 | tf_op jit(solution)/shard_map/ppermute | solution.py:299
  145.5 31.6 %collective-permute-start.15 = (bf16[1,384,4096]{2,1,0:T(8,128)(2,1)}, bf16[1,384,4096]{2,1,0:T(8,128)(2,1)}, u32[]{:S(2)}, u32[]{:S(2)}) collective-permute-start(bf16[1,384,4096]{2,1,0:T(8,128)(2,1)} %collective-permute-done.9.refs_5_), channel_id=1, source_target_pairs={{0,4},{2,6},{5,1},{7,3},{8,12},{10,14},{13,9},{15,11},{16,20},{18,... | collective-permute-start | bytes 9437192 | tf_op jit(solution)/shard_map/ppermute | solution.py:299
  146.8 30.3 %all-to-all-start.2 = ((bf16[16,16,4096]{2,1,0:T(8,128)(2,1)}), bf16[16,16,4096]{2,1,0:T(8,128)(2,1)}, u32[]{:S(2)}, u32[]{:S(2)}) async-start(bf16[16,16,4096]{2,1,0:T(8,128)(2,1)} %bitcast.7), calls=%async_computation.2 | async-start | bytes 4194304 | tf_op jit(solution)/shard_map/all_to_all | solution.py:387
  188.3 43.7 %all-to-all-start.3 = ((bf16[64,4,4096]{2,1,0:T(4,128)(2,1)}), bf16[64,4,4096]{2,1,0:T(4,128)(2,1)}, u32[]{:S(2)}, u32[]{:S(2)}) async-start(bf16[64,4,4096]{2,1,0:T(4,128)(2,1)} %expert_ffn.1), calls=%async_computation.3 | async-start | bytes 4194304 | tf_op jit(solution)/shard_map/all_to_all | solution.py:409
  (1 other events, 10.4 us)

commit v7 on v6

--- a/solution.py
+++ b/solution.py
@@ -17,7 +17,7 @@
 OUT_STEPS = 2
 CUTS = 8
 X_CUTS = 4
-COMBINE_STEPS = 4
+COMBINE_STEPS = 2
 
 
 EP = ("chip", "core")
@@ -47,43 +47,47 @@
     span = keys.shape[1]
     owner = lax.broadcasted_iota(jnp.int32, (H, HD), 0) // group
     position = lax.broadcasted_iota(jnp.int32, (H, span), 1)
-    for local_row in range(keys.shape[0]):
-        row = step * keys.shape[0] + local_row
-        q = q_buf[pl.ds(row * H, H), :]
+    each = keys.shape[0]
+    base = step * each
+    q_all = q_buf[pl.ds(base * H, each * H), :]
+
+    def fanned(value):
+        return jnp.concatenate(
+            [
+                jnp.broadcast_to(value[row : row + 1, g * HD : (g + 1) * HD], (group, HD))
+                for row in range(each)
+                for g in range(KVH)
+            ],
+            axis=0,
+        )
+
+    past = []
+    for row in range(each):
+        q = q_all[row * H : (row + 1) * H]
         blocks = [jnp.where(owner == g, q, 0.0).astype(jnp.bfloat16) for g in range(KVH)]
         scores = scale * lax.dot_general(
             jnp.concatenate(blocks, axis=1),
-            keys[local_row],
+            keys[row],
             (((1,), (1,)), ((), ())),
             preferred_element_type=jnp.float32,
         )
-        new_key = jnp.concatenate(
-            [
-                jnp.broadcast_to(nk[local_row : local_row + 1, g * HD : (g + 1) * HD], (group, HD))
-                for g in range(KVH)
-            ],
-            axis=0,
-        )
-        new_value = jnp.concatenate(
-            [
-                jnp.broadcast_to(nv[local_row : local_row + 1, g * HD : (g + 1) * HD], (group, HD))
-                for g in range(KVH)
-            ],
-            axis=0,
-        )
-        own = scale * jnp.sum(q * new_key, axis=1, keepdims=True)
-        scores = jnp.where(position < lengths[row], scores, -1e30)
-        peak = jnp.maximum(jnp.max(scores, axis=1, keepdims=True), own)
-        past_exp = jnp.exp(scores - peak)
-        own_exp = jnp.exp(own - peak)
-        denom = jnp.sum(past_exp, axis=1, keepdims=True) + own_exp
-        weights = (past_exp / denom).astype(jnp.bfloat16)
-        own_weight = (own_exp / denom).astype(jnp.bfloat16).astype(jnp.float32)
-        wide = jnp.dot(weights, values[local_row], preferred_element_type=jnp.float32)
+        past.append(jnp.where(position < lengths[base + row], scores, -1e30))
+    past = jnp.concatenate(past, axis=0)
+    own = scale * jnp.sum(q_all * fanned(nk), axis=1, keepdims=True)
+    peak = jnp.maximum(jnp.max(past, axis=1, keepdims=True), own)
+    past_exp = jnp.exp(past - peak)
+    own_exp = jnp.exp(own - peak)
+    denom = jnp.sum(past_exp, axis=1, keepdims=True) + own_exp
+    weights = (past_exp / denom).astype(jnp.bfloat16)
+    own_part = (own_exp / denom).astype(jnp.bfloat16).astype(jnp.float32) * fanned(nv)
+    for row in range(each):
+        wide = jnp.dot(
+            weights[row * H : (row + 1) * H], values[row], preferred_element_type=jnp.float32
+        )
         blended = jnp.concatenate(
             [wide[g * group : (g + 1) * group, g * HD : (g + 1) * HD] for g in range(KVH)], axis=0
         )
-        o_buf[pl.ds(row * H, H), :] = blended + own_weight * new_value
+        o_buf[pl.ds((base + row) * H, H), :] = blended + own_part[row * H : (row + 1) * H]
 
     @pl.when(step == pl.num_programs(0) - 1)
     def _():
@@ -131,8 +135,8 @@
 
 
 def ffn_kernel(flag, rows_in, *refs):
-    own, crossed, near, far = refs[0:3], refs[3:6], refs[6:9], refs[9:12]
-    out, x_buf, in_buf, down_buf, y_buf, x_sem, in_sem, down_sem, y_sem = refs[12:]
+    own, crossed, near, far = refs[0:3], refs[3:7], refs[7:10], refs[10:14]
+    out, x_buf, in_buf, down_buf, y_buf, x_sem, in_sem, down_sem, y_sem = refs[14:]
     hf = own[0].shape[2]
     deep = D // CUTS
     wide = D // OUT_STEPS
@@ -148,11 +152,18 @@
             in_sem.at[2 * side + part, cut],
         )
 
-    def down_copy(side, source, step):
+    def down_copy(row, source, step):
         return pltpu.make_async_copy(
-            source[2].at[0, :, pl.ds(step * wide, wide)],
-            down_buf.at[pl.ds(side * hf, hf), pl.ds(step * wide, wide)],
-            down_sem.at[side, step],
+            source.at[0, :, pl.ds(step * wide, wide)],
+            down_buf.at[pl.ds(row, source.shape[1]), pl.ds(step * wide, wide)],
+            down_sem.at[row // (hf // 2), step],
+        )
+
+    def down_copies(first, second, step):
+        return (
+            down_copy(0, first[2], step),
+            down_copy(hf, second[2], step),
+            down_copy(hf + hf // 2, second[3], step),
         )
 
     def start(first, second):
@@ -161,8 +172,8 @@
                 for cut in range(CUTS):
                     in_copy(side, source, part, cut).start()
         for step in range(OUT_STEPS):
-            down_copy(0, first, step).start()
-            down_copy(1, second, step).start()
+            for copy in down_copies(first, second, step):
+                copy.start()
 
     for cut in range(X_CUTS):
         x_copy(cut).start()
@@ -192,8 +203,8 @@
     copies = []
     for step in range(OUT_STEPS):
         columns = slice(step * wide, (step + 1) * wide)
-        for side in range(2):
-            down_copy(side, own, step).wait()
+        for copy in down_copies(own, crossed, step):
+            copy.wait()
         rows_out = jnp.dot(act, down_buf[:, columns], preferred_element_type=jnp.float32)
         for chunk in range(out.shape[0]):
             y_buf[chunk, :, columns] = rows_out[chunk * CAP : (chunk + 1) * CAP].astype(
@@ -217,7 +228,7 @@
         ffn_kernel,
         out_shape=jax.ShapeDtypeStruct((count // CAP, CAP, D), jnp.bfloat16),
         in_specs=[pl.BlockSpec(memory_space=pltpu.SMEM)]
-        + [pl.BlockSpec(memory_space=pltpu.HBM)] * 13,
+        + [pl.BlockSpec(memory_space=pltpu.HBM)] * 15,
         out_specs=pl.BlockSpec(memory_space=pltpu.HBM),
         scratch_shapes=[
             pltpu.VMEM((count, D), jnp.bfloat16),
@@ -226,7 +237,7 @@
             pltpu.VMEM((count // CAP, CAP, D), jnp.bfloat16),
             pltpu.SemaphoreType.DMA((X_CUTS,)),
             pltpu.SemaphoreType.DMA((4, CUTS)),
-            pltpu.SemaphoreType.DMA((2, OUT_STEPS)),
+            pltpu.SemaphoreType.DMA((4, OUT_STEPS)),
             pltpu.SemaphoreType.DMA((OUT_STEPS,)),
         ],
         compiler_params=pltpu.CompilerParams(vmem_limit_bytes=123 * 512 * 1024),
@@ -362,13 +373,12 @@
 
     partial = partial.astype(jnp.bfloat16)
     up_crossed = moved(up_slab, across, partial)
-    down_crossed = moved(down_slab, across, partial)
+    middle = down_slab.shape[1] // 2
+    held, _ = lax.optimization_barrier((down_slab, partial))
+    halves = lax.optimization_barrier((held[:, :middle], held[:, middle:]))
+    down_crossed = [moved(half, across) for half in halves]
     partial = lax.all_to_all(
-        partial.reshape(chips, rows, D),
-        "chip",
-        split_axis=0,
-        concat_axis=0,
-        tiled=True,
+        partial.reshape(chips, rows, D), "chip", split_axis=0, concat_axis=0, tiled=True
     )
     partial, dispatch, own_slots = lax.optimization_barrier((partial, dispatch, own_slots))
     hidden = resid.astype(jnp.float32) + jnp.sum(partial.astype(jnp.float32), axis=0)
@@ -383,7 +393,7 @@
     ).astype(jnp.bfloat16)
     gate_far = moved(gate_crossed, beside, outgoing)
     up_far = moved(up_crossed, beside, outgoing)
-    down_far = moved(down_crossed, beside, outgoing)
+    down_far = [moved(half, beside, outgoing) for half in down_crossed]
     incoming = lax.all_to_all(
         outgoing.reshape(chips, slots, D), "chip", split_axis=0, concat_axis=0, tiled=True
     )
@@ -402,9 +412,9 @@
         flag,
         incoming.reshape(chips * slots, D),
         (gate_slab, up_slab, down_slab),
-        (gate_crossed, up_crossed, down_crossed),
+        (gate_crossed, up_crossed, *down_crossed),
         (gate_near, up_near, down_near),
-        (gate_far, up_far, down_far),
+        (gate_far, up_far, *down_far),
     )
     returned = lax.all_to_all(produced, ("chip", "dp"), split_axis=0, concat_axis=0, tiled=True)
     return combined(combine.reshape(rows, chips * depths * CAP), returned, hidden)

time: 238 us -> 235 us (0.987)
  Pallas kernels: 24.4 us -> 19.1 us
  starting transfers between devices: 62.9 us -> 68.1 us
  waiting for transfers between devices: 124 us -> 119 us
    all_to_all x1, waiting for transfers between devices: 23.6 us -> 12 us  [local(): lax.all_to_all(outgoing.reshape(chips, slots, D), 'chip', split_axis=0, c...]
    all_to_all x1, waiting for transfers between devices: 4.54 us -> 13 us  [local(): lax.all_to_all(partial.reshape(chips, rows, D), 'chip', split_axis=0, con...]
    ppermute x6, waiting for transfers between devices: 12.6 us -> 6.42 us  [gathered(): blocks.append(lax.ppermute(blocks[-1], ('core', 'dp'), ring))]
    pallas_call x1, Pallas kernels: 9.39 us -> 4.98 us  [attention(): pl.pallas_call(attention_kernel, grid=(ATTN_STEPS,), out_shape=jax.ShapeD...]
    ppermute x9 -> x11, waiting for transfers between devices: 56.5 us -> 60.5 us  [moved(): return lax.ppermute(slab, ('core', 'dp'), pairs)]
    ppermute x6, starting transfers between devices: 16.4 us -> 19.7 us  [gathered(): blocks.append(lax.ppermute(blocks[-1], ('core', 'dp'), ring))]
    ppermute x9 -> x11, starting transfers between devices: 18.9 us -> 19.3 us  [moved(): return lax.ppermute(slab, ('core', 'dp'), pairs)]
  transfers between devices with their start and end apart: 19 -> 21, of which waited for: 10 -> 11; matrix products, arithmetic and copies ran while one was open for 2% -> 3% of each run, Pallas kernels for 4% -> 2%
where the time goes in v7:
time: 235 us; the launch traced here: 233 us
  waiting for transfers between devices  119 us (51%)
  starting transfers between devices  68.1 us (29%)
  Pallas kernels  19.1 us (8%)
  blocking collectives  15.3 us (7%)
  matrix products  7.11 us (3%)
  local copies, waits for them, and re-layouts  3.33 us (1%)
    ppermute x11, waiting for transfers between devices, moved(): return lax.ppermute(slab, ('core', 'dp'), pairs)  60.5 us
    all_to_all x1, waiting for transfers between devices, local(): lax.all_to_all(produced, ('chip', 'dp'), split_axis=0, concat_axis=0, til...  26.9 us
    ppermute x6, starting transfers between devices, gathered(): blocks.append(lax.ppermute(blocks[-1], ('core', 'dp'), ring))  19.7 us
    ppermute x11, starting transfers between devices, moved(): return lax.ppermute(slab, ('core', 'dp'), pairs)  19.3 us
    all_to_all x1, starting transfers between devices, local(): lax.all_to_all(produced, ('chip', 'dp'), split_axis=0, concat_axis=0, til...  17.2 us
    all_to_all x1, blocking collectives, local(): lax.all_to_all(sent, 'chip', split_axis=0, concat_axis=0, tiled=True)  15.3 us
    all_to_all x1, waiting for transfers between devices, local(): lax.all_to_all(partial.reshape(chips, rows, D), 'chip', split_axis=0, con...  13 us
    all_to_all x1, waiting for transfers between devices, local(): lax.all_to_all(outgoing.reshape(chips, slots, D), 'chip', split_axis=0, c...  12 us
  transfers between devices with their start and end apart: 21, of which 11 were waited for; matrix products, arithmetic and copies ran while one was open for 3% of the time, Pallas kernels for 2%

profile of v7, /device:TPU:1, one launch (start us, length us, event | category | flops | bytes accessed | tf_op | source)
XLA Modules:
  0.0 233.4 jit_solution(16212507298589175063)
XLA Ops:
  1.4 5.0 %attention.1 = bf16[16,16,512]{2,1,0:T(8,128)(2,1)} custom-call(s32[1]{0:T(128)} %bitcast.swap, s32[16]{0:T(128)} %lengths.1, bf16[16,8192]{1,0:T(8,128)(2,1)} %q_in.1, bf16[16,512]{1,0:T(8,128)(2,1)} %nk_in.1, bf16[16,512]{1,0:T(8,128)(2,1)} %nv_in.1, bf16[16,128,512]{2,1,0:T(8,128)(2,1)} %keys.1, bf16[16,128,512]{2,1,0:T(8,128)(2,1)} %values.1), custom_call_target="tpu_custom_call" | custom-call | flops 134217728 | bytes 4194304 | tf_op jit(solution)/shard_map/attention/pallas_call | solution.py:111
  6.4 15.3 %all_to_all.20 = bf16[16,16,512]{2,1,0:T(8,128)(2,1)S(1)} all-to-all(bf16[16,16,512]{2,1,0:T(8,128)(2,1)} %attention.1), channel_id=1, replica_groups=mesh['chip'=16,'core'=2,'dp'=4] {'chip'}, dimensions={0} | all-to-all | bytes 524288 | tf_op jit(solution)/shard_map/all_to_all | solution.py:339
  22.4 3.7 %fusion = bf16[256,4096]{1,0:T(8,128)(2,1)} fusion(f32[256,4096]{1,0:T(8,128)S(1)} %fusion.12, bf16[256,4096]{1,0:T(8,128)(2,1)} %collective-permute-done, bf16[256,512]{1,0:T(8,128)(2,1)S(1)} %bitcast.19), kind=kOutput, calls=%fused_computation.1 | convolution fusion | flops 538968064 | bytes 8519680 | tf_op jit(solution)/shard_map/dot_general | solution.py:342
  26.2 3.8 %all-to-all-start.1 = ((bf16[16,16,4096]{2,1,0:T(8,128)(2,1)}), bf16[16,16,4096]{2,1,0:T(8,128)(2,1)S(1)}, u32[]{:S(2)}, u32[]{:S(2)}) async-start(bf16[16,16,4096]{2,1,0:T(8,128)(2,1)} %bitcast.17), calls=%async_computation.1 | async-start | bytes 4194304 | tf_op jit(solution)/shard_map/all_to_all | solution.py:380
  30.1 3.8 %collective-permute-start.1 = (s32[16,8]{0,1:T(8,128)S(1)}, s32[16,8]{0,1:T(8,128)S(1)}, u32[]{:S(2)}, u32[]{:S(2)}) collective-permute-start(s32[16,8]{0,1:T(8,128)S(1)} %copy-done.6), channel_id=1, source_target_pairs={{0,1},{1,2},{2,3},{3,0},{4,7},{5,4},{6,5},{7,6},{8,9},{9,10},{10,1... | collective-permute-start | bytes 1544 | tf_op jit(solution)/shard_map/ppermute | solution.py:322
  33.9 2.9 %collective-permute-start.7 = (bf16[1,4096,384]{2,1,0:T(8,128)(2,1)}, bf16[1,4096,384]{2,1,0:T(8,128)(2,1)}, u32[]{:S(2)}, u32[]{:S(2)}) collective-permute-start(bf16[1,4096,384]{2,1,0:T(8,128)(2,1)} %refs_0_.1), channel_id=1, source_target_pairs={{1,0},{3,2},{4,5},{6,7},{9,8},{11,10},{12,13},{14,15},{17,16},{19,... | collective-permute-start | bytes 9437192 | tf_op jit(solution)/shard_map/ppermute | solution.py:310
  37.6 2.7 %collective-permute-done.2 = s32[16,8]{0,1:T(8,128)S(1)} collective-permute-done((s32[16,8]{0,1:T(8,128)S(1)}, s32[16,8]{0,1:T(8,128)S(1)}, u32[]{:S(2)}, u32[]{:S(2)}) %collective-permute-start.2) | collective-permute-done | bytes 544 | tf_op jit(solution)/shard_map/ppermute | solution.py:322
  43.6 3.6 %collective-permute-start.8 = (bf16[1,4096,384]{2,1,0:T(8,128)(2,1)}, bf16[1,4096,384]{2,1,0:T(8,128)(2,1)}, u32[]{:S(2)}, u32[]{:S(2)}) collective-permute-start(bf16[1,4096,384]{2,1,0:T(8,128)(2,1)} %refs_1_.1), channel_id=1, source_target_pairs={{1,0},{3,2},{4,5},{6,7},{9,8},{11,10},{12,13},{14,15},{17,16},{19,... | collective-permute-start | bytes 9437192 | tf_op jit(solution)/shard_map/ppermute | solution.py:310
  47.1 13.0 %all-to-all-done.1 = bf16[16,16,4096]{2,1,0:T(8,128)(2,1)S(1)} async-done(((bf16[16,16,4096]{2,1,0:T(8,128)(2,1)}), bf16[16,16,4096]{2,1,0:T(8,128)(2,1)S(1)}, u32[]{:S(2)}, u32[]{:S(2)}) %all-to-all-start.1) | async-done | bytes 2097184 | tf_op jit(solution)/shard_map/all_to_all | solution.py:380
  60.7 3.8 %collective-permute-start.4 = (bf16[16,4096]{1,0:T(8,128)(2,1)S(1)}, bf16[16,4096]{1,0:T(8,128)(2,1)S(1)}, u32[]{:S(2)}, u32[]{:S(2)}) collective-permute-start(bf16[16,4096]{1,0:T(8,128)(2,1)S(1)} %multiply_convert_fusion), channel_id=1, source_target_pairs={{0,1},{1,2},{2,3},{3,0},{4,7},{5,4},{6,5},{7,6},{8,9},{9,10},{10,1... | collective-permute-start | bytes 393224 | tf_op jit(solution)/shard_map/ppermute | solution.py:322
  66.5 3.0 %collective-permute-start.5 = (bf16[16,4096]{1,0:T(8,128)(2,1)S(1)}, bf16[16,4096]{1,0:T(8,128)(2,1)S(1)}, u32[]{:S(2)}, u32[]{:S(2)}) collective-permute-start(bf16[16,4096]{1,0:T(8,128)(2,1)S(1)} %collective-permute-done.4), channel_id=1, source_target_pairs={{0,1},{1,2},{2,3},{3,0},{4,7},{5,4},{6,5},{7,6},{8,9},{9,10},{10,1... | collective-permute-start | bytes 393224 | tf_op jit(solution)/shard_map/ppermute | solution.py:322
  72.2 7.6 %collective-permute-start.6 = (bf16[16,4096]{1,0:T(8,128)(2,1)S(1)}, bf16[16,4096]{1,0:T(8,128)(2,1)S(1)}, u32[]{:S(2)}, u32[]{:S(2)}) collective-permute-start(bf16[16,4096]{1,0:T(8,128)(2,1)S(1)} %collective-permute-done.5), channel_id=1, source_target_pairs={{0,1},{1,2},{2,3},{3,0},{4,7},{5,4},{6,5},{7,6},{8,9},{9,10},{10,1... | collective-permute-start | bytes 393224 | tf_op jit(solution)/shard_map/ppermute | solution.py:322
  83.4 2.4 %collective-permute-start.10 = (bf16[1,192,4096]{2,1,0:T(8,128)(2,1)S(1)}, bf16[1,192,4096]{2,1,0:T(8,128)(2,1)}, u32[]{:S(2)}, u32[]{:S(2)}) collective-permute-start(bf16[1,192,4096]{2,1,0:T(8,128)(2,1)S(1)} %get-tuple-element.22), channel_id=1, source_target_pairs={{1,0},{3,2},{4,5},{6,7},{9,8},{11,10},{12,13},{14,15},{17,16},{19,... | collective-permute-start | bytes 4718600 | tf_op jit(solution)/shard_map/ppermute | solution.py:310
  87.9 19.8 %collective-permute-done.8.refs_4_ = bf16[1,4096,384]{2,1,0:T(8,128)(2,1)} collective-permute-done((bf16[1,4096,384]{2,1,0:T(8,128)(2,1)}, bf16[1,4096,384]{2,1,0:T(8,128)(2,1)}, u32[]{:S(2)}, u32[]{:S(2)}) %collective-permute-start.8) | collective-permute-done | bytes 3145760 | tf_op jit(solution)/shard_map/ppermute | solution.py:310
  109.0 15.5 %collective-permute-done.9.refs_5_ = bf16[1,192,4096]{2,1,0:T(8,128)(2,1)S(1)} collective-permute-done((bf16[1,192,4096]{2,1,0:T(8,128)(2,1)S(1)}, bf16[1,192,4096]{2,1,0:T(8,128)(2,1)S(1)}, u32[]{:S(2)}, u32[]{:S(2)}) %collective-permute-start.9) | collective-permute-done | bytes 1572896 | tf_op jit(solution)/shard_map/ppermute | solution.py:310
  125.7 15.6 %collective-permute-done.10.refs_6_ = bf16[1,192,4096]{2,1,0:T(8,128)(2,1)} collective-permute-done((bf16[1,192,4096]{2,1,0:T(8,128)(2,1)S(1)}, bf16[1,192,4096]{2,1,0:T(8,128)(2,1)}, u32[]{:S(2)}, u32[]{:S(2)}) %collective-permute-start.10) | collective-permute-done | bytes 1572896 | tf_op jit(solution)/shard_map/ppermute | solution.py:310
  142.6 6.7 %all-to-all-start.2 = ((bf16[16,16,4096]{2,1,0:T(8,128)(2,1)}), bf16[16,16,4096]{2,1,0:T(8,128)(2,1)}, u32[]{:S(2)}, u32[]{:S(2)}) async-start(bf16[16,16,4096]{2,1,0:T(8,128)(2,1)} %bitcast.7), calls=%async_computation.2 | async-start | bytes 4194304 | tf_op jit(solution)/shard_map/all_to_all | solution.py:397
  151.9 7.0 %collective-permute-done.16.refs_12_ = bf16[1,192,4096]{2,1,0:T(8,128)(2,1)} collective-permute-done((bf16[1,192,4096]{2,1,0:T(8,128)(2,1)S(1)}, bf16[1,192,4096]{2,1,0:T(8,128)(2,1)}, u32[]{:S(2)}, u32[]{:S(2)}) %collective-permute-start.16) | collective-permute-done | bytes 1572896 | tf_op jit(solution)/shard_map/ppermute | solution.py:310
  158.9 2.7 %collective-permute-done.17.refs_13_ = bf16[1,192,4096]{2,1,0:T(8,128)(2,1)} collective-permute-done((bf16[1,192,4096]{2,1,0:T(8,128)(2,1)}, bf16[1,192,4096]{2,1,0:T(8,128)(2,1)}, u32[]{:S(2)}, u32[]{:S(2)}) %collective-permute-start.17) | collective-permute-done | bytes 1572896 | tf_op jit(solution)/shard_map/ppermute | solution.py:310
  161.6 12.0 %all-to-all-done.2 = bf16[16,16,4096]{2,1,0:T(8,128)(2,1)} async-done(((bf16[16,16,4096]{2,1,0:T(8,128)(2,1)}), bf16[16,16,4096]{2,1,0:T(8,128)(2,1)}, u32[]{:S(2)}, u32[]{:S(2)}) %all-to-all-start.2) | async-done | bytes 2097184 | tf_op jit(solution)/shard_map/all_to_all | solution.py:397
  173.6 11.4 %expert_ffn.1 = bf16[64,4,4096]{2,1,0:T(4,128)(2,1)} custom-call(s32[1]{0:T(128)} %bitcast.5.flag, bf16[256,4096]{1,0:T(8,128)(2,1)} %bitcast.8.rows_in, bf16[1,4096,384]{2,1,0:T(8,128)(2,1)} %refs_0_.1, bf16[1,4096,384]{2,1,0:T(8,128)(2,1)} %refs_1_.1, bf16[1,384,4096]{2,1,0:T(8,128)(2,1)} %refs_2_.1, bf16[1,4096,384]{2,1,0:T(8,128)(2,1)} %collective-permute-done.7.refs_3_, ...), custom_call_target="tpu_custom_call" | custom-call | flops 4831838208 | bytes 23068672 | tf_op jit(solution)/shard_map/expert_ffn/pallas_call | solution.py:227
  185.0 17.2 %all-to-all-start.3 = ((bf16[64,4,4096]{2,1,0:T(4,128)(2,1)}), bf16[64,4,4096]{2,1,0:T(4,128)(2,1)}, u32[]{:S(2)}, u32[]{:S(2)}) async-start(bf16[64,4,4096]{2,1,0:T(4,128)(2,1)} %expert_ffn.1), calls=%async_computation.3 | async-start | bytes 4194304 | tf_op jit(solution)/shard_map/all_to_all | solution.py:419
  203.8 26.9 %all-to-all-done.3.rows_in = bf16[64,4,4096]{2,1,0:T(4,128)(2,1)} async-done(((bf16[64,4,4096]{2,1,0:T(4,128)(2,1)}), bf16[64,4,4096]{2,1,0:T(4,128)(2,1)}, u32[]{:S(2)}, u32[]{:S(2)}) %all-to-all-start.3) | async-done | bytes 2097184 | tf_op jit(solution)/shard_map/all_to_all | solution.py:419
  230.8 2.7 %combined.1 = f32[16,4096]{1,0:T(8,128)} custom-call(bf16[16,256]{1,0:T(8,128)(2,1)} %copy.31.weights, bf16[64,4,4096]{2,1,0:T(4,128)(2,1)} %all-to-all-done.3.rows_in, f32[16,4096]{1,0:T(8,128)} %copy-done.1), custom_call_target="tpu_custom_call" | custom-call | flops 33554432 | bytes 2097152 | tf_op jit(solution)/shard_map/combined/pallas_call | solution.py:260
  (67 shorter events, 25.2 us)
Async XLA Ops:
  0.0 202.2 %copy-start = (bf16[4096,64]{0,1:T(8,128)(2,1)S(1)}, bf16[4096,64]{0,1:T(8,128)(2,1)}, u32[]{:S(2)}) copy-start(bf16[4096,64]{0,1:T(8,128)(2,1)} %param.23) | copy-start | bytes 1572868
  0.0 22.4 %collective-permute-start = (bf16[256,4096]{1,0:T(8,128)(2,1)}, bf16[256,4096]{1,0:T(8,128)(2,1)}, u32[]{:S(2)}, u32[]{:S(2)}) collective-permute-start(bf16[256,4096]{1,0:T(8,128)(2,1)} %param.21), channel_id=1, source_target_pairs={{0,4},{4,0},{1,5},{5,1},{2,6},{6,2},{3,7},{7,3},{8,12},{12,8},{9,1... | collective-permute-start | bytes 6291464 | tf_op jit(solution)/shard_map/ppermute | solution.py:29
  26.2 33.9 %all-to-all-start.1 = ((bf16[16,16,4096]{2,1,0:T(8,128)(2,1)}), bf16[16,16,4096]{2,1,0:T(8,128)(2,1)S(1)}, u32[]{:S(2)}, u32[]{:S(2)}) async-start(bf16[16,16,4096]{2,1,0:T(8,128)(2,1)} %bitcast.17), calls=%async_computation.1 | async-start | bytes 4194304 | tf_op jit(solution)/shard_map/all_to_all | solution.py:380
  30.0 30.4 %copy-start.4 = (bf16[16,4096]{1,0:T(8,128)(2,1)S(1)}, bf16[16,4096]{1,0:T(8,128)(2,1)}, u32[]{:S(2)}) copy-start(bf16[16,4096]{1,0:T(8,128)(2,1)} %param.14) | copy-start | bytes 393220
  30.1 30.5 %copy-start.5 = (f32[4096]{0:T(1024)S(1)}, f32[4096]{0:T(1024)}, u32[]{:S(2)}) copy-start(f32[4096]{0:T(1024)} %param.22) | copy-start | bytes 49156
  30.1 7.2 %collective-permute-start.1 = (s32[16,8]{0,1:T(8,128)S(1)}, s32[16,8]{0,1:T(8,128)S(1)}, u32[]{:S(2)}, u32[]{:S(2)}) collective-permute-start(s32[16,8]{0,1:T(8,128)S(1)} %copy-done.6), channel_id=1, source_target_pairs={{0,1},{1,2},{2,3},{3,0},{4,7},{5,4},{6,5},{7,6},{8,9},{9,10},{10,1... | collective-permute-start | bytes 1544 | tf_op jit(solution)/shard_map/ppermute | solution.py:322
  33.9 48.1 %collective-permute-start.7 = (bf16[1,4096,384]{2,1,0:T(8,128)(2,1)}, bf16[1,4096,384]{2,1,0:T(8,128)(2,1)}, u32[]{:S(2)}, u32[]{:S(2)}) collective-permute-start(bf16[1,4096,384]{2,1,0:T(8,128)(2,1)} %refs_0_.1), channel_id=1, source_target_pairs={{1,0},{3,2},{4,5},{6,7},{9,8},{11,10},{12,13},{14,15},{17,16},{19,... | collective-permute-start | bytes 9437192 | tf_op jit(solution)/shard_map/ppermute | solution.py:310
  37.3 3.0 %collective-permute-start.2 = (s32[16,8]{0,1:T(8,128)S(1)}, s32[16,8]{0,1:T(8,128)S(1)}, u32[]{:S(2)}, u32[]{:S(2)}) collective-permute-start(s32[16,8]{0,1:T(8,128)S(1)} %collective-permute-done.1), channel_id=1, source_target_pairs={{0,1},{1,2},{2,3},{3,0},{4,7},{5,4},{6,5},{7,6},{8,9},{9,10},{10,1... | collective-permute-start | bytes 1544 | tf_op jit(solution)/shard_map/ppermute | solution.py:322
  40.3 2.9 %collective-permute-start.3 = (s32[16,8]{0,1:T(8,128)S(1)}, s32[16,8]{0,1:T(8,128)S(1)}, u32[]{:S(2)}, u32[]{:S(2)}) collective-permute-start(s32[16,8]{0,1:T(8,128)S(1)} %collective-permute-done.2), channel_id=1, source_target_pairs={{0,1},{1,2},{2,3},{3,0},{4,7},{5,4},{6,5},{7,6},{8,9},{9,10},{10,1... | collective-permute-start | bytes 1544 | tf_op jit(solution)/shard_map/ppermute | solution.py:322
  43.6 64.1 %collective-permute-start.8 = (bf16[1,4096,384]{2,1,0:T(8,128)(2,1)}, bf16[1,4096,384]{2,1,0:T(8,128)(2,1)}, u32[]{:S(2)}, u32[]{:S(2)}) collective-permute-start(bf16[1,4096,384]{2,1,0:T(8,128)(2,1)} %refs_1_.1), channel_id=1, source_target_pairs={{1,0},{3,2},{4,5},{6,7},{9,8},{11,10},{12,13},{14,15},{17,16},{19,... | collective-permute-start | bytes 9437192 | tf_op jit(solution)/shard_map/ppermute | solution.py:310
  60.7 5.8 %collective-permute-start.4 = (bf16[16,4096]{1,0:T(8,128)(2,1)S(1)}, bf16[16,4096]{1,0:T(8,128)(2,1)S(1)}, u32[]{:S(2)}, u32[]{:S(2)}) collective-permute-start(bf16[16,4096]{1,0:T(8,128)(2,1)S(1)} %multiply_convert_fusion), channel_id=1, source_target_pairs={{0,1},{1,2},{2,3},{3,0},{4,7},{5,4},{6,5},{7,6},{8,9},{9,10},{10,1... | collective-permute-start | bytes 393224 | tf_op jit(solution)/shard_map/ppermute | solution.py:322
  66.5 5.6 %collective-permute-start.5 = (bf16[16,4096]{1,0:T(8,128)(2,1)S(1)}, bf16[16,4096]{1,0:T(8,128)(2,1)S(1)}, u32[]{:S(2)}, u32[]{:S(2)}) collective-permute-start(bf16[16,4096]{1,0:T(8,128)(2,1)S(1)} %collective-permute-done.4), channel_id=1, source_target_pairs={{0,1},{1,2},{2,3},{3,0},{4,7},{5,4},{6,5},{7,6},{8,9},{9,10},{10,1... | collective-permute-start | bytes 393224 | tf_op jit(solution)/shard_map/ppermute | solution.py:322
  69.5 79.7 %collective-permute-start.11 = (bf16[1,4096,384]{2,1,0:T(8,128)(2,1)}, bf16[1,4096,384]{2,1,0:T(8,128)(2,1)}, u32[]{:S(2)}, u32[]{:S(2)}) collective-permute-start(bf16[1,4096,384]{2,1,0:T(8,128)(2,1)} %refs_0_.1), channel_id=1, source_target_pairs={{0,4},{2,6},{5,1},{7,3},{8,12},{10,14},{13,9},{15,11},{16,20},{18,... | collective-permute-start | bytes 9437192 | tf_op jit(solution)/shard_map/ppermute | solution.py:310
  70.8 79.8 %collective-permute-start.12 = (bf16[1,4096,384]{2,1,0:T(8,128)(2,1)}, bf16[1,4096,384]{2,1,0:T(8,128)(2,1)}, u32[]{:S(2)}, u32[]{:S(2)}) collective-permute-start(bf16[1,4096,384]{2,1,0:T(8,128)(2,1)} %refs_1_.1), channel_id=1, source_target_pairs={{0,4},{2,6},{5,1},{7,3},{8,12},{10,14},{13,9},{15,11},{16,20},{18,... | collective-permute-start | bytes 9437192 | tf_op jit(solution)/shard_map/ppermute | solution.py:310
  72.2 11.2 %collective-permute-start.6 = (bf16[16,4096]{1,0:T(8,128)(2,1)S(1)}, bf16[16,4096]{1,0:T(8,128)(2,1)S(1)}, u32[]{:S(2)}, u32[]{:S(2)}) collective-permute-start(bf16[16,4096]{1,0:T(8,128)(2,1)S(1)} %collective-permute-done.5), channel_id=1, source_target_pairs={{0,1},{1,2},{2,3},{3,0},{4,7},{5,4},{6,5},{7,6},{8,9},{9,10},{10,1... | collective-permute-start | bytes 393224 | tf_op jit(solution)/shard_map/ppermute | solution.py:322
  82.0 42.5 %collective-permute-start.9 = (bf16[1,192,4096]{2,1,0:T(8,128)(2,1)S(1)}, bf16[1,192,4096]{2,1,0:T(8,128)(2,1)S(1)}, u32[]{:S(2)}, u32[]{:S(2)}) collective-permute-start(bf16[1,192,4096]{2,1,0:T(8,128)(2,1)S(1)} %get-tuple-element.21), channel_id=1, source_target_pairs={{1,0},{3,2},{4,5},{6,7},{9,8},{11,10},{12,13},{14,15},{17,16},{19,... | collective-permute-start | bytes 4718600 | tf_op jit(solution)/shard_map/ppermute | solution.py:310
  83.4 57.9 %collective-permute-start.10 = (bf16[1,192,4096]{2,1,0:T(8,128)(2,1)S(1)}, bf16[1,192,4096]{2,1,0:T(8,128)(2,1)}, u32[]{:S(2)}, u32[]{:S(2)}) collective-permute-start(bf16[1,192,4096]{2,1,0:T(8,128)(2,1)S(1)} %get-tuple-element.22), channel_id=1, source_target_pairs={{1,0},{3,2},{4,5},{6,7},{9,8},{11,10},{12,13},{14,15},{17,16},{19,... | collective-permute-start | bytes 4718600 | tf_op jit(solution)/shard_map/ppermute | solution.py:310
  107.7 44.2 %collective-permute-start.13 = (bf16[1,384,4096]{2,1,0:T(8,128)(2,1)}, bf16[1,384,4096]{2,1,0:T(8,128)(2,1)}, u32[]{:S(2)}, u32[]{:S(2)}) collective-permute-start(bf16[1,384,4096]{2,1,0:T(8,128)(2,1)} %refs_2_.1), channel_id=1, source_target_pairs={{0,4},{2,6},{5,1},{7,3},{8,12},{10,14},{13,9},{15,11},{16,20},{18,... | collective-permute-start | bytes 9437192 | tf_op jit(solution)/shard_map/ppermute | solution.py:310
  124.4 49.1 %collective-permute-start.14 = (bf16[1,4096,384]{2,1,0:T(8,128)(2,1)}, bf16[1,4096,384]{2,1,0:T(8,128)(2,1)}, u32[]{:S(2)}, u32[]{:S(2)}) collective-permute-start(bf16[1,4096,384]{2,1,0:T(8,128)(2,1)} %collective-permute-done.7.refs_3_), channel_id=1, source_target_pairs={{0,4},{2,6},{5,1},{7,3},{8,12},{10,14},{13,9},{15,11},{16,20},{18,... | collective-permute-start | bytes 9437192 | tf_op jit(solution)/shard_map/ppermute | solution.py:310
  141.3 32.3 %collective-permute-start.15 = (bf16[1,4096,384]{2,1,0:T(8,128)(2,1)}, bf16[1,4096,384]{2,1,0:T(8,128)(2,1)}, u32[]{:S(2)}, u32[]{:S(2)}) collective-permute-start(bf16[1,4096,384]{2,1,0:T(8,128)(2,1)} %collective-permute-done.8.refs_4_), channel_id=1, source_target_pairs={{0,4},{2,6},{5,1},{7,3},{8,12},{10,14},{13,9},{15,11},{16,20},{18,... | collective-permute-start | bytes 9437192 | tf_op jit(solution)/shard_map/ppermute | solution.py:310
  142.6 31.0 %all-to-all-start.2 = ((bf16[16,16,4096]{2,1,0:T(8,128)(2,1)}), bf16[16,16,4096]{2,1,0:T(8,128)(2,1)}, u32[]{:S(2)}, u32[]{:S(2)}) async-start(bf16[16,16,4096]{2,1,0:T(8,128)(2,1)} %bitcast.7), calls=%async_computation.2 | async-start | bytes 4194304 | tf_op jit(solution)/shard_map/all_to_all | solution.py:397
  149.3 9.6 %collective-permute-start.16 = (bf16[1,192,4096]{2,1,0:T(8,128)(2,1)S(1)}, bf16[1,192,4096]{2,1,0:T(8,128)(2,1)}, u32[]{:S(2)}, u32[]{:S(2)}) collective-permute-start(bf16[1,192,4096]{2,1,0:T(8,128)(2,1)S(1)} %collective-permute-done.9.refs_5_), channel_id=1, source_target_pairs={{0,4},{2,6},{5,1},{7,3},{8,12},{10,14},{13,9},{15,11},{16,20},{18,... | collective-permute-start | bytes 4718600 | tf_op jit(solution)/shard_map/ppermute | solution.py:310
  150.6 11.0 %collective-permute-start.17 = (bf16[1,192,4096]{2,1,0:T(8,128)(2,1)}, bf16[1,192,4096]{2,1,0:T(8,128)(2,1)}, u32[]{:S(2)}, u32[]{:S(2)}) collective-permute-start(bf16[1,192,4096]{2,1,0:T(8,128)(2,1)} %collective-permute-done.10.refs_6_), channel_id=1, source_target_pairs={{0,4},{2,6},{5,1},{7,3},{8,12},{10,14},{13,9},{15,11},{16,20},{18,... | collective-permute-start | bytes 4718600 | tf_op jit(solution)/shard_map/ppermute | solution.py:310
  185.0 45.8 %all-to-all-start.3 = ((bf16[64,4,4096]{2,1,0:T(4,128)(2,1)}), bf16[64,4,4096]{2,1,0:T(4,128)(2,1)}, u32[]{:S(2)}, u32[]{:S(2)}) async-start(bf16[64,4,4096]{2,1,0:T(4,128)(2,1)} %expert_ffn.1), calls=%async_computation.3 | async-start | bytes 4194304 | tf_op jit(solution)/shard_map/all_to_all | solution.py:419
  (4 other events, 70.4 us)

commit v8 on v7

--- a/solution.py
+++ b/solution.py
@@ -156,14 +156,14 @@
         return pltpu.make_async_copy(
             source.at[0, :, pl.ds(step * wide, wide)],
             down_buf.at[pl.ds(row, source.shape[1]), pl.ds(step * wide, wide)],
-            down_sem.at[row // (hf // 2), step],
+            down_sem.at[(4 * row) // hf, step],
         )
 
     def down_copies(first, second, step):
         return (
             down_copy(0, first[2], step),
             down_copy(hf, second[2], step),
-            down_copy(hf + hf // 2, second[3], step),
+            down_copy(hf + second[2].shape[1], second[3], step),
         )
 
     def start(first, second):
@@ -237,7 +237,7 @@
             pltpu.VMEM((count // CAP, CAP, D), jnp.bfloat16),
             pltpu.SemaphoreType.DMA((X_CUTS,)),
             pltpu.SemaphoreType.DMA((4, CUTS)),
-            pltpu.SemaphoreType.DMA((4, OUT_STEPS)),
+            pltpu.SemaphoreType.DMA((8, OUT_STEPS)),
             pltpu.SemaphoreType.DMA((OUT_STEPS,)),
         ],
         compiler_params=pltpu.CompilerParams(vmem_limit_bytes=123 * 512 * 1024),
@@ -373,10 +373,12 @@
 
     partial = partial.astype(jnp.bfloat16)
     up_crossed = moved(up_slab, across, partial)
-    middle = down_slab.shape[1] // 2
+    middle = down_slab.shape[1] // 4 * 3
     held, _ = lax.optimization_barrier((down_slab, partial))
     halves = lax.optimization_barrier((held[:, :middle], held[:, middle:]))
-    down_crossed = [moved(half, across) for half in halves]
+    most = moved(halves[0], across)
+    rest = moved(halves[1], across)
+    down_crossed = (most, rest)
     partial = lax.all_to_all(
         partial.reshape(chips, rows, D), "chip", split_axis=0, concat_axis=0, tiled=True
     )
@@ -385,7 +387,8 @@
     meansq = jnp.mean(hidden * hidden, axis=1, keepdims=True)
     normed = (hidden * lax.rsqrt(jnp.maximum(meansq, 0.25)) * norm_gain).astype(jnp.bfloat16)
 
-    tokens = jnp.concatenate(gathered(normed), axis=0)
+    blocks = gathered(normed)
+    tokens = jnp.concatenate(blocks, axis=0)
     outgoing = jnp.dot(
         dispatch.reshape(chips * slots, count).astype(jnp.bfloat16),
         tokens,

time: 235 us -> 234 us (level)
  waiting for transfers between devices: 119 us -> 107 us
  starting transfers between devices: 68.1 us -> 74.9 us
  local copies, waits for them, and re-layouts: 3.33 us -> 6.19 us
    all_to_all x1, waiting for transfers between devices: 13 us -> 0.01 us  [local(): lax.all_to_all(partial.reshape(chips, rows, D), 'chip', split_axis=0, con...]
    ppermute x11, starting transfers between devices: 19.3 us -> 26.3 us  [moved(): return lax.ppermute(slab, ('core', 'dp'), pairs)]
    ppermute x6, waiting for transfers between devices: 6.42 us -> 9.49 us  [gathered(): blocks.append(lax.ppermute(blocks[-1], ('core', 'dp'), ring))]
  transfers between devices with their start and end apart: 21 -> 21, of which waited for: 11 -> 11; matrix products, arithmetic and copies ran while one was open for 3% -> 4% of each run, Pallas kernels for 2% -> 2%
where the time goes in v8:
time: 234 us; the launch traced here: 232 us
  waiting for transfers between devices  107 us (46%)
  starting transfers between devices  74.9 us (32%)
  Pallas kernels  19.3 us (8%)
  blocking collectives  15.3 us (7%)
  matrix products  7.02 us (3%)
  local copies, waits for them, and re-layouts  6.19 us (3%)
    ppermute x11, waiting for transfers between devices, moved(): return lax.ppermute(slab, ('core', 'dp'), pairs)  59.7 us
    ppermute x11, starting transfers between devices, moved(): return lax.ppermute(slab, ('core', 'dp'), pairs)  26.3 us
    all_to_all x1, waiting for transfers between devices, local(): lax.all_to_all(produced, ('chip', 'dp'), split_axis=0, concat_axis=0, til...  26.3 us
    ppermute x6, starting transfers between devices, gathered(): blocks.append(lax.ppermute(blocks[-1], ('core', 'dp'), ring))  20.4 us
    all_to_all x1, starting transfers between devices, local(): lax.all_to_all(produced, ('chip', 'dp'), split_axis=0, concat_axis=0, til...  16.4 us
    all_to_all x1, blocking collectives, local(): lax.all_to_all(sent, 'chip', split_axis=0, concat_axis=0, tiled=True)  15.3 us
    all_to_all x1, waiting for transfers between devices, local(): lax.all_to_all(outgoing.reshape(chips, slots, D), 'chip', split_axis=0, c...  11.8 us
    pallas_call x1, Pallas kernels, expert_ffn(): pl.pallas_call(ffn_kernel, out_shape=jax.ShapeDtypeStruct((count // CAP,...  11.6 us
  transfers between devices with their start and end apart: 21, of which 11 were waited for; matrix products, arithmetic and copies ran while one was open for 4% of the time, Pallas kernels for 2%

profile of v8, /device:TPU:1, one launch (start us, length us, event | category | flops | bytes accessed | tf_op | source)
XLA Modules:
  0.0 231.7 jit_solution(16641249673604900192)
XLA Ops:
  1.4 5.0 %attention.1 = bf16[16,16,512]{2,1,0:T(8,128)(2,1)} custom-call(s32[1]{0:T(128)} %bitcast.swap, s32[16]{0:T(128)} %lengths.1, bf16[16,8192]{1,0:T(8,128)(2,1)} %q_in.1, bf16[16,512]{1,0:T(8,128)(2,1)} %nk_in.1, bf16[16,512]{1,0:T(8,128)(2,1)} %nv_in.1, bf16[16,128,512]{2,1,0:T(8,128)(2,1)} %keys.1, bf16[16,128,512]{2,1,0:T(8,128)(2,1)} %values.1), custom_call_target="tpu_custom_call" | custom-call | flops 134217728 | bytes 4194304 | tf_op jit(solution)/shard_map/attention/pallas_call | solution.py:111
  6.4 15.3 %all_to_all.20 = bf16[16,16,512]{2,1,0:T(8,128)(2,1)S(1)} all-to-all(bf16[16,16,512]{2,1,0:T(8,128)(2,1)} %attention.1), channel_id=1, replica_groups=mesh['chip'=16,'core'=2,'dp'=4] {'chip'}, dimensions={0} | all-to-all | bytes 524288 | tf_op jit(solution)/shard_map/all_to_all | solution.py:339
  22.4 3.7 %fusion = bf16[256,4096]{1,0:T(8,128)(2,1)} fusion(f32[256,4096]{1,0:T(8,128)S(1)} %fusion.12, bf16[256,4096]{1,0:T(8,128)(2,1)} %collective-permute-done, bf16[256,512]{1,0:T(8,128)(2,1)S(1)} %bitcast.19), kind=kOutput, calls=%fused_computation.1 | convolution fusion | flops 538968064 | bytes 8519680 | tf_op jit(solution)/shard_map/dot_general | solution.py:342
  26.1 3.8 %all-to-all-start.1 = ((bf16[16,16,4096]{2,1,0:T(8,128)(2,1)}), bf16[16,16,4096]{2,1,0:T(8,128)(2,1)S(1)}, u32[]{:S(2)}, u32[]{:S(2)}) async-start(bf16[16,16,4096]{2,1,0:T(8,128)(2,1)} %bitcast.17), calls=%async_computation.1 | async-start | bytes 4194304 | tf_op jit(solution)/shard_map/all_to_all | solution.py:382
  30.0 5.2 %collective-permute-start.7 = (bf16[1,4096,384]{2,1,0:T(8,128)(2,1)}, bf16[1,4096,384]{2,1,0:T(8,128)(2,1)}, u32[]{:S(2)}, u32[]{:S(2)}) collective-permute-start(bf16[1,4096,384]{2,1,0:T(8,128)(2,1)} %refs_0_.1), channel_id=1, source_target_pairs={{1,0},{3,2},{4,5},{6,7},{9,8},{11,10},{12,13},{14,15},{17,16},{19,... | collective-permute-start | bytes 9437192 | tf_op jit(solution)/shard_map/ppermute | solution.py:310
  36.5 6.0 %collective-permute-start.1 = (s32[16,8]{0,1:T(8,128)S(1)}, s32[16,8]{0,1:T(8,128)S(1)}, u32[]{:S(2)}, u32[]{:S(2)}) collective-permute-start(s32[16,8]{0,1:T(8,128)S(1)} %copy-done.7), channel_id=1, source_target_pairs={{0,1},{1,2},{2,3},{3,0},{4,7},{5,4},{6,5},{7,6},{8,9},{9,10},{10,1... | collective-permute-start | bytes 1544 | tf_op jit(solution)/shard_map/ppermute | solution.py:322
  43.3 3.2 %collective-permute-start.2 = (s32[16,8]{0,1:T(8,128)S(1)}, s32[16,8]{0,1:T(8,128)S(1)}, u32[]{:S(2)}, u32[]{:S(2)}) collective-permute-start(s32[16,8]{0,1:T(8,128)S(1)} %collective-permute-done.1), channel_id=1, source_target_pairs={{0,1},{1,2},{2,3},{3,0},{4,7},{5,4},{6,5},{7,6},{8,9},{9,10},{10,1... | collective-permute-start | bytes 1544 | tf_op jit(solution)/shard_map/ppermute | solution.py:322
  47.2 3.2 %collective-permute-start.3 = (s32[16,8]{0,1:T(8,128)S(1)}, s32[16,8]{0,1:T(8,128)S(1)}, u32[]{:S(2)}, u32[]{:S(2)}) collective-permute-start(s32[16,8]{0,1:T(8,128)S(1)} %collective-permute-done.2), channel_id=1, source_target_pairs={{0,1},{1,2},{2,3},{3,0},{4,7},{5,4},{6,5},{7,6},{8,9},{9,10},{10,1... | collective-permute-start | bytes 1544 | tf_op jit(solution)/shard_map/ppermute | solution.py:322
  51.3 3.0 %collective-permute-start.8 = (bf16[1,4096,384]{2,1,0:T(8,128)(2,1)}, bf16[1,4096,384]{2,1,0:T(8,128)(2,1)}, u32[]{:S(2)}, u32[]{:S(2)}) collective-permute-start(bf16[1,4096,384]{2,1,0:T(8,128)(2,1)} %refs_1_.1), channel_id=1, source_target_pairs={{1,0},{3,2},{4,5},{6,7},{9,8},{11,10},{12,13},{14,15},{17,16},{19,... | collective-permute-start | bytes 9437192 | tf_op jit(solution)/shard_map/ppermute | solution.py:310
  55.8 3.3 %slice.14 = bf16[1,288,4096]{2,1,0:T(8,128)(2,1)} slice(bf16[1,384,4096]{2,1,0:T(8,128)(2,1)} %refs_2_.1), slice={[0:1], [0:288], [0:4096]} | slice | bytes 4718592 | tf_op jit(solution)/shard_map/slice | solution.py:378
  59.1 2.8 %collective-permute-start.9 = (bf16[1,288,4096]{2,1,0:T(8,128)(2,1)}, bf16[1,288,4096]{2,1,0:T(8,128)(2,1)}, u32[]{:S(2)}, u32[]{:S(2)}) collective-permute-start(bf16[1,288,4096]{2,1,0:T(8,128)(2,1)} %slice.14), channel_id=1, source_target_pairs={{1,0},{3,2},{4,5},{6,7},{9,8},{11,10},{12,13},{14,15},{17,16},{19,... | collective-permute-start | bytes 7077896 | tf_op jit(solution)/shard_map/ppermute | solution.py:310
  65.0 3.7 %collective-permute-done.4 = bf16[16,4096]{1,0:T(8,128)(2,1)S(1)} collective-permute-done((bf16[16,4096]{1,0:T(8,128)(2,1)S(1)}, bf16[16,4096]{1,0:T(8,128)(2,1)S(1)}, u32[]{:S(2)}, u32[]{:S(2)}) %collective-permute-start.4) | collective-permute-done | bytes 131104 | tf_op jit(solution)/shard_map/ppermute | solution.py:322
  68.8 3.0 %collective-permute-start.5 = (bf16[16,4096]{1,0:T(8,128)(2,1)S(1)}, bf16[16,4096]{1,0:T(8,128)(2,1)S(1)}, u32[]{:S(2)}, u32[]{:S(2)}) collective-permute-start(bf16[16,4096]{1,0:T(8,128)(2,1)S(1)} %collective-permute-done.4), channel_id=1, source_target_pairs={{0,1},{1,2},{2,3},{3,0},{4,7},{5,4},{6,5},{7,6},{8,9},{9,10},{10,1... | collective-permute-start | bytes 393224 | tf_op jit(solution)/shard_map/ppermute | solution.py:322
  74.4 3.0 %collective-permute-start.6 = (bf16[16,4096]{1,0:T(8,128)(2,1)S(1)}, bf16[16,4096]{1,0:T(8,128)(2,1)S(1)}, u32[]{:S(2)}, u32[]{:S(2)}) collective-permute-start(bf16[16,4096]{1,0:T(8,128)(2,1)S(1)} %collective-permute-done.5), channel_id=1, source_target_pairs={{0,1},{1,2},{2,3},{3,0},{4,7},{5,4},{6,5},{7,6},{8,9},{9,10},{10,1... | collective-permute-start | bytes 393224 | tf_op jit(solution)/shard_map/ppermute | solution.py:322
  80.0 6.3 %collective-permute-start.10 = (bf16[1,96,4096]{2,1,0:T(8,128)(2,1)S(1)}, bf16[1,96,4096]{2,1,0:T(8,128)(2,1)S(1)}, u32[]{:S(2)}, u32[]{:S(2)}) collective-permute-start(bf16[1,96,4096]{2,1,0:T(8,128)(2,1)S(1)} %slice.15), channel_id=1, source_target_pairs={{1,0},{3,2},{4,5},{6,7},{9,8},{11,10},{12,13},{14,15},{17,16},{19,... | collective-permute-start | bytes 2359304 | tf_op jit(solution)/shard_map/ppermute | solution.py:310
  88.4 17.7 %collective-permute-done.8.refs_4_ = bf16[1,4096,384]{2,1,0:T(8,128)(2,1)} collective-permute-done((bf16[1,4096,384]{2,1,0:T(8,128)(2,1)}, bf16[1,4096,384]{2,1,0:T(8,128)(2,1)}, u32[]{:S(2)}, u32[]{:S(2)}) %collective-permute-start.8) | collective-permute-done | bytes 3145760 | tf_op jit(solution)/shard_map/ppermute | solution.py:310
  107.4 32.3 %collective-permute-done.10.refs_6_ = bf16[1,96,4096]{2,1,0:T(8,128)(2,1)S(1)} collective-permute-done((bf16[1,96,4096]{2,1,0:T(8,128)(2,1)S(1)}, bf16[1,96,4096]{2,1,0:T(8,128)(2,1)S(1)}, u32[]{:S(2)}, u32[]{:S(2)}) %collective-permute-start.10) | collective-permute-done | bytes 786464 | tf_op jit(solution)/shard_map/ppermute | solution.py:310
  143.6 6.6 %all-to-all-start.2 = ((bf16[16,16,4096]{2,1,0:T(8,128)(2,1)}), bf16[16,16,4096]{2,1,0:T(8,128)(2,1)}, u32[]{:S(2)}, u32[]{:S(2)}) async-start(bf16[16,16,4096]{2,1,0:T(8,128)(2,1)} %bitcast.7), calls=%async_computation.2 | async-start | bytes 4194304 | tf_op jit(solution)/shard_map/all_to_all | solution.py:400
  151.6 9.6 %collective-permute-done.17.refs_13_ = bf16[1,96,4096]{2,1,0:T(8,128)(2,1)S(1)} collective-permute-done((bf16[1,96,4096]{2,1,0:T(8,128)(2,1)S(1)}, bf16[1,96,4096]{2,1,0:T(8,128)(2,1)S(1)}, u32[]{:S(2)}, u32[]{:S(2)}) %collective-permute-start.17) | collective-permute-done | bytes 786464 | tf_op jit(solution)/shard_map/ppermute | solution.py:310
  161.2 11.8 %all-to-all-done.2 = bf16[16,16,4096]{2,1,0:T(8,128)(2,1)} async-done(((bf16[16,16,4096]{2,1,0:T(8,128)(2,1)}), bf16[16,16,4096]{2,1,0:T(8,128)(2,1)}, u32[]{:S(2)}, u32[]{:S(2)}) %all-to-all-start.2) | async-done | bytes 2097184 | tf_op jit(solution)/shard_map/all_to_all | solution.py:400
  173.1 11.6 %expert_ffn.1 = bf16[64,4,4096]{2,1,0:T(4,128)(2,1)} custom-call(s32[1]{0:T(128)} %bitcast.5.flag, bf16[256,4096]{1,0:T(8,128)(2,1)} %bitcast.8.rows_in, bf16[1,4096,384]{2,1,0:T(8,128)(2,1)} %refs_0_.1, bf16[1,4096,384]{2,1,0:T(8,128)(2,1)} %refs_1_.1, bf16[1,384,4096]{2,1,0:T(8,128)(2,1)} %refs_2_.1, bf16[1,4096,384]{2,1,0:T(8,128)(2,1)} %collective-permute-done.7.refs_3_, ...), custom_call_target="tpu_custom_call" | custom-call | flops 4831838208 | bytes 23068672 | tf_op jit(solution)/shard_map/expert_ffn/pallas_call | solution.py:227
  184.7 16.4 %all-to-all-start.3 = ((bf16[64,4,4096]{2,1,0:T(4,128)(2,1)}), bf16[64,4,4096]{2,1,0:T(4,128)(2,1)}, u32[]{:S(2)}, u32[]{:S(2)}) async-start(bf16[64,4,4096]{2,1,0:T(4,128)(2,1)} %expert_ffn.1), calls=%async_computation.3 | async-start | bytes 4194304 | tf_op jit(solution)/shard_map/all_to_all | solution.py:422
  202.8 26.3 %all-to-all-done.3.rows_in = bf16[64,4,4096]{2,1,0:T(4,128)(2,1)} async-done(((bf16[64,4,4096]{2,1,0:T(4,128)(2,1)}), bf16[64,4,4096]{2,1,0:T(4,128)(2,1)}, u32[]{:S(2)}, u32[]{:S(2)}) %all-to-all-start.3) | async-done | bytes 2097184 | tf_op jit(solution)/shard_map/all_to_all | solution.py:422
  229.1 2.7 %combined.1 = f32[16,4096]{1,0:T(8,128)} custom-call(bf16[16,256]{1,0:T(8,128)(2,1)} %copy.31.weights, bf16[64,4,4096]{2,1,0:T(4,128)(2,1)} %all-to-all-done.3.rows_in, f32[16,4096]{1,0:T(8,128)} %copy-done.1), custom_call_target="tpu_custom_call" | custom-call | flops 33554432 | bytes 2097152 | tf_op jit(solution)/shard_map/combined/pallas_call | solution.py:260
  (70 shorter events, 25.8 us)
Async XLA Ops:
  0.0 201.1 %copy-start = (bf16[4096,64]{0,1:T(8,128)(2,1)S(1)}, bf16[4096,64]{0,1:T(8,128)(2,1)}, u32[]{:S(2)}) copy-start(bf16[4096,64]{0,1:T(8,128)(2,1)} %param.23) | copy-start | bytes 1572868
  0.0 22.4 %collective-permute-start = (bf16[256,4096]{1,0:T(8,128)(2,1)}, bf16[256,4096]{1,0:T(8,128)(2,1)}, u32[]{:S(2)}, u32[]{:S(2)}) collective-permute-start(bf16[256,4096]{1,0:T(8,128)(2,1)} %param.21), channel_id=1, source_target_pairs={{0,4},{4,0},{1,5},{5,1},{2,6},{6,2},{3,7},{7,3},{8,12},{12,8},{9,1... | collective-permute-start | bytes 6291464 | tf_op jit(solution)/shard_map/ppermute | solution.py:29
  26.1 35.8 %all-to-all-start.1 = ((bf16[16,16,4096]{2,1,0:T(8,128)(2,1)}), bf16[16,16,4096]{2,1,0:T(8,128)(2,1)S(1)}, u32[]{:S(2)}, u32[]{:S(2)}) async-start(bf16[16,16,4096]{2,1,0:T(8,128)(2,1)} %bitcast.17), calls=%async_computation.1 | async-start | bytes 4194304 | tf_op jit(solution)/shard_map/all_to_all | solution.py:382
  30.0 47.4 %collective-permute-start.7 = (bf16[1,4096,384]{2,1,0:T(8,128)(2,1)}, bf16[1,4096,384]{2,1,0:T(8,128)(2,1)}, u32[]{:S(2)}, u32[]{:S(2)}) collective-permute-start(bf16[1,4096,384]{2,1,0:T(8,128)(2,1)} %refs_0_.1), channel_id=1, source_target_pairs={{1,0},{3,2},{4,5},{6,7},{9,8},{11,10},{12,13},{14,15},{17,16},{19,... | collective-permute-start | bytes 9437192 | tf_op jit(solution)/shard_map/ppermute | solution.py:310
  35.2 107.1 %collective-permute-start.11 = (bf16[1,4096,384]{2,1,0:T(8,128)(2,1)}, bf16[1,4096,384]{2,1,0:T(8,128)(2,1)}, u32[]{:S(2)}, u32[]{:S(2)}) collective-permute-start(bf16[1,4096,384]{2,1,0:T(8,128)(2,1)} %refs_0_.1), channel_id=1, source_target_pairs={{0,4},{2,6},{5,1},{7,3},{8,12},{10,14},{13,9},{15,11},{16,20},{18,... | collective-permute-start | bytes 9437192 | tf_op jit(solution)/shard_map/ppermute | solution.py:310
  36.5 6.8 %collective-permute-start.1 = (s32[16,8]{0,1:T(8,128)S(1)}, s32[16,8]{0,1:T(8,128)S(1)}, u32[]{:S(2)}, u32[]{:S(2)}) collective-permute-start(s32[16,8]{0,1:T(8,128)S(1)} %copy-done.7), channel_id=1, source_target_pairs={{0,1},{1,2},{2,3},{3,0},{4,7},{5,4},{6,5},{7,6},{8,9},{9,10},{10,1... | collective-permute-start | bytes 1544 | tf_op jit(solution)/shard_map/ppermute | solution.py:322
  43.3 4.0 %collective-permute-start.2 = (s32[16,8]{0,1:T(8,128)S(1)}, s32[16,8]{0,1:T(8,128)S(1)}, u32[]{:S(2)}, u32[]{:S(2)}) collective-permute-start(s32[16,8]{0,1:T(8,128)S(1)} %collective-permute-done.1), channel_id=1, source_target_pairs={{0,1},{1,2},{2,3},{3,0},{4,7},{5,4},{6,5},{7,6},{8,9},{9,10},{10,1... | collective-permute-start | bytes 1544 | tf_op jit(solution)/shard_map/ppermute | solution.py:322
  47.2 4.0 %collective-permute-start.3 = (s32[16,8]{0,1:T(8,128)S(1)}, s32[16,8]{0,1:T(8,128)S(1)}, u32[]{:S(2)}, u32[]{:S(2)}) collective-permute-start(s32[16,8]{0,1:T(8,128)S(1)} %collective-permute-done.2), channel_id=1, source_target_pairs={{0,1},{1,2},{2,3},{3,0},{4,7},{5,4},{6,5},{7,6},{8,9},{9,10},{10,1... | collective-permute-start | bytes 1544 | tf_op jit(solution)/shard_map/ppermute | solution.py:322
  51.3 54.8 %collective-permute-start.8 = (bf16[1,4096,384]{2,1,0:T(8,128)(2,1)}, bf16[1,4096,384]{2,1,0:T(8,128)(2,1)}, u32[]{:S(2)}, u32[]{:S(2)}) collective-permute-start(bf16[1,4096,384]{2,1,0:T(8,128)(2,1)} %refs_1_.1), channel_id=1, source_target_pairs={{1,0},{3,2},{4,5},{6,7},{9,8},{11,10},{12,13},{14,15},{17,16},{19,... | collective-permute-start | bytes 9437192 | tf_op jit(solution)/shard_map/ppermute | solution.py:310
  59.1 81.9 %collective-permute-start.9 = (bf16[1,288,4096]{2,1,0:T(8,128)(2,1)}, bf16[1,288,4096]{2,1,0:T(8,128)(2,1)}, u32[]{:S(2)}, u32[]{:S(2)}) collective-permute-start(bf16[1,288,4096]{2,1,0:T(8,128)(2,1)} %slice.14), channel_id=1, source_target_pairs={{1,0},{3,2},{4,5},{6,7},{9,8},{11,10},{12,13},{14,15},{17,16},{19,... | collective-permute-start | bytes 7077896 | tf_op jit(solution)/shard_map/ppermute | solution.py:310
  63.0 80.7 %copy-start.1 = (f32[16,4096]{1,0:T(8,128)}, f32[16,4096]{1,0:T(8,128)S(1)}, u32[]{:S(2)}) copy-start(f32[16,4096]{1,0:T(8,128)S(1)} %get-tuple-element.28.hidden) | copy-start | bytes 786436
  63.1 5.7 %collective-permute-start.4 = (bf16[16,4096]{1,0:T(8,128)(2,1)S(1)}, bf16[16,4096]{1,0:T(8,128)(2,1)S(1)}, u32[]{:S(2)}, u32[]{:S(2)}) collective-permute-start(bf16[16,4096]{1,0:T(8,128)(2,1)S(1)} %multiply_convert_fusion), channel_id=1, source_target_pairs={{0,1},{1,2},{2,3},{3,0},{4,7},{5,4},{6,5},{7,6},{8,9},{9,10},{10,1... | collective-permute-start | bytes 393224 | tf_op jit(solution)/shard_map/ppermute | solution.py:322
  68.8 5.6 %collective-permute-start.5 = (bf16[16,4096]{1,0:T(8,128)(2,1)S(1)}, bf16[16,4096]{1,0:T(8,128)(2,1)S(1)}, u32[]{:S(2)}, u32[]{:S(2)}) collective-permute-start(bf16[16,4096]{1,0:T(8,128)(2,1)S(1)} %collective-permute-done.4), channel_id=1, source_target_pairs={{0,1},{1,2},{2,3},{3,0},{4,7},{5,4},{6,5},{7,6},{8,9},{9,10},{10,1... | collective-permute-start | bytes 393224 | tf_op jit(solution)/shard_map/ppermute | solution.py:322
  74.4 5.6 %collective-permute-start.6 = (bf16[16,4096]{1,0:T(8,128)(2,1)S(1)}, bf16[16,4096]{1,0:T(8,128)(2,1)S(1)}, u32[]{:S(2)}, u32[]{:S(2)}) collective-permute-start(bf16[16,4096]{1,0:T(8,128)(2,1)S(1)} %collective-permute-done.5), channel_id=1, source_target_pairs={{0,1},{1,2},{2,3},{3,0},{4,7},{5,4},{6,5},{7,6},{8,9},{9,10},{10,1... | collective-permute-start | bytes 393224 | tf_op jit(solution)/shard_map/ppermute | solution.py:322
  77.4 72.9 %collective-permute-start.12 = (bf16[1,4096,384]{2,1,0:T(8,128)(2,1)}, bf16[1,4096,384]{2,1,0:T(8,128)(2,1)}, u32[]{:S(2)}, u32[]{:S(2)}) collective-permute-start(bf16[1,4096,384]{2,1,0:T(8,128)(2,1)} %refs_1_.1), channel_id=1, source_target_pairs={{0,4},{2,6},{5,1},{7,3},{8,12},{10,14},{13,9},{15,11},{16,20},{18,... | collective-permute-start | bytes 9437192 | tf_op jit(solution)/shard_map/ppermute | solution.py:310
  80.0 59.7 %collective-permute-start.10 = (bf16[1,96,4096]{2,1,0:T(8,128)(2,1)S(1)}, bf16[1,96,4096]{2,1,0:T(8,128)(2,1)S(1)}, u32[]{:S(2)}, u32[]{:S(2)}) collective-permute-start(bf16[1,96,4096]{2,1,0:T(8,128)(2,1)S(1)} %slice.15), channel_id=1, source_target_pairs={{1,0},{3,2},{4,5},{6,7},{9,8},{11,10},{12,13},{14,15},{17,16},{19,... | collective-permute-start | bytes 2359304 | tf_op jit(solution)/shard_map/ppermute | solution.py:310
  106.1 45.5 %collective-permute-start.13 = (bf16[1,384,4096]{2,1,0:T(8,128)(2,1)}, bf16[1,384,4096]{2,1,0:T(8,128)(2,1)}, u32[]{:S(2)}, u32[]{:S(2)}) collective-permute-start(bf16[1,384,4096]{2,1,0:T(8,128)(2,1)} %refs_2_.1), channel_id=1, source_target_pairs={{0,4},{2,6},{5,1},{7,3},{8,12},{10,14},{13,9},{15,11},{16,20},{18,... | collective-permute-start | bytes 9437192 | tf_op jit(solution)/shard_map/ppermute | solution.py:310
  139.7 33.4 %copy-start.3 = (bf16[1,96,4096]{2,1,0:T(8,128)(2,1)}, bf16[1,96,4096]{2,1,0:T(8,128)(2,1)S(1)}, u32[]{:S(2)}) copy-start(bf16[1,96,4096]{2,1,0:T(8,128)(2,1)S(1)} %collective-permute-done.10.refs_6_) | copy-start | bytes 2359300
  139.7 33.4 %collective-permute-start.14 = (bf16[1,4096,384]{2,1,0:T(8,128)(2,1)}, bf16[1,4096,384]{2,1,0:T(8,128)(2,1)}, u32[]{:S(2)}, u32[]{:S(2)}) collective-permute-start(bf16[1,4096,384]{2,1,0:T(8,128)(2,1)} %collective-permute-done.7.refs_3_), channel_id=1, source_target_pairs={{0,4},{2,6},{5,1},{7,3},{8,12},{10,14},{13,9},{15,11},{16,20},{18,... | collective-permute-start | bytes 9437192 | tf_op jit(solution)/shard_map/ppermute | solution.py:310
  141.0 32.1 %collective-permute-start.15 = (bf16[1,4096,384]{2,1,0:T(8,128)(2,1)}, bf16[1,4096,384]{2,1,0:T(8,128)(2,1)}, u32[]{:S(2)}, u32[]{:S(2)}) collective-permute-start(bf16[1,4096,384]{2,1,0:T(8,128)(2,1)} %collective-permute-done.8.refs_4_), channel_id=1, source_target_pairs={{0,4},{2,6},{5,1},{7,3},{8,12},{10,14},{13,9},{15,11},{16,20},{18,... | collective-permute-start | bytes 9437192 | tf_op jit(solution)/shard_map/ppermute | solution.py:310
  142.3 30.7 %collective-permute-start.16 = (bf16[1,288,4096]{2,1,0:T(8,128)(2,1)}, bf16[1,288,4096]{2,1,0:T(8,128)(2,1)}, u32[]{:S(2)}, u32[]{:S(2)}) collective-permute-start(bf16[1,288,4096]{2,1,0:T(8,128)(2,1)} %collective-permute-done.9.refs_5_), channel_id=1, source_target_pairs={{0,4},{2,6},{5,1},{7,3},{8,12},{10,14},{13,9},{15,11},{16,20},{18,... | collective-permute-start | bytes 7077896 | tf_op jit(solution)/shard_map/ppermute | solution.py:310
  143.6 29.4 %all-to-all-start.2 = ((bf16[16,16,4096]{2,1,0:T(8,128)(2,1)}), bf16[16,16,4096]{2,1,0:T(8,128)(2,1)}, u32[]{:S(2)}, u32[]{:S(2)}) async-start(bf16[16,16,4096]{2,1,0:T(8,128)(2,1)} %bitcast.7), calls=%async_computation.2 | async-start | bytes 4194304 | tf_op jit(solution)/shard_map/all_to_all | solution.py:400
  150.3 10.9 %collective-permute-start.17 = (bf16[1,96,4096]{2,1,0:T(8,128)(2,1)S(1)}, bf16[1,96,4096]{2,1,0:T(8,128)(2,1)S(1)}, u32[]{:S(2)}, u32[]{:S(2)}) collective-permute-start(bf16[1,96,4096]{2,1,0:T(8,128)(2,1)S(1)} %collective-permute-done.10.refs_6_), channel_id=1, source_target_pairs={{0,4},{2,6},{5,1},{7,3},{8,12},{10,14},{13,9},{15,11},{16,20},{18,... | collective-permute-start | bytes 2359304 | tf_op jit(solution)/shard_map/ppermute | solution.py:310
  184.7 44.4 %all-to-all-start.3 = ((bf16[64,4,4096]{2,1,0:T(4,128)(2,1)}), bf16[64,4,4096]{2,1,0:T(4,128)(2,1)}, u32[]{:S(2)}, u32[]{:S(2)}) async-start(bf16[64,4,4096]{2,1,0:T(4,128)(2,1)} %expert_ffn.1), calls=%async_computation.3 | async-start | bytes 4194304 | tf_op jit(solution)/shard_map/all_to_all | solution.py:422
  (5 other events, 47.3 us)

commit v9 on v8

--- a/solution.py
+++ b/solution.py
@@ -14,9 +14,10 @@
 HD = 128
 CAP = 4
 ATTN_STEPS = 2
-OUT_STEPS = 2
-CUTS = 8
-X_CUTS = 4
+OUT_STEPS = 4
+CUTS = 1
+X_CUTS = 1
+AHEAD = 2
 COMBINE_STEPS = 2
 
 
@@ -166,37 +167,42 @@
             down_copy(hf + second[2].shape[1], second[3], step),
         )
 
-    def start(first, second):
-        for side, source in ((0, first), (1, second)):
-            for part in range(2):
-                for cut in range(CUTS):
-                    in_copy(side, source, part, cut).start()
+    def slab(first, second, at):
+        for cut in range(CUTS):
+            in_copy(at // 2, (first, second)[at // 2], at % 2, cut).start()
+
+    def downs(first, second, at):
         for step in range(OUT_STEPS):
             for copy in down_copies(first, second, step):
                 copy.start()
 
+    def start(task, at):
+        @pl.when(flag[0] == 1)
+        def _():
+            task(own, crossed, at)
+
+        @pl.when(flag[0] != 1)
+        def _():
+            task(near, far, at)
+
     for cut in range(X_CUTS):
         x_copy(cut).start()
-
-    @pl.when(flag[0] == 1)
-    def _():
-        start(own, crossed)
-
-    @pl.when(flag[0] != 1)
-    def _():
-        start(near, far)
-
+    for at in range(AHEAD):
+        start(slab, at)
     for cut in range(X_CUTS):
         x_copy(cut).wait()
     acts = []
     for side in range(2):
         vals = []
         for part in range(2):
+            at = 2 * side + part
             for cut in range(CUTS):
                 in_copy(side, own, part, cut).wait()
-            vals.append(
-                jnp.dot(x_buf[...], in_buf[2 * side + part], preferred_element_type=jnp.float32)
-            )
+            if at + AHEAD < 4:
+                start(slab, at + AHEAD)
+            elif at + AHEAD == 4:
+                start(downs, 0)
+            vals.append(jnp.dot(x_buf[...], in_buf[at], preferred_element_type=jnp.float32))
         gate_val, up_val = vals
         acts.append((gate_val / (1.0 + jnp.exp(-gate_val)) * up_val).astype(jnp.bfloat16))
     act = jnp.concatenate(acts, axis=1)

time: 234 us -> 233 us (level)
  no operation moved by 1% of the time
where the time goes in v9:
time: 233 us; the launch traced here: 231 us
  waiting for transfers between devices  107 us (46%)
  starting transfers between devices  75.1 us (32%)
  Pallas kernels  18.8 us (8%)
  blocking collectives  15.3 us (7%)
  matrix products  7.02 us (3%)
  local copies, waits for them, and re-layouts  6.19 us (3%)
    ppermute x11, waiting for transfers between devices, moved(): return lax.ppermute(slab, ('core', 'dp'), pairs)  59.5 us
    ppermute x11, starting transfers between devices, moved(): return lax.ppermute(slab, ('core', 'dp'), pairs)  26.5 us
    all_to_all x1, waiting for transfers between devices, local(): lax.all_to_all(produced, ('chip', 'dp'), split_axis=0, concat_axis=0, til...  26.3 us
    ppermute x6, starting transfers between devices, gathered(): blocks.append(lax.ppermute(blocks[-1], ('core', 'dp'), ring))  20.4 us
    all_to_all x1, starting transfers between devices, local(): lax.all_to_all(produced, ('chip', 'dp'), split_axis=0, concat_axis=0, til...  16.3 us
    all_to_all x1, blocking collectives, local(): lax.all_to_all(sent, 'chip', split_axis=0, concat_axis=0, tiled=True)  15.3 us
    all_to_all x1, waiting for transfers between devices, local(): lax.all_to_all(outgoing.reshape(chips, slots, D), 'chip', split_axis=0, c...  11.8 us
    pallas_call x1, Pallas kernels, expert_ffn(): pl.pallas_call(ffn_kernel, out_shape=jax.ShapeDtypeStruct((count // CAP,...  11.1 us
  transfers between devices with their start and end apart: 21, of which 11 were waited for; matrix products, arithmetic and copies ran while one was open for 4% of the time, Pallas kernels for 2%

profile of v9, /device:TPU:1, one launch (start us, length us, event | category | flops | bytes accessed | tf_op | source)
XLA Modules:
  0.0 231.2 jit_solution(14816643681995536998)
XLA Ops:
  1.4 5.0 %attention.1 = bf16[16,16,512]{2,1,0:T(8,128)(2,1)} custom-call(s32[1]{0:T(128)} %bitcast.swap, s32[16]{0:T(128)} %lengths.1, bf16[16,8192]{1,0:T(8,128)(2,1)} %q_in.1, bf16[16,512]{1,0:T(8,128)(2,1)} %nk_in.1, bf16[16,512]{1,0:T(8,128)(2,1)} %nv_in.1, bf16[16,128,512]{2,1,0:T(8,128)(2,1)} %keys.1, bf16[16,128,512]{2,1,0:T(8,128)(2,1)} %values.1), custom_call_target="tpu_custom_call" | custom-call | flops 134217728 | bytes 4194304 | tf_op jit(solution)/shard_map/attention/pallas_call | solution.py:112
  6.4 15.3 %all_to_all.20 = bf16[16,16,512]{2,1,0:T(8,128)(2,1)S(1)} all-to-all(bf16[16,16,512]{2,1,0:T(8,128)(2,1)} %attention.1), channel_id=1, replica_groups=mesh['chip'=16,'core'=2,'dp'=4] {'chip'}, dimensions={0} | all-to-all | bytes 524288 | tf_op jit(solution)/shard_map/all_to_all | solution.py:345
  22.4 3.7 %fusion = bf16[256,4096]{1,0:T(8,128)(2,1)} fusion(f32[256,4096]{1,0:T(8,128)S(1)} %fusion.12, bf16[256,4096]{1,0:T(8,128)(2,1)} %collective-permute-done, bf16[256,512]{1,0:T(8,128)(2,1)S(1)} %bitcast.19), kind=kOutput, calls=%fused_computation.1 | convolution fusion | flops 538968064 | bytes 8519680 | tf_op jit(solution)/shard_map/dot_general | solution.py:348
  26.1 3.8 %all-to-all-start.1 = ((bf16[16,16,4096]{2,1,0:T(8,128)(2,1)}), bf16[16,16,4096]{2,1,0:T(8,128)(2,1)S(1)}, u32[]{:S(2)}, u32[]{:S(2)}) async-start(bf16[16,16,4096]{2,1,0:T(8,128)(2,1)} %bitcast.17), calls=%async_computation.1 | async-start | bytes 4194304 | tf_op jit(solution)/shard_map/all_to_all | solution.py:388
  30.0 5.2 %collective-permute-start.7 = (bf16[1,4096,384]{2,1,0:T(8,128)(2,1)}, bf16[1,4096,384]{2,1,0:T(8,128)(2,1)}, u32[]{:S(2)}, u32[]{:S(2)}) collective-permute-start(bf16[1,4096,384]{2,1,0:T(8,128)(2,1)} %refs_0_.1), channel_id=1, source_target_pairs={{1,0},{3,2},{4,5},{6,7},{9,8},{11,10},{12,13},{14,15},{17,16},{19,... | collective-permute-start | bytes 9437192 | tf_op jit(solution)/shard_map/ppermute | solution.py:316
  36.5 6.0 %collective-permute-start.1 = (s32[16,8]{0,1:T(8,128)S(1)}, s32[16,8]{0,1:T(8,128)S(1)}, u32[]{:S(2)}, u32[]{:S(2)}) collective-permute-start(s32[16,8]{0,1:T(8,128)S(1)} %copy-done.7), channel_id=1, source_target_pairs={{0,1},{1,2},{2,3},{3,0},{4,7},{5,4},{6,5},{7,6},{8,9},{9,10},{10,1... | collective-permute-start | bytes 1544 | tf_op jit(solution)/shard_map/ppermute | solution.py:328
  43.3 3.2 %collective-permute-start.2 = (s32[16,8]{0,1:T(8,128)S(1)}, s32[16,8]{0,1:T(8,128)S(1)}, u32[]{:S(2)}, u32[]{:S(2)}) collective-permute-start(s32[16,8]{0,1:T(8,128)S(1)} %collective-permute-done.1), channel_id=1, source_target_pairs={{0,1},{1,2},{2,3},{3,0},{4,7},{5,4},{6,5},{7,6},{8,9},{9,10},{10,1... | collective-permute-start | bytes 1544 | tf_op jit(solution)/shard_map/ppermute | solution.py:328
  47.2 3.2 %collective-permute-start.3 = (s32[16,8]{0,1:T(8,128)S(1)}, s32[16,8]{0,1:T(8,128)S(1)}, u32[]{:S(2)}, u32[]{:S(2)}) collective-permute-start(s32[16,8]{0,1:T(8,128)S(1)} %collective-permute-done.2), channel_id=1, source_target_pairs={{0,1},{1,2},{2,3},{3,0},{4,7},{5,4},{6,5},{7,6},{8,9},{9,10},{10,1... | collective-permute-start | bytes 1544 | tf_op jit(solution)/shard_map/ppermute | solution.py:328
  51.3 3.0 %collective-permute-start.8 = (bf16[1,4096,384]{2,1,0:T(8,128)(2,1)}, bf16[1,4096,384]{2,1,0:T(8,128)(2,1)}, u32[]{:S(2)}, u32[]{:S(2)}) collective-permute-start(bf16[1,4096,384]{2,1,0:T(8,128)(2,1)} %refs_1_.1), channel_id=1, source_target_pairs={{1,0},{3,2},{4,5},{6,7},{9,8},{11,10},{12,13},{14,15},{17,16},{19,... | collective-permute-start | bytes 9437192 | tf_op jit(solution)/shard_map/ppermute | solution.py:316
  55.8 3.3 %slice.14 = bf16[1,288,4096]{2,1,0:T(8,128)(2,1)} slice(bf16[1,384,4096]{2,1,0:T(8,128)(2,1)} %refs_2_.1), slice={[0:1], [0:288], [0:4096]} | slice | bytes 4718592 | tf_op jit(solution)/shard_map/slice | solution.py:384
  59.1 2.8 %collective-permute-start.9 = (bf16[1,288,4096]{2,1,0:T(8,128)(2,1)}, bf16[1,288,4096]{2,1,0:T(8,128)(2,1)}, u32[]{:S(2)}, u32[]{:S(2)}) collective-permute-start(bf16[1,288,4096]{2,1,0:T(8,128)(2,1)} %slice.14), channel_id=1, source_target_pairs={{1,0},{3,2},{4,5},{6,7},{9,8},{11,10},{12,13},{14,15},{17,16},{19,... | collective-permute-start | bytes 7077896 | tf_op jit(solution)/shard_map/ppermute | solution.py:316
  65.0 3.7 %collective-permute-done.4 = bf16[16,4096]{1,0:T(8,128)(2,1)S(1)} collective-permute-done((bf16[16,4096]{1,0:T(8,128)(2,1)S(1)}, bf16[16,4096]{1,0:T(8,128)(2,1)S(1)}, u32[]{:S(2)}, u32[]{:S(2)}) %collective-permute-start.4) | collective-permute-done | bytes 131104 | tf_op jit(solution)/shard_map/ppermute | solution.py:328
  68.8 3.0 %collective-permute-start.5 = (bf16[16,4096]{1,0:T(8,128)(2,1)S(1)}, bf16[16,4096]{1,0:T(8,128)(2,1)S(1)}, u32[]{:S(2)}, u32[]{:S(2)}) collective-permute-start(bf16[16,4096]{1,0:T(8,128)(2,1)S(1)} %collective-permute-done.4), channel_id=1, source_target_pairs={{0,1},{1,2},{2,3},{3,0},{4,7},{5,4},{6,5},{7,6},{8,9},{9,10},{10,1... | collective-permute-start | bytes 393224 | tf_op jit(solution)/shard_map/ppermute | solution.py:328
  74.4 3.0 %collective-permute-start.6 = (bf16[16,4096]{1,0:T(8,128)(2,1)S(1)}, bf16[16,4096]{1,0:T(8,128)(2,1)S(1)}, u32[]{:S(2)}, u32[]{:S(2)}) collective-permute-start(bf16[16,4096]{1,0:T(8,128)(2,1)S(1)} %collective-permute-done.5), channel_id=1, source_target_pairs={{0,1},{1,2},{2,3},{3,0},{4,7},{5,4},{6,5},{7,6},{8,9},{9,10},{10,1... | collective-permute-start | bytes 393224 | tf_op jit(solution)/shard_map/ppermute | solution.py:328
  80.0 6.3 %collective-permute-start.10 = (bf16[1,96,4096]{2,1,0:T(8,128)(2,1)S(1)}, bf16[1,96,4096]{2,1,0:T(8,128)(2,1)S(1)}, u32[]{:S(2)}, u32[]{:S(2)}) collective-permute-start(bf16[1,96,4096]{2,1,0:T(8,128)(2,1)S(1)} %slice.15), channel_id=1, source_target_pairs={{1,0},{3,2},{4,5},{6,7},{9,8},{11,10},{12,13},{14,15},{17,16},{19,... | collective-permute-start | bytes 2359304 | tf_op jit(solution)/shard_map/ppermute | solution.py:316
  88.4 17.7 %collective-permute-done.8.refs_4_ = bf16[1,4096,384]{2,1,0:T(8,128)(2,1)} collective-permute-done((bf16[1,4096,384]{2,1,0:T(8,128)(2,1)}, bf16[1,4096,384]{2,1,0:T(8,128)(2,1)}, u32[]{:S(2)}, u32[]{:S(2)}) %collective-permute-start.8) | collective-permute-done | bytes 3145760 | tf_op jit(solution)/shard_map/ppermute | solution.py:316
  107.4 32.3 %collective-permute-done.10.refs_6_ = bf16[1,96,4096]{2,1,0:T(8,128)(2,1)S(1)} collective-permute-done((bf16[1,96,4096]{2,1,0:T(8,128)(2,1)S(1)}, bf16[1,96,4096]{2,1,0:T(8,128)(2,1)S(1)}, u32[]{:S(2)}, u32[]{:S(2)}) %collective-permute-start.10) | collective-permute-done | bytes 786464 | tf_op jit(solution)/shard_map/ppermute | solution.py:316
  143.6 6.6 %all-to-all-start.2 = ((bf16[16,16,4096]{2,1,0:T(8,128)(2,1)}), bf16[16,16,4096]{2,1,0:T(8,128)(2,1)}, u32[]{:S(2)}, u32[]{:S(2)}) async-start(bf16[16,16,4096]{2,1,0:T(8,128)(2,1)} %bitcast.7), calls=%async_computation.2 | async-start | bytes 4194304 | tf_op jit(solution)/shard_map/all_to_all | solution.py:406
  151.8 9.4 %collective-permute-done.17.refs_13_ = bf16[1,96,4096]{2,1,0:T(8,128)(2,1)S(1)} collective-permute-done((bf16[1,96,4096]{2,1,0:T(8,128)(2,1)S(1)}, bf16[1,96,4096]{2,1,0:T(8,128)(2,1)S(1)}, u32[]{:S(2)}, u32[]{:S(2)}) %collective-permute-start.17) | collective-permute-done | bytes 786464 | tf_op jit(solution)/shard_map/ppermute | solution.py:316
  161.2 11.8 %all-to-all-done.2 = bf16[16,16,4096]{2,1,0:T(8,128)(2,1)} async-done(((bf16[16,16,4096]{2,1,0:T(8,128)(2,1)}), bf16[16,16,4096]{2,1,0:T(8,128)(2,1)}, u32[]{:S(2)}, u32[]{:S(2)}) %all-to-all-start.2) | async-done | bytes 2097184 | tf_op jit(solution)/shard_map/all_to_all | solution.py:406
  173.1 11.1 %expert_ffn.1 = bf16[64,4,4096]{2,1,0:T(4,128)(2,1)} custom-call(s32[1]{0:T(128)} %bitcast.5.flag, bf16[256,4096]{1,0:T(8,128)(2,1)} %bitcast.8.rows_in, bf16[1,4096,384]{2,1,0:T(8,128)(2,1)} %refs_0_.1, bf16[1,4096,384]{2,1,0:T(8,128)(2,1)} %refs_1_.1, bf16[1,384,4096]{2,1,0:T(8,128)(2,1)} %refs_2_.1, bf16[1,4096,384]{2,1,0:T(8,128)(2,1)} %collective-permute-done.7.refs_3_, ...), custom_call_target="tpu_custom_call" | custom-call | flops 4831838208 | bytes 23068672 | tf_op jit(solution)/shard_map/expert_ffn/pallas_call | solution.py:233
  184.2 16.3 %all-to-all-start.3 = ((bf16[64,4,4096]{2,1,0:T(4,128)(2,1)}), bf16[64,4,4096]{2,1,0:T(4,128)(2,1)}, u32[]{:S(2)}, u32[]{:S(2)}) async-start(bf16[64,4,4096]{2,1,0:T(4,128)(2,1)} %expert_ffn.1), calls=%async_computation.3 | async-start | bytes 4194304 | tf_op jit(solution)/shard_map/all_to_all | solution.py:428
  202.3 26.3 %all-to-all-done.3.rows_in = bf16[64,4,4096]{2,1,0:T(4,128)(2,1)} async-done(((bf16[64,4,4096]{2,1,0:T(4,128)(2,1)}), bf16[64,4,4096]{2,1,0:T(4,128)(2,1)}, u32[]{:S(2)}, u32[]{:S(2)}) %all-to-all-start.3) | async-done | bytes 2097184 | tf_op jit(solution)/shard_map/all_to_all | solution.py:428
  228.6 2.7 %combined.1 = f32[16,4096]{1,0:T(8,128)} custom-call(bf16[16,256]{1,0:T(8,128)(2,1)} %copy.31.weights, bf16[64,4,4096]{2,1,0:T(4,128)(2,1)} %all-to-all-done.3.rows_in, f32[16,4096]{1,0:T(8,128)} %copy-done.1), custom_call_target="tpu_custom_call" | custom-call | flops 33554432 | bytes 2097152 | tf_op jit(solution)/shard_map/combined/pallas_call | solution.py:266
  (70 shorter events, 25.9 us)
Async XLA Ops:
  0.0 200.6 %copy-start = (bf16[4096,64]{0,1:T(8,128)(2,1)S(1)}, bf16[4096,64]{0,1:T(8,128)(2,1)}, u32[]{:S(2)}) copy-start(bf16[4096,64]{0,1:T(8,128)(2,1)} %param.23) | copy-start | bytes 1572868
  0.0 22.4 %collective-permute-start = (bf16[256,4096]{1,0:T(8,128)(2,1)}, bf16[256,4096]{1,0:T(8,128)(2,1)}, u32[]{:S(2)}, u32[]{:S(2)}) collective-permute-start(bf16[256,4096]{1,0:T(8,128)(2,1)} %param.21), channel_id=1, source_target_pairs={{0,4},{4,0},{1,5},{5,1},{2,6},{6,2},{3,7},{7,3},{8,12},{12,8},{9,1... | collective-permute-start | bytes 6291464 | tf_op jit(solution)/shard_map/ppermute | solution.py:30
  26.1 35.8 %all-to-all-start.1 = ((bf16[16,16,4096]{2,1,0:T(8,128)(2,1)}), bf16[16,16,4096]{2,1,0:T(8,128)(2,1)S(1)}, u32[]{:S(2)}, u32[]{:S(2)}) async-start(bf16[16,16,4096]{2,1,0:T(8,128)(2,1)} %bitcast.17), calls=%async_computation.1 | async-start | bytes 4194304 | tf_op jit(solution)/shard_map/all_to_all | solution.py:388
  30.0 47.4 %collective-permute-start.7 = (bf16[1,4096,384]{2,1,0:T(8,128)(2,1)}, bf16[1,4096,384]{2,1,0:T(8,128)(2,1)}, u32[]{:S(2)}, u32[]{:S(2)}) collective-permute-start(bf16[1,4096,384]{2,1,0:T(8,128)(2,1)} %refs_0_.1), channel_id=1, source_target_pairs={{1,0},{3,2},{4,5},{6,7},{9,8},{11,10},{12,13},{14,15},{17,16},{19,... | collective-permute-start | bytes 9437192 | tf_op jit(solution)/shard_map/ppermute | solution.py:316
  35.2 107.1 %collective-permute-start.11 = (bf16[1,4096,384]{2,1,0:T(8,128)(2,1)}, bf16[1,4096,384]{2,1,0:T(8,128)(2,1)}, u32[]{:S(2)}, u32[]{:S(2)}) collective-permute-start(bf16[1,4096,384]{2,1,0:T(8,128)(2,1)} %refs_0_.1), channel_id=1, source_target_pairs={{0,4},{2,6},{5,1},{7,3},{8,12},{10,14},{13,9},{15,11},{16,20},{18,... | collective-permute-start | bytes 9437192 | tf_op jit(solution)/shard_map/ppermute | solution.py:316
  36.5 6.8 %collective-permute-start.1 = (s32[16,8]{0,1:T(8,128)S(1)}, s32[16,8]{0,1:T(8,128)S(1)}, u32[]{:S(2)}, u32[]{:S(2)}) collective-permute-start(s32[16,8]{0,1:T(8,128)S(1)} %copy-done.7), channel_id=1, source_target_pairs={{0,1},{1,2},{2,3},{3,0},{4,7},{5,4},{6,5},{7,6},{8,9},{9,10},{10,1... | collective-permute-start | bytes 1544 | tf_op jit(solution)/shard_map/ppermute | solution.py:328
  43.3 4.0 %collective-permute-start.2 = (s32[16,8]{0,1:T(8,128)S(1)}, s32[16,8]{0,1:T(8,128)S(1)}, u32[]{:S(2)}, u32[]{:S(2)}) collective-permute-start(s32[16,8]{0,1:T(8,128)S(1)} %collective-permute-done.1), channel_id=1, source_target_pairs={{0,1},{1,2},{2,3},{3,0},{4,7},{5,4},{6,5},{7,6},{8,9},{9,10},{10,1... | collective-permute-start | bytes 1544 | tf_op jit(solution)/shard_map/ppermute | solution.py:328
  47.2 4.0 %collective-permute-start.3 = (s32[16,8]{0,1:T(8,128)S(1)}, s32[16,8]{0,1:T(8,128)S(1)}, u32[]{:S(2)}, u32[]{:S(2)}) collective-permute-start(s32[16,8]{0,1:T(8,128)S(1)} %collective-permute-done.2), channel_id=1, source_target_pairs={{0,1},{1,2},{2,3},{3,0},{4,7},{5,4},{6,5},{7,6},{8,9},{9,10},{10,1... | collective-permute-start | bytes 1544 | tf_op jit(solution)/shard_map/ppermute | solution.py:328
  51.3 54.8 %collective-permute-start.8 = (bf16[1,4096,384]{2,1,0:T(8,128)(2,1)}, bf16[1,4096,384]{2,1,0:T(8,128)(2,1)}, u32[]{:S(2)}, u32[]{:S(2)}) collective-permute-start(bf16[1,4096,384]{2,1,0:T(8,128)(2,1)} %refs_1_.1), channel_id=1, source_target_pairs={{1,0},{3,2},{4,5},{6,7},{9,8},{11,10},{12,13},{14,15},{17,16},{19,... | collective-permute-start | bytes 9437192 | tf_op jit(solution)/shard_map/ppermute | solution.py:316
  59.1 81.9 %collective-permute-start.9 = (bf16[1,288,4096]{2,1,0:T(8,128)(2,1)}, bf16[1,288,4096]{2,1,0:T(8,128)(2,1)}, u32[]{:S(2)}, u32[]{:S(2)}) collective-permute-start(bf16[1,288,4096]{2,1,0:T(8,128)(2,1)} %slice.14), channel_id=1, source_target_pairs={{1,0},{3,2},{4,5},{6,7},{9,8},{11,10},{12,13},{14,15},{17,16},{19,... | collective-permute-start | bytes 7077896 | tf_op jit(solution)/shard_map/ppermute | solution.py:316
  63.0 80.7 %copy-start.1 = (f32[16,4096]{1,0:T(8,128)}, f32[16,4096]{1,0:T(8,128)S(1)}, u32[]{:S(2)}) copy-start(f32[16,4096]{1,0:T(8,128)S(1)} %get-tuple-element.28.hidden) | copy-start | bytes 786436
  63.1 5.7 %collective-permute-start.4 = (bf16[16,4096]{1,0:T(8,128)(2,1)S(1)}, bf16[16,4096]{1,0:T(8,128)(2,1)S(1)}, u32[]{:S(2)}, u32[]{:S(2)}) collective-permute-start(bf16[16,4096]{1,0:T(8,128)(2,1)S(1)} %multiply_convert_fusion), channel_id=1, source_target_pairs={{0,1},{1,2},{2,3},{3,0},{4,7},{5,4},{6,5},{7,6},{8,9},{9,10},{10,1... | collective-permute-start | bytes 393224 | tf_op jit(solution)/shard_map/ppermute | solution.py:328
  68.8 5.6 %collective-permute-start.5 = (bf16[16,4096]{1,0:T(8,128)(2,1)S(1)}, bf16[16,4096]{1,0:T(8,128)(2,1)S(1)}, u32[]{:S(2)}, u32[]{:S(2)}) collective-permute-start(bf16[16,4096]{1,0:T(8,128)(2,1)S(1)} %collective-permute-done.4), channel_id=1, source_target_pairs={{0,1},{1,2},{2,3},{3,0},{4,7},{5,4},{6,5},{7,6},{8,9},{9,10},{10,1... | collective-permute-start | bytes 393224 | tf_op jit(solution)/shard_map/ppermute | solution.py:328
  74.4 5.6 %collective-permute-start.6 = (bf16[16,4096]{1,0:T(8,128)(2,1)S(1)}, bf16[16,4096]{1,0:T(8,128)(2,1)S(1)}, u32[]{:S(2)}, u32[]{:S(2)}) collective-permute-start(bf16[16,4096]{1,0:T(8,128)(2,1)S(1)} %collective-permute-done.5), channel_id=1, source_target_pairs={{0,1},{1,2},{2,3},{3,0},{4,7},{5,4},{6,5},{7,6},{8,9},{9,10},{10,1... | collective-permute-start | bytes 393224 | tf_op jit(solution)/shard_map/ppermute | solution.py:328
  77.4 72.9 %collective-permute-start.12 = (bf16[1,4096,384]{2,1,0:T(8,128)(2,1)}, bf16[1,4096,384]{2,1,0:T(8,128)(2,1)}, u32[]{:S(2)}, u32[]{:S(2)}) collective-permute-start(bf16[1,4096,384]{2,1,0:T(8,128)(2,1)} %refs_1_.1), channel_id=1, source_target_pairs={{0,4},{2,6},{5,1},{7,3},{8,12},{10,14},{13,9},{15,11},{16,20},{18,... | collective-permute-start | bytes 9437192 | tf_op jit(solution)/shard_map/ppermute | solution.py:316
  80.0 59.7 %collective-permute-start.10 = (bf16[1,96,4096]{2,1,0:T(8,128)(2,1)S(1)}, bf16[1,96,4096]{2,1,0:T(8,128)(2,1)S(1)}, u32[]{:S(2)}, u32[]{:S(2)}) collective-permute-start(bf16[1,96,4096]{2,1,0:T(8,128)(2,1)S(1)} %slice.15), channel_id=1, source_target_pairs={{1,0},{3,2},{4,5},{6,7},{9,8},{11,10},{12,13},{14,15},{17,16},{19,... | collective-permute-start | bytes 2359304 | tf_op jit(solution)/shard_map/ppermute | solution.py:316
  106.1 45.7 %collective-permute-start.13 = (bf16[1,384,4096]{2,1,0:T(8,128)(2,1)}, bf16[1,384,4096]{2,1,0:T(8,128)(2,1)}, u32[]{:S(2)}, u32[]{:S(2)}) collective-permute-start(bf16[1,384,4096]{2,1,0:T(8,128)(2,1)} %refs_2_.1), channel_id=1, source_target_pairs={{0,4},{2,6},{5,1},{7,3},{8,12},{10,14},{13,9},{15,11},{16,20},{18,... | collective-permute-start | bytes 9437192 | tf_op jit(solution)/shard_map/ppermute | solution.py:316
  139.7 33.4 %copy-start.3 = (bf16[1,96,4096]{2,1,0:T(8,128)(2,1)}, bf16[1,96,4096]{2,1,0:T(8,128)(2,1)S(1)}, u32[]{:S(2)}) copy-start(bf16[1,96,4096]{2,1,0:T(8,128)(2,1)S(1)} %collective-permute-done.10.refs_6_) | copy-start | bytes 2359300
  139.7 33.4 %collective-permute-start.14 = (bf16[1,4096,384]{2,1,0:T(8,128)(2,1)}, bf16[1,4096,384]{2,1,0:T(8,128)(2,1)}, u32[]{:S(2)}, u32[]{:S(2)}) collective-permute-start(bf16[1,4096,384]{2,1,0:T(8,128)(2,1)} %collective-permute-done.7.refs_3_), channel_id=1, source_target_pairs={{0,4},{2,6},{5,1},{7,3},{8,12},{10,14},{13,9},{15,11},{16,20},{18,... | collective-permute-start | bytes 9437192 | tf_op jit(solution)/shard_map/ppermute | solution.py:316
  141.0 32.1 %collective-permute-start.15 = (bf16[1,4096,384]{2,1,0:T(8,128)(2,1)}, bf16[1,4096,384]{2,1,0:T(8,128)(2,1)}, u32[]{:S(2)}, u32[]{:S(2)}) collective-permute-start(bf16[1,4096,384]{2,1,0:T(8,128)(2,1)} %collective-permute-done.8.refs_4_), channel_id=1, source_target_pairs={{0,4},{2,6},{5,1},{7,3},{8,12},{10,14},{13,9},{15,11},{16,20},{18,... | collective-permute-start | bytes 9437192 | tf_op jit(solution)/shard_map/ppermute | solution.py:316
  142.3 30.7 %collective-permute-start.16 = (bf16[1,288,4096]{2,1,0:T(8,128)(2,1)}, bf16[1,288,4096]{2,1,0:T(8,128)(2,1)}, u32[]{:S(2)}, u32[]{:S(2)}) collective-permute-start(bf16[1,288,4096]{2,1,0:T(8,128)(2,1)} %collective-permute-done.9.refs_5_), channel_id=1, source_target_pairs={{0,4},{2,6},{5,1},{7,3},{8,12},{10,14},{13,9},{15,11},{16,20},{18,... | collective-permute-start | bytes 7077896 | tf_op jit(solution)/shard_map/ppermute | solution.py:316
  143.6 29.4 %all-to-all-start.2 = ((bf16[16,16,4096]{2,1,0:T(8,128)(2,1)}), bf16[16,16,4096]{2,1,0:T(8,128)(2,1)}, u32[]{:S(2)}, u32[]{:S(2)}) async-start(bf16[16,16,4096]{2,1,0:T(8,128)(2,1)} %bitcast.7), calls=%async_computation.2 | async-start | bytes 4194304 | tf_op jit(solution)/shard_map/all_to_all | solution.py:406
  150.3 10.9 %collective-permute-start.17 = (bf16[1,96,4096]{2,1,0:T(8,128)(2,1)S(1)}, bf16[1,96,4096]{2,1,0:T(8,128)(2,1)S(1)}, u32[]{:S(2)}, u32[]{:S(2)}) collective-permute-start(bf16[1,96,4096]{2,1,0:T(8,128)(2,1)S(1)} %collective-permute-done.10.refs_6_), channel_id=1, source_target_pairs={{0,4},{2,6},{5,1},{7,3},{8,12},{10,14},{13,9},{15,11},{16,20},{18,... | collective-permute-start | bytes 2359304 | tf_op jit(solution)/shard_map/ppermute | solution.py:316
  184.2 44.3 %all-to-all-start.3 = ((bf16[64,4,4096]{2,1,0:T(4,128)(2,1)}), bf16[64,4,4096]{2,1,0:T(4,128)(2,1)}, u32[]{:S(2)}, u32[]{:S(2)}) async-start(bf16[64,4,4096]{2,1,0:T(4,128)(2,1)} %expert_ffn.1), calls=%async_computation.3 | async-start | bytes 4194304 | tf_op jit(solution)/shard_map/all_to_all | solution.py:428
  (5 other events, 47.3 us)

commit v10 on v9

--- a/solution.py
+++ b/solution.py
@@ -16,7 +16,7 @@
 ATTN_STEPS = 2
 OUT_STEPS = 4
 CUTS = 1
-X_CUTS = 1
+X_CUTS = 2
 AHEAD = 2
 COMBINE_STEPS = 2
 
@@ -135,16 +135,21 @@
     )(swap, cache_len, queries, new_keys, new_values, cache_keys, cache_values)
 
 
-def ffn_kernel(flag, rows_in, *refs):
+def ffn_kernel(flag, order, early, late, *refs):
     own, crossed, near, far = refs[0:3], refs[3:7], refs[7:10], refs[10:14]
     out, x_buf, in_buf, down_buf, y_buf, x_sem, in_sem, down_sem, y_sem = refs[14:]
     hf = own[0].shape[2]
     deep = D // CUTS
     wide = D // OUT_STEPS
+    depths = order.shape[0]
+    chips = out.shape[0] // depths
 
     def x_copy(cut):
-        part = pl.ds(cut * rows_in.shape[0] // X_CUTS, rows_in.shape[0] // X_CUTS)
-        return pltpu.make_async_copy(rows_in.at[part], x_buf.at[part], x_sem.at[cut])
+        source = (early, late)[cut]
+        deep_rows = source.shape[0]
+        return pltpu.make_async_copy(
+            source, x_buf.at[pl.ds(cut * deep_rows, deep_rows)], x_sem.at[cut]
+        )
 
     def in_copy(side, source, part, cut):
         return pltpu.make_async_copy(
@@ -213,9 +218,10 @@
             copy.wait()
         rows_out = jnp.dot(act, down_buf[:, columns], preferred_element_type=jnp.float32)
         for chunk in range(out.shape[0]):
-            y_buf[chunk, :, columns] = rows_out[chunk * CAP : (chunk + 1) * CAP].astype(
-                jnp.bfloat16
-            )
+            part, chip, turn = chunk // (2 * chips), chunk // 2 % chips, chunk % 2
+            y_buf[chip * depths + order[2 * part + turn], :, columns] = rows_out[
+                chunk * CAP : (chunk + 1) * CAP
+            ].astype(jnp.bfloat16)
         copy = pltpu.make_async_copy(
             y_buf.at[:, :, pl.ds(step * wide, wide)],
             out.at[:, :, pl.ds(step * wide, wide)],
@@ -227,14 +233,14 @@
         copy.wait()
 
 
-def expert_ffn(flag, rows_in, own, crossed, near, far):
-    count = rows_in.shape[0]
+def expert_ffn(flag, order, early, late, own, crossed, near, far):
+    count = early.shape[0] + late.shape[0]
     hf = own[0].shape[2]
     return pl.pallas_call(
         ffn_kernel,
         out_shape=jax.ShapeDtypeStruct((count // CAP, CAP, D), jnp.bfloat16),
-        in_specs=[pl.BlockSpec(memory_space=pltpu.SMEM)]
-        + [pl.BlockSpec(memory_space=pltpu.HBM)] * 15,
+        in_specs=[pl.BlockSpec(memory_space=pltpu.SMEM)] * 2
+        + [pl.BlockSpec(memory_space=pltpu.HBM)] * 16,
         out_specs=pl.BlockSpec(memory_space=pltpu.HBM),
         scratch_shapes=[
             pltpu.VMEM((count, D), jnp.bfloat16),
@@ -251,7 +257,7 @@
             flops=12 * count * D * hf, bytes_accessed=12 * D * hf + 4 * count * D, transcendentals=0
         ),
         name="expert_ffn",
-    )(flag, rows_in, *own, *crossed, *near, *far)
+    )(flag, order, early, late, *own, *crossed, *near, *far)
 
 
 def combine_kernel(weights, rows_in, hidden, out):
@@ -359,9 +365,8 @@
         before.astype(jnp.bfloat16),
         preferred_element_type=jnp.float32,
     ).astype(jnp.int32)
-    source = (depth + depths + (2 * core - 1) * (at // rows)) % depths
-    place = jnp.where(member, rank + CAP * source[None, :], -1)
-    slots = CAP * depths
+    place = jnp.where(member, rank + CAP * (at // rows % 2)[None, :], -1)
+    slots = CAP * 2
     dispatch = place[:, None, :] == jnp.arange(slots, dtype=jnp.int32)[None, :, None]
 
     chunk = jnp.arange(chips * depths, dtype=jnp.int32)
@@ -378,8 +383,9 @@
     own_slots = own_rank[:, :, None] == jnp.arange(CAP, dtype=jnp.int32)[None, None, :]
 
     partial = partial.astype(jnp.bfloat16)
+    gate_far = moved(gate_crossed, beside, partial)
     up_crossed = moved(up_slab, across, partial)
-    middle = down_slab.shape[1] // 4 * 3
+    middle = down_slab.shape[1] // 8 * 7
     held, _ = lax.optimization_barrier((down_slab, partial))
     halves = lax.optimization_barrier((held[:, :middle], held[:, middle:]))
     most = moved(halves[0], across)
@@ -394,18 +400,30 @@
     normed = (hidden * lax.rsqrt(jnp.maximum(meansq, 0.25)) * norm_gain).astype(jnp.bfloat16)
 
     blocks = gathered(normed)
-    tokens = jnp.concatenate(blocks, axis=0)
-    outgoing = jnp.dot(
-        dispatch.reshape(chips * slots, count).astype(jnp.bfloat16),
-        tokens,
-        preferred_element_type=jnp.float32,
-    ).astype(jnp.bfloat16)
-    gate_far = moved(gate_crossed, beside, outgoing)
-    up_far = moved(up_crossed, beside, outgoing)
-    down_far = [moved(half, beside, outgoing) for half in down_crossed]
-    incoming = lax.all_to_all(
-        outgoing.reshape(chips, slots, D), "chip", split_axis=0, concat_axis=0, tiled=True
-    )
+    half = count // 2
+    outgoing = [
+        jnp.dot(
+            dispatch[:, :, part * half : (part + 1) * half]
+            .reshape(chips * slots, half)
+            .astype(jnp.bfloat16),
+            jnp.concatenate(blocks[2 * part : 2 * part + 2], axis=0),
+            preferred_element_type=jnp.float32,
+        ).astype(jnp.bfloat16)
+        for part in range(2)
+    ]
+    up_far = moved(up_crossed, beside, outgoing[1])
+    down_far = [moved(half, beside, outgoing[1]) for half in down_crossed]
+    incoming = []
+    for part in range(2):
+        incoming.append(
+            lax.all_to_all(
+                outgoing[part].reshape(chips, slots, D),
+                "chip",
+                split_axis=0,
+                concat_axis=0,
+                tiled=True,
+            ).reshape(chips * slots, D)
+        )
 
     logits = jnp.dot(normed, router, preferred_element_type=jnp.float32)
     experts = router.shape[1]
@@ -419,7 +437,9 @@
 
     produced = expert_ffn(
         flag,
-        incoming.reshape(chips * slots, D),
+        (depth + depths + (2 * core - 1) * jnp.arange(depths, dtype=jnp.int32)) % depths,
+        incoming[0],
+        incoming[1],
         (gate_slab, up_slab, down_slab),
         (gate_crossed, up_crossed, *down_crossed),
         (gate_near, up_near, down_near),

time: 233 us -> 242 us (1.039)
  blocking collectives: 15.3 us -> 33.6 us
  starting transfers between devices: 75.1 us -> 66.2 us
  waiting for transfers between devices: 107 us -> 103 us
    all_to_all x0 -> x1, blocking collectives: none -> 18.3 us  [local(): lax.all_to_all(outgoing[part].reshape(chips, slots, D), 'chip', split_axi...]
    all_to_all x1, waiting for transfers between devices: 11.8 us -> 0.34 us  [local(): lax.all_to_all(outgoing[part].reshape(chips, slots, D), 'chip', split_axi...]
    ppermute x6, starting transfers between devices: 20.4 us -> 15.4 us  [gathered(): blocks.append(lax.ppermute(blocks[-1], ('core', 'dp'), ring))]
    ppermute x6, waiting for transfers between devices: 9.49 us -> 13.8 us  [gathered(): blocks.append(lax.ppermute(blocks[-1], ('core', 'dp'), ring))]
    ppermute x11, waiting for transfers between devices: 59.5 us -> 63 us  [moved(): return lax.ppermute(slab, ('core', 'dp'), pairs)]
    all_to_all x1, starting transfers between devices: 6.65 us -> 3.65 us  [local(): lax.all_to_all(outgoing[part].reshape(chips, slots, D), 'chip', split_axi...]
  transfers between devices with their start and end apart: 21 -> 21, of which waited for: 11 -> 10; matrix products, arithmetic and copies ran while one was open for 4% -> 5% of each run, Pallas kernels for 2% -> 2%
where the time goes in v10:
time: 242 us; the launch traced here: 239 us
  waiting for transfers between devices  103 us (43%)
  starting transfers between devices  66.2 us (27%)
  blocking collectives  33.6 us (14%)
  Pallas kernels  19.3 us (8%)
  local copies, waits for them, and re-layouts  7.9 us (3%)
  matrix products  6.85 us (3%)
    ppermute x11, waiting for transfers between devices, moved(): return lax.ppermute(slab, ('core', 'dp'), pairs)  63 us
    all_to_all x1, waiting for transfers between devices, local(): lax.all_to_all(produced, ('chip', 'dp'), split_axis=0, concat_axis=0, til...  26 us
    ppermute x11, starting transfers between devices, moved(): return lax.ppermute(slab, ('core', 'dp'), pairs)  24.2 us
    all_to_all x1, blocking collectives, local(): lax.all_to_all(outgoing[part].reshape(chips, slots, D), 'chip', split_axi...  18.3 us
    all_to_all x1, starting transfers between devices, local(): lax.all_to_all(produced, ('chip', 'dp'), split_axis=0, concat_axis=0, til...  17.7 us
    ppermute x6, starting transfers between devices, gathered(): blocks.append(lax.ppermute(blocks[-1], ('core', 'dp'), ring))  15.4 us
    all_to_all x1, blocking collectives, local(): lax.all_to_all(sent, 'chip', split_axis=0, concat_axis=0, tiled=True)  15.3 us
    ppermute x6, waiting for transfers between devices, gathered(): blocks.append(lax.ppermute(blocks[-1], ('core', 'dp'), ring))  13.8 us
  transfers between devices with their start and end apart: 21, of which 10 were waited for; matrix products, arithmetic and copies ran while one was open for 5% of the time, Pallas kernels for 2%

profile of v10, /device:TPU:1, one launch (start us, length us, event | category | flops | bytes accessed | tf_op | source)
XLA Modules:
  0.0 239.3 jit_solution(6665964437119788762)
XLA Ops:
  1.4 4.8 %attention.1 = bf16[16,16,512]{2,1,0:T(8,128)(2,1)} custom-call(s32[1]{0:T(128)} %bitcast.swap, s32[16]{0:T(128)} %lengths.1, bf16[16,8192]{1,0:T(8,128)(2,1)} %q_in.1, bf16[16,512]{1,0:T(8,128)(2,1)} %nk_in.1, bf16[16,512]{1,0:T(8,128)(2,1)} %nv_in.1, bf16[16,128,512]{2,1,0:T(8,128)(2,1)} %keys.1, bf16[16,128,512]{2,1,0:T(8,128)(2,1)} %values.1), custom_call_target="tpu_custom_call" | custom-call | flops 134217728 | bytes 4194304 | tf_op jit(solution)/shard_map/attention/pallas_call | solution.py:112
  6.2 15.3 %all_to_all.25 = bf16[16,16,512]{2,1,0:T(8,128)(2,1)S(1)} all-to-all(bf16[16,16,512]{2,1,0:T(8,128)(2,1)} %attention.1), channel_id=1, replica_groups=mesh['chip'=16,'core'=2,'dp'=4] {'chip'}, dimensions={0} | all-to-all | bytes 524288 | tf_op jit(solution)/shard_map/all_to_all | solution.py:351
  22.3 3.7 %fusion = bf16[256,4096]{1,0:T(8,128)(2,1)} fusion(f32[256,4096]{1,0:T(8,128)S(1)} %fusion.12, bf16[256,4096]{1,0:T(8,128)(2,1)} %collective-permute-done, bf16[256,512]{1,0:T(8,128)(2,1)S(1)} %bitcast.29), kind=kOutput, calls=%fused_computation.1 | convolution fusion | flops 538968064 | bytes 8519680 | tf_op jit(solution)/shard_map/dot_general | solution.py:354
  25.9 3.8 %all-to-all-start.1 = ((bf16[16,16,4096]{2,1,0:T(8,128)(2,1)}), bf16[16,16,4096]{2,1,0:T(8,128)(2,1)S(1)}, u32[]{:S(2)}, u32[]{:S(2)}) async-start(bf16[16,16,4096]{2,1,0:T(8,128)(2,1)} %bitcast.24), calls=%async_computation.1 | async-start | bytes 4194304 | tf_op jit(solution)/shard_map/all_to_all | solution.py:394
  29.8 5.2 %collective-permute-start.7 = (bf16[1,4096,384]{2,1,0:T(8,128)(2,1)}, bf16[1,4096,384]{2,1,0:T(8,128)(2,1)}, u32[]{:S(2)}, u32[]{:S(2)}) collective-permute-start(bf16[1,4096,384]{2,1,0:T(8,128)(2,1)} %refs_0_.1), channel_id=1, source_target_pairs={{1,0},{3,2},{4,5},{6,7},{9,8},{11,10},{12,13},{14,15},{17,16},{19,... | collective-permute-start | bytes 9437192 | tf_op jit(solution)/shard_map/ppermute | solution.py:322
  36.3 6.1 %collective-permute-start.1 = (s32[16,8]{0,1:T(8,128)S(1)}, s32[16,8]{0,1:T(8,128)S(1)}, u32[]{:S(2)}, u32[]{:S(2)}) collective-permute-start(s32[16,8]{0,1:T(8,128)S(1)} %copy-done.8), channel_id=1, source_target_pairs={{0,1},{1,2},{2,3},{3,0},{4,7},{5,4},{6,5},{7,6},{8,9},{9,10},{10,1... | collective-permute-start | bytes 1544 | tf_op jit(solution)/shard_map/ppermute | solution.py:334
  43.1 3.2 %collective-permute-start.2 = (s32[16,8]{0,1:T(8,128)S(1)}, s32[16,8]{0,1:T(8,128)S(1)}, u32[]{:S(2)}, u32[]{:S(2)}) collective-permute-start(s32[16,8]{0,1:T(8,128)S(1)} %collective-permute-done.1), channel_id=1, source_target_pairs={{0,1},{1,2},{2,3},{3,0},{4,7},{5,4},{6,5},{7,6},{8,9},{9,10},{10,1... | collective-permute-start | bytes 1544 | tf_op jit(solution)/shard_map/ppermute | solution.py:334
  47.1 3.2 %collective-permute-start.3 = (s32[16,8]{0,1:T(8,128)S(1)}, s32[16,8]{0,1:T(8,128)S(1)}, u32[]{:S(2)}, u32[]{:S(2)}) collective-permute-start(s32[16,8]{0,1:T(8,128)S(1)} %collective-permute-done.2), channel_id=1, source_target_pairs={{0,1},{1,2},{2,3},{3,0},{4,7},{5,4},{6,5},{7,6},{8,9},{9,10},{10,1... | collective-permute-start | bytes 1544 | tf_op jit(solution)/shard_map/ppermute | solution.py:334
  50.3 3.0 %collective-permute-start.8 = (bf16[1,4096,384]{2,1,0:T(8,128)(2,1)}, bf16[1,4096,384]{2,1,0:T(8,128)(2,1)}, u32[]{:S(2)}, u32[]{:S(2)}) collective-permute-start(bf16[1,4096,384]{2,1,0:T(8,128)(2,1)} %refs_1_.1), channel_id=1, source_target_pairs={{1,0},{3,2},{4,5},{6,7},{9,8},{11,10},{12,13},{14,15},{17,16},{19,... | collective-permute-start | bytes 9437192 | tf_op jit(solution)/shard_map/ppermute | solution.py:322
  55.2 3.7 %slice.22 = bf16[1,336,4096]{2,1,0:T(8,128)(2,1)} slice(bf16[1,384,4096]{2,1,0:T(8,128)(2,1)} %refs_2_.1), slice={[0:1], [0:336], [0:4096]} | slice | bytes 5505024 | tf_op jit(solution)/shard_map/slice | solution.py:390
  58.9 2.9 %collective-permute-start.9 = (bf16[1,336,4096]{2,1,0:T(8,128)(2,1)}, bf16[1,336,4096]{2,1,0:T(8,128)(2,1)}, u32[]{:S(2)}, u32[]{:S(2)}) collective-permute-start(bf16[1,336,4096]{2,1,0:T(8,128)(2,1)} %slice.22), channel_id=1, source_target_pairs={{1,0},{3,2},{4,5},{6,7},{9,8},{11,10},{12,13},{14,15},{17,16},{19,... | collective-permute-start | bytes 8257544 | tf_op jit(solution)/shard_map/ppermute | solution.py:322
  64.0 4.3 %collective-permute-done.4 = bf16[16,4096]{1,0:T(8,128)(2,1)S(1)} collective-permute-done((bf16[16,4096]{1,0:T(8,128)(2,1)S(1)}, bf16[16,4096]{1,0:T(8,128)(2,1)S(1)}, u32[]{:S(2)}, u32[]{:S(2)}) %collective-permute-start.4) | collective-permute-done | bytes 131104 | tf_op jit(solution)/shard_map/ppermute | solution.py:334
  69.1 4.9 %collective-permute-done.5 = bf16[16,4096]{1,0:T(8,128)(2,1)S(1)} collective-permute-done((bf16[16,4096]{1,0:T(8,128)(2,1)S(1)}, bf16[16,4096]{1,0:T(8,128)(2,1)S(1)}, u32[]{:S(2)}, u32[]{:S(2)}) %collective-permute-start.5) | collective-permute-done | bytes 131104 | tf_op jit(solution)/shard_map/ppermute | solution.py:334
  76.0 3.6 %collective-permute-done.6 = bf16[16,4096]{1,0:T(8,128)(2,1)S(1)} collective-permute-done((bf16[16,4096]{1,0:T(8,128)(2,1)S(1)}, bf16[16,4096]{1,0:T(8,128)(2,1)S(1)}, u32[]{:S(2)}, u32[]{:S(2)}) %collective-permute-start.6) | collective-permute-done | bytes 131104 | tf_op jit(solution)/shard_map/ppermute | solution.py:334
  79.6 4.0 %collective-permute-start.10 = (bf16[1,48,4096]{2,1,0:T(8,128)(2,1)}, bf16[1,48,4096]{2,1,0:T(8,128)(2,1)S(1)}, u32[]{:S(2)}, u32[]{:S(2)}) collective-permute-start(bf16[1,48,4096]{2,1,0:T(8,128)(2,1)} %slice.23), channel_id=1, source_target_pairs={{1,0},{3,2},{4,5},{6,7},{9,8},{11,10},{12,13},{14,15},{17,16},{19,... | collective-permute-start | bytes 1179656 | tf_op jit(solution)/shard_map/ppermute | solution.py:322
  85.0 20.9 %collective-permute-done.8.refs_4_ = bf16[1,4096,384]{2,1,0:T(8,128)(2,1)} collective-permute-done((bf16[1,4096,384]{2,1,0:T(8,128)(2,1)}, bf16[1,4096,384]{2,1,0:T(8,128)(2,1)}, u32[]{:S(2)}, u32[]{:S(2)}) %collective-permute-start.8) | collective-permute-done | bytes 3145760 | tf_op jit(solution)/shard_map/ppermute | solution.py:322
  107.2 32.4 %collective-permute-done.10.refs_6_ = bf16[1,48,4096]{2,1,0:T(8,128)(2,1)S(1)} collective-permute-done((bf16[1,48,4096]{2,1,0:T(8,128)(2,1)}, bf16[1,48,4096]{2,1,0:T(8,128)(2,1)S(1)}, u32[]{:S(2)}, u32[]{:S(2)}) %collective-permute-start.10) | collective-permute-done | bytes 393248 | tf_op jit(solution)/shard_map/ppermute | solution.py:322
  143.9 18.3 %all_to_all.26 = bf16[16,8,4096]{2,1,0:T(8,128)(2,1)} all-to-all(bf16[16,8,4096]{2,1,0:T(8,128)(2,1)S(1)} %fusion.1), channel_id=1, replica_groups=mesh['chip'=16,'core'=2,'dp'=4] {'chip'}, dimensions={0} | all-to-all | bytes 2097152 | tf_op jit(solution)/shard_map/all_to_all | solution.py:419
  162.3 3.7 %all-to-all-start.3 = ((bf16[16,8,4096]{2,1,0:T(8,128)(2,1)}), bf16[16,8,4096]{2,1,0:T(8,128)(2,1)S(1)}, u32[]{:S(2)}, u32[]{:S(2)}) async-start(bf16[16,8,4096]{2,1,0:T(8,128)(2,1)} %bitcast.27), calls=%async_computation.3 | async-start | bytes 2097152 | tf_op jit(solution)/shard_map/all_to_all | solution.py:419
  168.1 9.7 %collective-permute-done.17.refs_13_ = bf16[1,48,4096]{2,1,0:T(8,128)(2,1)S(1)} collective-permute-done((bf16[1,48,4096]{2,1,0:T(8,128)(2,1)S(1)}, bf16[1,48,4096]{2,1,0:T(8,128)(2,1)S(1)}, u32[]{:S(2)}, u32[]{:S(2)}) %collective-permute-start.17) | collective-permute-done | bytes 393248 | tf_op jit(solution)/shard_map/ppermute | solution.py:322
  179.5 11.8 %expert_ffn.1 = bf16[64,4,4096]{2,1,0:T(4,128)(2,1)} custom-call(s32[1]{0:T(128)} %bitcast.5.flag, s32[4]{0:T(128)} %and_select_fusion.order, bf16[128,4096]{1,0:T(8,128)(2,1)} %bitcast.25, bf16[128,4096]{1,0:T(8,128)(2,1)} %bitcast.26, bf16[1,4096,384]{2,1,0:T(8,128)(2,1)} %refs_0_.1, bf16[1,4096,384]{2,1,0:T(8,128)(2,1)} %refs_1_.1, ...), custom_call_target="tpu_custom_call" | custom-call | flops 4831838208 | bytes 23068672 | tf_op jit(solution)/shard_map/expert_ffn/pallas_call | solution.py:239
  191.2 17.7 %all-to-all-start.4 = ((bf16[64,4,4096]{2,1,0:T(4,128)(2,1)}), bf16[64,4,4096]{2,1,0:T(4,128)(2,1)}, u32[]{:S(2)}, u32[]{:S(2)}) async-start(bf16[64,4,4096]{2,1,0:T(4,128)(2,1)} %expert_ffn.1), calls=%async_computation.4 | async-start | bytes 4194304 | tf_op jit(solution)/shard_map/all_to_all | solution.py:448
  210.6 26.0 %all-to-all-done.4.rows_in = bf16[64,4,4096]{2,1,0:T(4,128)(2,1)} async-done(((bf16[64,4,4096]{2,1,0:T(4,128)(2,1)}), bf16[64,4,4096]{2,1,0:T(4,128)(2,1)}, u32[]{:S(2)}, u32[]{:S(2)}) %all-to-all-start.4) | async-done | bytes 2097184 | tf_op jit(solution)/shard_map/all_to_all | solution.py:448
  236.7 2.7 %combined.1 = f32[16,4096]{1,0:T(8,128)} custom-call(bf16[16,256]{1,0:T(8,128)(2,1)} %copy.31.weights, bf16[64,4,4096]{2,1,0:T(4,128)(2,1)} %all-to-all-done.4.rows_in, f32[16,4096]{1,0:T(8,128)} %copy-done.2), custom_call_target="tpu_custom_call" | custom-call | flops 33554432 | bytes 2097152 | tf_op jit(solution)/shard_map/combined/pallas_call | solution.py:272
  (75 shorter events, 24.3 us)
Async XLA Ops:
  0.0 208.9 %copy-start = (bf16[4096,64]{0,1:T(8,128)(2,1)S(1)}, bf16[4096,64]{0,1:T(8,128)(2,1)}, u32[]{:S(2)}) copy-start(bf16[4096,64]{0,1:T(8,128)(2,1)} %param.23) | copy-start | bytes 1572868
  0.0 22.2 %collective-permute-start = (bf16[256,4096]{1,0:T(8,128)(2,1)}, bf16[256,4096]{1,0:T(8,128)(2,1)}, u32[]{:S(2)}, u32[]{:S(2)}) collective-permute-start(bf16[256,4096]{1,0:T(8,128)(2,1)} %param.21), channel_id=1, source_target_pairs={{0,4},{4,0},{1,5},{5,1},{2,6},{6,2},{3,7},{7,3},{8,12},{12,8},{9,1... | collective-permute-start | bytes 6291464 | tf_op jit(solution)/shard_map/ppermute | solution.py:30
  25.9 36.1 %all-to-all-start.1 = ((bf16[16,16,4096]{2,1,0:T(8,128)(2,1)}), bf16[16,16,4096]{2,1,0:T(8,128)(2,1)S(1)}, u32[]{:S(2)}, u32[]{:S(2)}) async-start(bf16[16,16,4096]{2,1,0:T(8,128)(2,1)} %bitcast.24), calls=%async_computation.1 | async-start | bytes 4194304 | tf_op jit(solution)/shard_map/all_to_all | solution.py:394
  29.8 44.9 %collective-permute-start.7 = (bf16[1,4096,384]{2,1,0:T(8,128)(2,1)}, bf16[1,4096,384]{2,1,0:T(8,128)(2,1)}, u32[]{:S(2)}, u32[]{:S(2)}) collective-permute-start(bf16[1,4096,384]{2,1,0:T(8,128)(2,1)} %refs_0_.1), channel_id=1, source_target_pairs={{1,0},{3,2},{4,5},{6,7},{9,8},{11,10},{12,13},{14,15},{17,16},{19,... | collective-permute-start | bytes 9437192 | tf_op jit(solution)/shard_map/ppermute | solution.py:322
  35.0 107.2 %collective-permute-start.11 = (bf16[1,4096,384]{2,1,0:T(8,128)(2,1)}, bf16[1,4096,384]{2,1,0:T(8,128)(2,1)}, u32[]{:S(2)}, u32[]{:S(2)}) collective-permute-start(bf16[1,4096,384]{2,1,0:T(8,128)(2,1)} %refs_0_.1), channel_id=1, source_target_pairs={{0,4},{2,6},{5,1},{7,3},{8,12},{10,14},{13,9},{15,11},{16,20},{18,... | collective-permute-start | bytes 9437192 | tf_op jit(solution)/shard_map/ppermute | solution.py:322
  36.3 6.9 %collective-permute-start.1 = (s32[16,8]{0,1:T(8,128)S(1)}, s32[16,8]{0,1:T(8,128)S(1)}, u32[]{:S(2)}, u32[]{:S(2)}) collective-permute-start(s32[16,8]{0,1:T(8,128)S(1)} %copy-done.8), channel_id=1, source_target_pairs={{0,1},{1,2},{2,3},{3,0},{4,7},{5,4},{6,5},{7,6},{8,9},{9,10},{10,1... | collective-permute-start | bytes 1544 | tf_op jit(solution)/shard_map/ppermute | solution.py:334
  43.1 4.0 %collective-permute-start.2 = (s32[16,8]{0,1:T(8,128)S(1)}, s32[16,8]{0,1:T(8,128)S(1)}, u32[]{:S(2)}, u32[]{:S(2)}) collective-permute-start(s32[16,8]{0,1:T(8,128)S(1)} %collective-permute-done.1), channel_id=1, source_target_pairs={{0,1},{1,2},{2,3},{3,0},{4,7},{5,4},{6,5},{7,6},{8,9},{9,10},{10,1... | collective-permute-start | bytes 1544 | tf_op jit(solution)/shard_map/ppermute | solution.py:334
  47.1 6.2 %collective-permute-start.3 = (s32[16,8]{0,1:T(8,128)S(1)}, s32[16,8]{0,1:T(8,128)S(1)}, u32[]{:S(2)}, u32[]{:S(2)}) collective-permute-start(s32[16,8]{0,1:T(8,128)S(1)} %collective-permute-done.2), channel_id=1, source_target_pairs={{0,1},{1,2},{2,3},{3,0},{4,7},{5,4},{6,5},{7,6},{8,9},{9,10},{10,1... | collective-permute-start | bytes 1544 | tf_op jit(solution)/shard_map/ppermute | solution.py:334
  50.3 55.6 %collective-permute-start.8 = (bf16[1,4096,384]{2,1,0:T(8,128)(2,1)}, bf16[1,4096,384]{2,1,0:T(8,128)(2,1)}, u32[]{:S(2)}, u32[]{:S(2)}) collective-permute-start(bf16[1,4096,384]{2,1,0:T(8,128)(2,1)} %refs_1_.1), channel_id=1, source_target_pairs={{1,0},{3,2},{4,5},{6,7},{9,8},{11,10},{12,13},{14,15},{17,16},{19,... | collective-permute-start | bytes 9437192 | tf_op jit(solution)/shard_map/ppermute | solution.py:322
  58.9 82.0 %collective-permute-start.9 = (bf16[1,336,4096]{2,1,0:T(8,128)(2,1)}, bf16[1,336,4096]{2,1,0:T(8,128)(2,1)}, u32[]{:S(2)}, u32[]{:S(2)}) collective-permute-start(bf16[1,336,4096]{2,1,0:T(8,128)(2,1)} %slice.22), channel_id=1, source_target_pairs={{1,0},{3,2},{4,5},{6,7},{9,8},{11,10},{12,13},{14,15},{17,16},{19,... | collective-permute-start | bytes 8257544 | tf_op jit(solution)/shard_map/ppermute | solution.py:322
  62.5 99.8 %copy-start.2 = (f32[16,4096]{1,0:T(8,128)}, f32[16,4096]{1,0:T(8,128)S(1)}, u32[]{:S(2)}) copy-start(f32[16,4096]{1,0:T(8,128)S(1)} %get-tuple-element.28.hidden) | copy-start | bytes 786436
  62.6 5.7 %collective-permute-start.4 = (bf16[16,4096]{1,0:T(8,128)(2,1)S(1)}, bf16[16,4096]{1,0:T(8,128)(2,1)S(1)}, u32[]{:S(2)}, u32[]{:S(2)}) collective-permute-start(bf16[16,4096]{1,0:T(8,128)(2,1)S(1)} %multiply_convert_fusion), channel_id=1, source_target_pairs={{0,1},{1,2},{2,3},{3,0},{4,7},{5,4},{6,5},{7,6},{8,9},{9,10},{10,1... | collective-permute-start | bytes 393224 | tf_op jit(solution)/shard_map/ppermute | solution.py:334
  68.3 5.6 %collective-permute-start.5 = (bf16[16,4096]{1,0:T(8,128)(2,1)S(1)}, bf16[16,4096]{1,0:T(8,128)(2,1)S(1)}, u32[]{:S(2)}, u32[]{:S(2)}) collective-permute-start(bf16[16,4096]{1,0:T(8,128)(2,1)S(1)} %collective-permute-done.4), channel_id=1, source_target_pairs={{0,1},{1,2},{2,3},{3,0},{4,7},{5,4},{6,5},{7,6},{8,9},{9,10},{10,1... | collective-permute-start | bytes 393224 | tf_op jit(solution)/shard_map/ppermute | solution.py:334
  74.0 5.6 %collective-permute-start.6 = (bf16[16,4096]{1,0:T(8,128)(2,1)S(1)}, bf16[16,4096]{1,0:T(8,128)(2,1)S(1)}, u32[]{:S(2)}, u32[]{:S(2)}) collective-permute-start(bf16[16,4096]{1,0:T(8,128)(2,1)S(1)} %collective-permute-done.5), channel_id=1, source_target_pairs={{0,1},{1,2},{2,3},{3,0},{4,7},{5,4},{6,5},{7,6},{8,9},{9,10},{10,1... | collective-permute-start | bytes 393224 | tf_op jit(solution)/shard_map/ppermute | solution.py:334
  74.7 91.2 %collective-permute-start.12 = (bf16[1,4096,384]{2,1,0:T(8,128)(2,1)}, bf16[1,4096,384]{2,1,0:T(8,128)(2,1)}, u32[]{:S(2)}, u32[]{:S(2)}) collective-permute-start(bf16[1,4096,384]{2,1,0:T(8,128)(2,1)} %refs_1_.1), channel_id=1, source_target_pairs={{0,4},{2,6},{5,1},{7,3},{8,12},{10,14},{13,9},{15,11},{16,20},{18,... | collective-permute-start | bytes 9437192 | tf_op jit(solution)/shard_map/ppermute | solution.py:322
  79.6 60.0 %collective-permute-start.10 = (bf16[1,48,4096]{2,1,0:T(8,128)(2,1)}, bf16[1,48,4096]{2,1,0:T(8,128)(2,1)S(1)}, u32[]{:S(2)}, u32[]{:S(2)}) collective-permute-start(bf16[1,48,4096]{2,1,0:T(8,128)(2,1)} %slice.23), channel_id=1, source_target_pairs={{1,0},{3,2},{4,5},{6,7},{9,8},{11,10},{12,13},{14,15},{17,16},{19,... | collective-permute-start | bytes 1179656 | tf_op jit(solution)/shard_map/ppermute | solution.py:322
  105.9 62.1 %collective-permute-start.13 = (bf16[1,384,4096]{2,1,0:T(8,128)(2,1)}, bf16[1,384,4096]{2,1,0:T(8,128)(2,1)}, u32[]{:S(2)}, u32[]{:S(2)}) collective-permute-start(bf16[1,384,4096]{2,1,0:T(8,128)(2,1)} %refs_2_.1), channel_id=1, source_target_pairs={{0,4},{2,6},{5,1},{7,3},{8,12},{10,14},{13,9},{15,11},{16,20},{18,... | collective-permute-start | bytes 9437192 | tf_op jit(solution)/shard_map/ppermute | solution.py:322
  139.6 26.3 %copy-start.4 = (bf16[1,48,4096]{2,1,0:T(8,128)(2,1)}, bf16[1,48,4096]{2,1,0:T(8,128)(2,1)S(1)}, u32[]{:S(2)}) copy-start(bf16[1,48,4096]{2,1,0:T(8,128)(2,1)S(1)} %collective-permute-done.10.refs_6_) | copy-start | bytes 1179652
  139.6 38.9 %collective-permute-start.14 = (bf16[1,4096,384]{2,1,0:T(8,128)(2,1)}, bf16[1,4096,384]{2,1,0:T(8,128)(2,1)}, u32[]{:S(2)}, u32[]{:S(2)}) collective-permute-start(bf16[1,4096,384]{2,1,0:T(8,128)(2,1)} %collective-permute-done.7.refs_3_), channel_id=1, source_target_pairs={{0,4},{2,6},{5,1},{7,3},{8,12},{10,14},{13,9},{15,11},{16,20},{18,... | collective-permute-start | bytes 9437192 | tf_op jit(solution)/shard_map/ppermute | solution.py:322
  140.9 37.6 %collective-permute-start.15 = (bf16[1,4096,384]{2,1,0:T(8,128)(2,1)}, bf16[1,4096,384]{2,1,0:T(8,128)(2,1)}, u32[]{:S(2)}, u32[]{:S(2)}) collective-permute-start(bf16[1,4096,384]{2,1,0:T(8,128)(2,1)} %collective-permute-done.8.refs_4_), channel_id=1, source_target_pairs={{0,4},{2,6},{5,1},{7,3},{8,12},{10,14},{13,9},{15,11},{16,20},{18,... | collective-permute-start | bytes 9437192 | tf_op jit(solution)/shard_map/ppermute | solution.py:322
  142.2 36.3 %collective-permute-start.16 = (bf16[1,336,4096]{2,1,0:T(8,128)(2,1)}, bf16[1,336,4096]{2,1,0:T(8,128)(2,1)}, u32[]{:S(2)}, u32[]{:S(2)}) collective-permute-start(bf16[1,336,4096]{2,1,0:T(8,128)(2,1)} %collective-permute-done.9.refs_5_), channel_id=1, source_target_pairs={{0,4},{2,6},{5,1},{7,3},{8,12},{10,14},{13,9},{15,11},{16,20},{18,... | collective-permute-start | bytes 8257544 | tf_op jit(solution)/shard_map/ppermute | solution.py:322
  162.3 15.8 %all-to-all-start.3 = ((bf16[16,8,4096]{2,1,0:T(8,128)(2,1)}), bf16[16,8,4096]{2,1,0:T(8,128)(2,1)S(1)}, u32[]{:S(2)}, u32[]{:S(2)}) async-start(bf16[16,8,4096]{2,1,0:T(8,128)(2,1)} %bitcast.27), calls=%async_computation.3 | async-start | bytes 2097152 | tf_op jit(solution)/shard_map/all_to_all | solution.py:419
  165.9 11.8 %collective-permute-start.17 = (bf16[1,48,4096]{2,1,0:T(8,128)(2,1)S(1)}, bf16[1,48,4096]{2,1,0:T(8,128)(2,1)S(1)}, u32[]{:S(2)}, u32[]{:S(2)}) collective-permute-start(bf16[1,48,4096]{2,1,0:T(8,128)(2,1)S(1)} %collective-permute-done.10.refs_6_), channel_id=1, source_target_pairs={{0,4},{2,6},{5,1},{7,3},{8,12},{10,14},{13,9},{15,11},{16,20},{18,... | collective-permute-start | bytes 1179656 | tf_op jit(solution)/shard_map/ppermute | solution.py:322
  191.2 45.4 %all-to-all-start.4 = ((bf16[64,4,4096]{2,1,0:T(4,128)(2,1)}), bf16[64,4,4096]{2,1,0:T(4,128)(2,1)}, u32[]{:S(2)}, u32[]{:S(2)}) async-start(bf16[64,4,4096]{2,1,0:T(4,128)(2,1)} %expert_ffn.1), calls=%async_computation.4 | async-start | bytes 4194304 | tf_op jit(solution)/shard_map/all_to_all | solution.py:448
  (6 other events, 44.3 us)
